TPU v7x, 32 devices: a whole 2x2x4 slice. The times are simulated.
32 devices in a mesh: model: 4 (over z), data: 8 (over y, x, core).
Axes of the slice: x: 2, y: 2, z: 4, core: 2. Of those that a mesh axis runs over, the one named last changes fastest.
Arguments:
- tokens: bfloat16 [65536, 768], P('data')
- w_up: bfloat16 [768, 3072], P(None, 'model')
- w_down: bfloat16 [3072, 768], P('model')
- task_heads: bfloat16 [2, 768, 19], replicated
- labels: int32 [2, 65536], P(None, 'data')
Outputs:
- output 1: float32 [2], replicated
- output 2: float32 [768, 3072], P('data', 'model')
- output 3: float32 [3072, 768], P(('model', 'data'))
All inputs are finite; a program needn't handle non-finite values.
Results may differ from a plain program's by a relative error of at most 0.001.
Values are sent between devices in bfloat16 or wider.
A program may use at most 1 GiB of HBM per device.

v0:
```python
import jax
import jax.numpy as jnp
from jax import lax
from jax.sharding import PartitionSpec as P

STEPS = 20


def simplex_weights(gram_mat):
    n_task = gram_mat.shape[0]
    trace_scale = jnp.trace(gram_mat) / n_task

    def eg_step(step_idx, weights):
        updated = weights * jnp.exp(-jnp.sum(gram_mat * weights[None, :], axis=1) / trace_scale)
        return updated / jnp.sum(updated)

    return lax.fori_loop(0, STEPS, eg_step, jnp.full((n_task,), 1.0 / n_task, jnp.float32))


def solution(mesh):
    n_data = mesh.shape['data']

    def local_step(tokens, w_up, w_down, task_heads, labels):
        n_total = tokens.shape[0] * n_data
        n_class = task_heads.shape[2]
        pre_act = jnp.dot(tokens, w_up, preferred_element_type=jnp.float32)
        act_val, gelu_slope = jax.jvp(jax.nn.gelu, (pre_act,), (jnp.ones_like(pre_act),))
        act_bf = act_val.astype(jnp.bfloat16)
        part_out = jnp.dot(act_bf, w_down, preferred_element_type=jnp.float32)
        mlp_out = lax.psum(part_out, 'model')
        trunk_out = (tokens.astype(jnp.float32) + mlp_out).astype(jnp.bfloat16)
        logits = jnp.einsum('bd,tdc->tbc', trunk_out, task_heads, preferred_element_type=jnp.float32)
        class_prob = jax.nn.softmax(logits, axis=-1)
        onehot = jax.nn.one_hot(labels, n_class, dtype=jnp.float32)
        dlogit = (class_prob - onehot) / n_total
        d_trunk = jnp.einsum('tbc,tdc->tbd', dlogit, task_heads.astype(jnp.float32), precision=lax.Precision.HIGHEST).astype(jnp.bfloat16)
        g_down = jnp.einsum('bf,tbd->tfd', act_bf, d_trunk, preferred_element_type=jnp.float32)
        d_act = jnp.einsum('tbd,fd->tbf', d_trunk, w_down, preferred_element_type=jnp.float32)
        d_pre = (d_act * gelu_slope[None]).astype(jnp.bfloat16)
        g_up = jnp.einsum('bd,tbf->tdf', tokens, d_pre, preferred_element_type=jnp.float32)
        up_shard = lax.psum_scatter(g_up, 'data', scatter_dimension=1, tiled=True)
        down_shard = lax.psum_scatter(g_down, 'data', scatter_dimension=1, tiled=True)
        gram_part = (jnp.einsum('tij,sij->ts', up_shard, up_shard, precision=lax.Precision.HIGHEST)
                     + jnp.einsum('tij,sij->ts', down_shard, down_shard, precision=lax.Precision.HIGHEST))
        gram_mat = lax.psum(gram_part, ('model', 'data'))
        task_weights = simplex_weights(gram_mat)
        grad_up = jnp.einsum('t,tij->ij', task_weights, up_shard, precision=lax.Precision.HIGHEST)
        grad_down = jnp.einsum('t,tij->ij', task_weights, down_shard, precision=lax.Precision.HIGHEST)
        return task_weights, grad_up, grad_down

    return jax.shard_map(
        local_step, mesh=mesh,
        in_specs=(P('data', None), P(None, 'model'), P('model', None), P(None, None, None), P(None, 'data')),
        out_specs=(P(None), P('data', 'model'), P(('model', 'data'), None)),
        check_vma=False)
```

profile of v0, /device:TPU:0, one launch (start us, length us, event | category | flops | bytes accessed | tf_op | source)
XLA Modules:
  0.0 1299.6 jit_solution(1557602126020767671)
XLA Ops:
  7.2 28.7 %fusion.10 = (f32[8192,768]{1,0:T(8,128)}, f32[8192,768]{1,0:T(8,128)}) fusion(bf16[8192,768]{1,0:T(8,128)(2,1)} %param.7, bf16[768,768]{1,0:T(8,128)(2,1)} %param.8), kind=kOutput, calls=%fused_computation.17 | convolution fusion | flops 9764339712 | bytes 64094208 | tf_op jit(solution)/shard_map/dot_general | solution.py:26
  35.9 24.5 %fusion.58 = f32[8192,768]{1,0:T(8,128)} fusion(bf16[768,768]{1,0:T(8,128)(2,1)S(1)} %copy-done, f32[8192,768]{1,0:T(8,128)} %get-tuple-element.56), kind=kOutput, calls=%fused_computation.65 | convolution fusion | flops 9720299520 | bytes 51511296 | tf_op jit(solution)/shard_map/dot_general | solution.py:29
  60.5 25.2 %copy.18 = f32[8192,768]{0,1:T(8,128)} copy(f32[8192,768]{1,0:T(8,128)} %get-tuple-element.55) | data formatting | bytes 50331648 | tf_op jit(solution)/shard_map/jvp()/add_any | solution.py:27
  85.7 806.9 %all-reduce.6.cloned.1.call-done = f32[8192,768]{1,0:T(8,128)} async-done(((f32[8192,768]{1,0:T(8,128)}), f32[8192,768]{1,0:T(8,128)}) %all-reduce.6.cloned.1.call-update) | async-done | bytes 25165840 | tf_op jit(solution)/shard_map/psum | solution.py:30
  892.5 13.8 %fusion.60 = (f32[2,8192]{1,0:T(2,128)S(1)}, f32[2,8192,19]{1,2,0:T(8,128)S(1)}) fusion(f32[8192,768]{1,0:T(8,128)} %all-reduce.6.cloned.1.call-done, bf16[8192,768]{1,0:T(8,128)(2,1)} %param.7, bf16[2,768,19]{1,0,2:T(2,128)(2,1)S(1)} %copy-done.2), kind=kOutput, calls=%fused_computation.67 | convolution fusion | flops 497647648 | bytes 39117824 | tf_op jit(solution)/shard_map/sub | solution.py:33
  906.3 23.2 %convolution_convert_fusion = bf16[2,8192,768]{2,1,0:T(8,128)(2,1)} fusion(f32[2,8192,19]{1,2,0:T(8,128)S(1)} %get-tuple-element.54, s32[2,8192]{1,0:T(2,128)S(1)} %copy-done.1, f32[2,8192]{1,0:T(2,128)S(1)} %get-tuple-element.53, bf16[2,768,19]{1,0,2:T(2,128)(2,1)S(1)} %copy-done.2), kind=kOutput, calls=%fused_computation.22 | convolution fusion | flops 2883043328 | bytes 26600448 | tf_op jit(solution)/shard_map/tbc,tdc->tbd/dot_general | solution.py:36
  929.5 33.3 %fusion.29 = f32[2,768,768]{1,2,0:T(8,128)} fusion(bf16[2,8192,768]{2,1,0:T(8,128)(2,1)} %convolution_convert_fusion, f32[8192,768]{1,0:T(8,128)} %get-tuple-element.56), kind=kOutput, calls=%fused_computation.33 | convolution fusion | flops 19383975936 | bytes 55050240 | tf_op jit(solution)/shard_map/bf,tbd->tfd/dot_general | solution.py:37
  962.9 8.2 copy.21
  971.1 60.2 %multiply_convert_fusion.9 = bf16[2,8192,768]{1,2,0:T(8,128)(2,1)} fusion(f32[8192,768]{0,1:T(8,128)} %copy.18, bf16[2,8192,768]{2,1,0:T(8,128)(2,1)} %convolution_convert_fusion, bf16[768,768]{1,0:T(8,128)(2,1)S(1)} %copy-done), kind=kOutput, calls=%fused_computation.5.clone.clone.clone.clone.1 | convolution fusion | flops 19352518656 | bytes 76677120 | tf_op jit(solution)/shard_map/tbd,fd->tbf/dot_general | solution.py:38
  1031.2 26.5 %fusion.26 = f32[2,768,768]{1,2,0:T(8,128)} fusion(bf16[8192,768]{1,0:T(8,128)(2,1)} %param.7, bf16[2,8192,768]{1,2,0:T(8,128)(2,1)} %multiply_convert_fusion.9), kind=kOutput, calls=%fused_computation.32 | convolution fusion | flops 19327352832 | bytes 42467328 | tf_op jit(solution)/shard_map/bd,tbf->tdf/dot_general | solution.py:40
  1057.7 8.2 copy.19
  1067.2 135.0 %all-reduce.8.cloned.1.call-done = (f32[2,768,768]{2,0,1:T(2,128)}, f32[2,768,768]{2,0,1:T(2,128)}) async-done(((f32[2,768,768]{2,0,1:T(2,128)}, f32[2,768,768]{2,0,1:T(2,128)}), (f32[2,768,768]{2,0,1:T(2,128)}, f32[2,768,768]{2,0,1:T(2,128)})) %all-reduce.8.cloned.1.call-update) | async-done | bytes 9437200
  1202.2 6.8 convolution_bitcast_fusion
  1209.0 6.8 fusion.38
  1215.8 39.8 %psum.15 = f32[2,2]{1,0:T(2,128)S(1)} all-reduce(f32[2,2]{1,0:T(2,128)S(1)} %fusion.38), channel_id=1, replica_groups=mesh['model'=4,'data'=8] {'model','data'}, use_global_device_ids=true, to_apply=%region_5.6 | all-reduce | flops 4 | bytes 32 | tf_op jit(solution)/shard_map/psum | solution.py:45
  1256.8 28.4 %while.11 = (s32[]{:T(128)}, f32[2]{0:T(128)S(1)}, f32[2,2]{1,0:T(2,128)S(1)}, f32[]{:T(128)}, s32[]{:T(128)}, /*index=5*/s32[]{:T(128)}) while((s32[]{:T(128)}, f32[2]{0:T(128)S(1)}, f32[2,2]{1,0:T(2,128)S(1)}, f32[]{:T(128)}, s32[]{:T(128)}, /*index=5*/s32[]{:T(128)}) %tuple.32), condition=%wide.region_10.11_spmd.clone, body=%wide.region_7.10_spmd.clone.sunk | while | flops 22 | bytes 180 | solution.py:17
  1256.9 0.6 fusion.79
  1257.6 0.6 broadcast_divide_fusion.2
  1259.0 0.6 broadcast_divide_fusion.2
  1259.8 0.6 fusion.79
  1260.4 0.6 broadcast_divide_fusion.2
  1261.2 0.6 fusion.79
  1261.8 0.6 broadcast_divide_fusion.2
  1263.2 0.6 broadcast_divide_fusion.2
  1264.0 0.6 fusion.79
  1264.7 0.6 broadcast_divide_fusion.2
  1265.5 0.6 fusion.79
  1266.1 0.6 broadcast_divide_fusion.2
  1267.5 0.6 broadcast_divide_fusion.2
  1268.3 0.6 fusion.79
  1268.9 0.6 broadcast_divide_fusion.2
  1269.7 0.6 fusion.79
  1270.3 0.6 broadcast_divide_fusion.2
  1271.8 0.6 broadcast_divide_fusion.2
  1272.6 0.6 fusion.79
  1273.2 0.6 broadcast_divide_fusion.2
  1274.0 0.6 fusion.79
  1274.6 0.6 broadcast_divide_fusion.2
  1276.0 0.6 broadcast_divide_fusion.2
  1277.4 0.6 broadcast_divide_fusion.2
  1278.9 0.6 broadcast_divide_fusion.2
  1280.3 0.6 broadcast_divide_fusion.2
  1281.7 0.6 broadcast_divide_fusion.2
  1283.1 0.6 broadcast_divide_fusion.2
  1284.5 0.6 broadcast_divide_fusion.2
  1285.2 3.1 fusion.45
  1288.3 3.1 fusion.42
  1291.4 0.9 copy_bitcast_fusion
  (68 shorter events, 10.5 us)
Async XLA Ops:
  7.2 28.7 %copy-start = (bf16[768,768]{1,0:T(8,128)(2,1)S(1)}, bf16[768,768]{1,0:T(8,128)(2,1)}, u32[]{:S(2)}) copy-start(bf16[768,768]{1,0:T(8,128)(2,1)} %param.9) | copy-start | bytes 3538948
  7.2 885.4 %all-reduce.6.cloned.1.call-start = ((), (), s32[]{:S(2)}) async-start(), calls=%async_computation | async-start | bytes 50331648 | tf_op jit(solution)/shard_map/psum | solution.py:30
  60.4 1141.7 %all-reduce.8.cloned.1.call-start = ((), (), s32[]{:S(2)}) async-start(), calls=%async_computation.1 | async-start | bytes 18874368
  60.5 832.1 %copy-start.2 = (bf16[2,768,19]{1,0,2:T(2,128)(2,1)S(1)}, bf16[2,768,19]{1,0,2:T(2,128)(2,1)}, u32[]{:S(2)}) copy-start(bf16[2,768,19]{1,0,2:T(2,128)(2,1)} %param.10) | copy-start | bytes 175108
  85.7 820.7 %copy-start.1 = (s32[2,8192]{1,0:T(2,128)S(1)}, s32[2,8192]{1,0:T(2,128)}, u32[]{:S(2)}) copy-start(s32[2,8192]{1,0:T(2,128)} %param.11) | copy-start | bytes 196612
  1031.2 34.7 %copy-start.4 = (u32[32]{0:T(128)S(1)}, u32[32]{0:T(128)}, u32[]{:S(2)}) copy-start(u32[32]{0:T(128)} %constant.36) | copy-start | bytes 388
  1285.2 7.1 copy-start.3
Sparse Core Ops, SparseCore 0:
  60.6 831.9 all-reduce.5
  1066.1 136.0 all-reduce.7
where the time goes:
time: 1310 us; the launch traced here: 1300 us
  waiting for transfers between devices  942 us (72%)
  matrix products  230 us (18%)
  local copies, waits for them, and re-layouts  43 us (3%)
  blocking collectives  39.8 us (3%)
  other arithmetic  28.3 us (2%)
  between operations  15.9 us (1%)
    psum x1, waiting for transfers between devices, local_step(): mlp_out = lax.psum(part_out, 'model')  807 us
    unnamed x3, waiting for transfers between devices  135 us
    dot_general x1, matrix products, local_step(): jnp.einsum('tbd,fd->tbf', d_trunk, w_down, preferred_element_type=jnp.flo...  60.2 us
    psum x1, blocking collectives, local_step(): gram_mat = lax.psum(gram_part, ('model', 'data'))  39.8 us
    dot_general x1, matrix products, local_step(): jnp.einsum('bf,tbd->tfd', act_bf, d_trunk, preferred_element_type=jnp.flo...  33.3 us
    dot_general x1, matrix products, local_step(): pre_act = jnp.dot(tokens, w_up, preferred_element_type=jnp.float32)  28.7 us
    dot_general x1, matrix products, local_step(): jnp.einsum('bd,tbf->tdf', tokens, d_pre, preferred_element_type=jnp.float32)  26.5 us
  transfers between devices with their start and end apart: 2, of which 2 were waited for; matrix products, arithmetic and copies ran while one was open for 2% of the time, Pallas kernels for 0%

commit v1 on v0

v1 whole, which is shorter than its diff:
```python
import jax
import jax.numpy as jnp
from jax import lax
from jax.experimental import pallas as pl
from jax.experimental.pallas import tpu as pltpu
from jax.sharding import PartitionSpec as P

STEPS = 20
BF = jnp.bfloat16
F32 = jnp.float32
MESH = pl.DeviceIdType.MESH
VMEM_BYTES = 63 * 1024 * 1024

D = 768
FL = 768
NTOK = 8192
NOWN = 2048
TB = 1024
NC = 19
ER = 40
CH = 256
NCH = 3

G0 = 0.7978845608028654
G1C = 0.044715 * G0


def dot_nn(a, b):
    return lax.dot_general(a, b, (((1,), (0,)), ((), ())), preferred_element_type=F32)


def dot_nt(a, b):
    return lax.dot_general(a, b, (((1,), (1,)), ((), ())), preferred_element_type=F32)


def dot_tn(a, b):
    return lax.dot_general(a, b, (((0,), (0,)), ((), ())), preferred_element_type=F32)


def gelu(x):
    t = jnp.tanh(x * (G0 + G1C * (x * x)))
    h = 0.5 * x
    return h + h * t


def gelu_and_slope(x):
    x2 = x * x
    t = jnp.tanh(x * (G0 + G1C * x2))
    h = 0.5 * x
    u = h + h * t
    s = 0.5 + 0.5 * t + h * (1.0 - t * t) * (G0 + (3.0 * G1C) * x2)
    return u, s


class Place:
    def __init__(self):
        self.z = lax.axis_index('model')
        self.j = lax.axis_index('data')
        self.core = self.j % 2
        self.x = (self.j // 2) % 2
        self.y = self.j // 4
        self.jc = self.j + 1 - 2 * self.core
        self.jx = self.j + 2 - 4 * self.x
        self.jy = self.j + 4 - 8 * self.y
        self.jd = self.jx + 4 - 8 * self.y

    def zmate(self, k):
        if isinstance(k, int):
            k0, k1 = k % 2, k // 2
        else:
            k0, k1 = k % 2, k // 2
        return (self.z % 2 + k0) % 2 + 2 * ((self.z // 2 + k1) % 2)


def remote(src, dst, ssem, rsem, z, j):
    return pltpu.make_async_remote_copy(
        src_ref=src, dst_ref=dst, send_sem=ssem, recv_sem=rsem, device_id=(z, j), device_id_type=MESH)


def forward_kernel(x_hbm, w1_ref, w2_hbm, hcat_ref, lab_hbm,
                   a_hbm, e_ref,
                   wg, w1t, xo, acc, xs, ast, lab_v, us,
                   zss, zrs, xss, xrs, yss, yrs, dss, drs, css, crs,
                   ld_sem, w2_sem, xs_sem, as_sem):
    pos = Place()
    z, j = pos.z, pos.j
    n_gran = 3 * NCH

    barrier = pltpu.get_barrier_semaphore()
    for k in (1, 2, 3):
        pl.semaphore_signal(barrier, 1, device_id=(pos.zmate(k), j), device_id_type=MESH)
    for jj in (pos.jc, pos.jx, pos.jy):
        pl.semaphore_signal(barrier, 1, device_id=(z, jj), device_id_type=MESH)

    own_rows = pl.multiple_of(z * NOWN, NOWN)
    ld_x = pltpu.make_async_copy(x_hbm.at[pl.ds(own_rows, NOWN)], xo, ld_sem.at[0])
    ld_l = pltpu.make_async_copy(lab_hbm.at[:, pl.ds(own_rows, NOWN)], lab_v, ld_sem.at[1])
    ld_w2 = [pltpu.make_async_copy(w2_hbm.at[:, c], wg.at[0, c, 1], w2_sem.at[c]) for c in range(NCH)]
    for cp in ld_w2:
        cp.start()

    def x_load(i):
        k = 1 + i // 2
        row = (pos.zmate(k) * 2 + i % 2) * TB
        return pltpu.make_async_copy(
            x_hbm.at[pl.ds(pl.multiple_of(row, TB), TB)], xs.at[i % 2], xs_sem.at[i % 2])

    x_load(0).start()
    ld_x.start()
    ld_l.start()

    w1t[...] = w1_ref[...].T
    for c in range(NCH):
        for g in range(8):
            wg[0, c, 0, g] = w1t[g * 96 + c * 32:g * 96 + c * 32 + 32, :]
    for cp in ld_w2:
        cp.wait()
    pl.semaphore_wait(barrier, 6)

    def piece(i, jj):
        return wg.at[1 + i // NCH, i % NCH, :, jj]

    def z_copy(i):
        k, c = 1 + i // NCH, i % NCH
        return remote(wg.at[0, c, :, j], wg.at[k, c, :, j], zss.at[i], zrs.at[i], pos.zmate(k), j)

    def x_copy(i):
        return remote(piece(i, j), piece(i, j), xss.at[i], xrs.at[i], z, pos.jx)

    def y_copy(i):
        return remote(piece(i, j), piece(i, j), yss.at[i], yrs.at[i], z, pos.jy)

    def diag_copy_y(i):
        return remote(piece(i, pos.jx), piece(i, pos.jx), dss.at[i], drs.at[i], z, pos.jy)

    def diag_copy_x(i):
        return remote(piece(i, pos.jy), piece(i, pos.jy), dss.at[i], drs.at[i], z, pos.jx)

    def core_copy(i, q):
        jj = (j, pos.jx, pos.jy, pos.jd)[q]
        return remote(piece(i, jj), piece(i, jj), css.at[i, q], crs.at[i, q], z, pos.jc)

    def send_own(i):
        z_copy(i).wait_recv()
        x_copy(i).start()
        y_copy(i).start()
        core_copy(i, 0).start()

    def send_side(i):
        x_copy(i).wait_recv()

        @pl.when(pos.core == 0)
        def _():
            diag_copy_y(i).start()

        core_copy(i, 1).start()
        y_copy(i).wait_recv()

        @pl.when(pos.core == 1)
        def _():
            diag_copy_x(i).start()

        core_copy(i, 2).start()

    def send_diag(i):
        diag_copy_y(i).wait_recv()
        core_copy(i, 3).start()

    def tick(i):
        if isinstance(i, int):
            if 0 <= i - 2 < n_gran:
                send_diag(i - 2)
            if 0 <= i - 1 < n_gran:
                send_side(i - 1)
            if i < n_gran:
                send_own(i)
        else:
            @pl.when(jnp.logical_and(i >= 2, i < n_gran + 2))
            def _():
                send_diag(i - 2)

            @pl.when(jnp.logical_and(i >= 1, i < n_gran + 1))
            def _():
                send_side(i - 1)

            @pl.when(i < n_gran)
            def _():
                send_own(i)

    def start_z(i, carry):
        z_copy(i).start()
        return carry

    lax.fori_loop(0, n_gran, start_z, 0)

    def a_store(c, row, slot):
        return pltpu.make_async_copy(
            ast.at[slot, c], a_hbm.at[c, pl.ds(pl.multiple_of(row, TB), TB)], as_sem.at[slot, c])

    def other_tokens(i, carry):
        slot = i % 2
        k = 1 + i // 2
        row = (pos.zmate(k) * 2 + i % 2) * TB
        x_load(i).wait()

        @pl.when(i < 5)
        def _():
            x_load(i + 1).start()

        @pl.when(i >= 2)
        def _():
            for c in range(NCH):
                a_store(c, row, slot).wait()

        for c in range(NCH):
            ast[slot, c] = dot_nt(xs[slot], wg[0, c, 0].reshape(CH, D))
            a_store(c, row, slot).start()

        @pl.when(i == 2)
        def _():
            tick(0)

        @pl.when(i == 4)
        def _():
            tick(1)

        return carry

    lax.fori_loop(0, 6, other_tokens, 0)
    ld_x.wait()

    def own_block(b, carry):
        rows = pl.ds(pl.multiple_of(b * TB, TB), TB)
        row = (z * 2 + b) * TB
        for c in range(NCH):
            a_store(c, row, b).wait()
        for c in range(NCH):
            a = dot_nt(xo[rows, :], wg[0, c, 0].reshape(CH, D))
            ast[b, c] = a
            us[:, c * CH:(c + 1) * CH] = gelu(a).astype(BF)
            a_store(c, row, b).start()
        total = dot_nn(us[:, 0:CH], wg[0, 0, 1].reshape(CH, D))
        total = total + dot_nn(us[:, CH:2 * CH], wg[0, 1, 1].reshape(CH, D))
        total = total + dot_nn(us[:, 2 * CH:3 * CH], wg[0, 2, 1].reshape(CH, D))
        acc[rows, :] = total

        @pl.when(b == 0)
        def _():
            tick(2)

        return carry

    lax.fori_loop(0, 2, own_block, 0)

    def granule(n, carry):
        tick(n + 3)
        for q in range(4):
            core_copy(n, q).wait_recv()
        k, c = 1 + n // NCH, n % NCH

        def block(b, inner):
            rows = pl.ds(pl.multiple_of(b * TB, TB), TB)
            u = gelu(dot_nt(xo[rows, :], wg[k, c, 0].reshape(CH, D))).astype(BF)
            us[:, 0:CH] = u
            acc[rows, :] += dot_nn(us[:, 0:CH], wg[k, c, 1].reshape(CH, D))
            return inner

        return lax.fori_loop(0, 2, block, carry)

    lax.fori_loop(0, n_gran, granule, 0)

    ld_l.wait()
    blk = 512
    for b in range(NOWN // blk):
        rows = slice(b * blk, (b + 1) * blk)
        zb = (xo[rows, :].astype(F32) + acc[rows, :]).astype(BF)
        logit = dot_nt(hcat_ref[...], zb)
        r = lax.broadcasted_iota(jnp.int32, (ER, blk), 0)
        first = r < NC
        second = jnp.logical_and(r >= NC, r < 2 * NC)
        neg = jnp.float32(-jnp.inf)
        m0 = jnp.max(jnp.where(first, logit, neg), axis=0, keepdims=True)
        m1 = jnp.max(jnp.where(second, logit, neg), axis=0, keepdims=True)
        ex = jnp.exp(logit - jnp.where(first, m0, m1))
        ex = jnp.where(r < 2 * NC, ex, 0.0)
        s0 = jnp.sum(jnp.where(first, ex, 0.0), axis=0, keepdims=True)
        s1 = jnp.sum(jnp.where(second, ex, 0.0), axis=0, keepdims=True)
        prob = ex / jnp.where(first, s0, s1)
        lab = jnp.where(first, lab_v[0:1, rows], lab_v[1:2, rows] + NC)
        hot = jnp.where(r == lab, 1.0, 0.0)
        e_ref[:, rows] = (prob - hot) / (NTOK * 8.0)

    for c in range(NCH):
        for b in range(2):
            a_store(c, (z * 2 + b) * TB, b).wait()

    def drain(i, carry):
        z_copy(i).wait_send()
        x_copy(i).wait_send()
        y_copy(i).wait_send()
        diag_copy_y(i).wait_send()
        for q in range(4):
            core_copy(i, q).wait_send()
        return carry

    lax.fori_loop(0, n_gran, drain, 0)


def forward(x, w1, w2r, hcat, labels):
    n_gran = 3 * NCH
    dma = pltpu.SemaphoreType.DMA
    anyspec = pl.BlockSpec(memory_space=pl.ANY)
    vspec = pl.BlockSpec(memory_space=pltpu.VMEM)
    return pl.pallas_call(
        forward_kernel,
        out_shape=(jax.ShapeDtypeStruct((NCH, NTOK, CH), F32), jax.ShapeDtypeStruct((ER, NOWN), F32)),
        in_specs=[anyspec, vspec, anyspec, vspec, anyspec],
        out_specs=(anyspec, vspec),
        scratch_shapes=[
            pltpu.VMEM((4, NCH, 2, 8, 32, D), BF),
            pltpu.VMEM((FL, D), BF),
            pltpu.VMEM((NOWN, D), BF),
            pltpu.VMEM((NOWN, D), F32),
            pltpu.VMEM((2, TB, D), BF),
            pltpu.VMEM((2, NCH, TB, CH), F32),
            pltpu.VMEM((2, NOWN), jnp.int32),
            pltpu.VMEM((TB, FL), BF),
            dma((n_gran,)), dma((n_gran,)), dma((n_gran,)), dma((n_gran,)), dma((n_gran,)), dma((n_gran,)),
            dma((n_gran,)), dma((n_gran,)), dma((n_gran, 4)), dma((n_gran, 4)),
            dma((2,)), dma((NCH,)), dma((2,)), dma((2, NCH)),
        ],
        compiler_params=pltpu.CompilerParams(
            collective_id=0, has_side_effects=True, vmem_limit_bytes=VMEM_BYTES),
        name='forward',
    )(x, w1, w2r, hcat, labels)


def backward_kernel(x_hbm, a_hbm, w2_hbm, hcat_ref, e_ref,
                    aw_ref, g1_ref, g2_ref,
                    dz, acc1, acc2, r1a, r1b, r2a, r2b, r3a, r3b,
                    abuf, xbuf, us, das, eall, w2v, hbd, mbuf, nbuf,
                    ess, ers, w2_sem, a_sem, x_sem,
                    s1s, s1r, s2s, s2r, s3s, s3r, mss, mrs, nss, nrs):
    pos = Place()
    z, j, core, px, py = pos.z, pos.j, pos.core, pos.x, pos.y

    barrier = pltpu.get_barrier_semaphore()
    for k in (1, 2, 3):
        pl.semaphore_signal(barrier, 1, device_id=(pos.zmate(k), j), device_id_type=MESH)
    for i in range(1, 8):
        pl.semaphore_signal(barrier, 1, device_id=(z, (j + i) % 8), device_id_type=MESH)

    ld_w2 = [pltpu.make_async_copy(w2_hbm.at[:, c], w2v.at[c], w2_sem.at[c]) for c in range(NCH)]
    for cp in ld_w2:
        cp.start()

    def step_of(s):
        early = s < 12
        s2 = s - 12
        c = jnp.where(early, (s % 6) // 2, s2 // 4)
        k = jnp.where(early, s // 6, 2 + (s2 % 4) // 2)
        return c, k, s % 2

    def a_load(s):
        c, k, b = step_of(s)
        row = pl.multiple_of((pos.zmate(k) * 2 + b) * TB, TB)
        return pltpu.make_async_copy(a_hbm.at[c, pl.ds(row, TB)], abuf.at[s % 2], a_sem.at[s % 2])

    def x_load(s):
        c, k, b = step_of(s)
        row = pl.multiple_of((pos.zmate(k) * 2 + b) * TB, TB)
        return pltpu.make_async_copy(x_hbm.at[pl.ds(row, TB)], xbuf.at[s % 2], x_sem.at[s % 2])

    a_load(0).start()
    x_load(0).start()

    acc1[...] = jnp.zeros_like(acc1)
    acc2[...] = jnp.zeros_like(acc2)
    hc = hcat_ref[...].astype(F32)
    r = lax.broadcasted_iota(jnp.int32, (ER, D), 0)
    h0 = jnp.where(r < NC, hc, 0.0)
    h1 = jnp.where(r >= NC, hc, 0.0)
    hb = jnp.concatenate([h0, h1], axis=1)
    hbd[...] = jnp.concatenate([hb, hb, hb], axis=0).astype(BF)
    eall[0] = e_ref[...]
    for cp in ld_w2:
        cp.wait()
    pl.semaphore_wait(barrier, 10)

    def e_copy(k):
        return remote(e_ref, eall.at[k], ess.at[k], ers.at[k], pos.zmate(k), j)

    for k in (1, 2, 3):
        e_copy(k).start()

    def core_copies(c):
        return (remote(acc1.at[c, :, :, 1 - core], r1a.at[c], s1s.at[c, 0], s1r.at[c, 0], z, pos.jc),
                remote(acc2.at[c, :, :, 1 - core], r1b.at[c], s1s.at[c, 1], s1r.at[c, 1], z, pos.jc))

    def side_copies(c):
        return (remote(acc1.at[c, :, 1 - px, core], r2a.at[c], s2s.at[c, 0], s2r.at[c, 0], z, pos.jx),
                remote(acc2.at[c, 1 - py, :, core], r2b.at[c], s2s.at[c, 1], s2r.at[c, 1], z, pos.jy))

    def last_copies(c):
        return (remote(acc1.at[c, 1 - py, px, core], r3a.at[c], s3s.at[c, 0], s3r.at[c, 0], z, pos.jy),
                remote(acc2.at[c, py, 1 - px, core], r3b.at[c], s3s.at[c, 1], s3r.at[c, 1], z, pos.jx))

    def rs_core(c):
        for cp in core_copies(c):
            cp.start()

    def rs_side(c):
        for cp in core_copies(c):
            cp.wait_recv()
        for yy in range(2):
            for xx in range(2):
                acc1[c, yy, xx, core] += r1a[c, yy, xx]
                acc2[c, yy, xx, core] += r1b[c, yy, xx]
        for cp in side_copies(c):
            cp.start()

    def rs_last(c):
        for cp in side_copies(c):
            cp.wait_recv()
        for i in range(2):
            acc1[c, i, px, core] += r2a[c, i]
            acc2[c, py, i, core] += r2b[c, i]
        for cp in last_copies(c):
            cp.start()

    def rs_done(c):
        for cp in last_copies(c):
            cp.wait_recv()
        acc1[c, py, px, core] += r3a[c]
        acc2[c, py, px, core] += r3b[c]

    sub = 256

    def step(s, carry):
        c, k, b = step_of(s)
        slot = s % 2
        t = k * 2 + b
        a_load(s).wait()
        x_load(s).wait()

        @pl.when(s < 23)
        def _():
            a_load(s + 1).start()
            x_load(s + 1).start()

        @pl.when(c == 0)
        def _():
            @pl.when(jnp.logical_and(b == 0, k > 0))
            def _():
                e_copy(k).wait_recv()

            e = eall[k, :, pl.ds(pl.multiple_of(b * TB, TB), TB)]
            e1 = e.astype(BF).astype(F32)
            rest = e - e1
            e2 = rest.astype(BF).astype(F32)
            e3 = rest - e2
            es = jnp.concatenate([e1, e2, e3], axis=0).astype(BF)
            dz[t] = dot_tn(es, hbd[...]).astype(BF)

        w2c = w2v[c].reshape(CH, D)
        for m in range(TB // sub):
            rows = slice(m * sub, (m + 1) * sub)
            u, slope = gelu_and_slope(abuf[slot, rows, :])
            us[rows, :] = u.astype(BF)
            for task in range(2):
                da = dot_nt(dz[t, rows, task * D:(task + 1) * D], w2c)
                das[rows, task * CH:(task + 1) * CH] = (da * slope).astype(BF)
        acc2[c] += dot_tn(us[...], dz[t]).reshape(2, 2, 2, 32, 2 * D)
        acc1[c] += dot_tn(xbuf[slot], das[...]).reshape(2, 2, 2, 96, 2 * CH)

        @pl.when(s == 15)
        def _():
            rs_core(0)

        @pl.when(s == 16)
        def _():
            rs_side(0)

        @pl.when(s == 19)
        def _():
            rs_core(1)

        @pl.when(s == 20)
        def _():
            rs_last(0)
            rs_side(1)

        @pl.when(s == 22)
        def _():
            rs_done(0)

        return carry

    lax.fori_loop(0, 24, step, 0)
    rs_core(2)
    rs_last(1)
    rs_side(2)
    rs_done(1)
    rs_last(2)
    rs_done(2)

    m00 = jnp.zeros((8, 128), F32)
    m01 = jnp.zeros((8, 128), F32)
    m11 = jnp.zeros((8, 128), F32)

    def fold(v):
        rows, cols = v.shape
        total = jnp.zeros((8, 128), F32)
        for q in range(cols // 128):
            total = total + jnp.sum(v[:, q * 128:(q + 1) * 128].reshape(rows // 8, 8, 128), axis=0)
        return total

    for c in range(NCH):
        for ref, width in ((acc1, CH), (acc2, D)):
            v0 = ref[c, py, px, core, :, 0:width]
            v1 = ref[c, py, px, core, :, width:2 * width]
            m00 = m00 + fold(v0 * v0)
            m01 = m01 + fold(v0 * v1)
            m11 = m11 + fold(v1 * v1)

    def full(v):
        return jnp.sum(jnp.sum(v, axis=0, keepdims=True), axis=1, keepdims=True)

    row = lax.broadcasted_iota(jnp.int32, (8, 128), 0)
    part = jnp.where(row == 0, full(m00), jnp.where(row == 1, full(m01), full(m11)))
    mbuf[j] = part

    def m_copy(i):
        return remote(mbuf.at[j], mbuf.at[j], mss.at[i], mrs.at[i], z, (j + i) % 8)

    for i in range(1, 8):
        m_copy(i).start()
    for i in range(1, 8):
        m_copy(i).wait_recv()
    total = mbuf[0]
    for i in range(1, 8):
        total = total + mbuf[i]
    nbuf[z] = total

    def n_copy(k):
        return remote(nbuf.at[z], nbuf.at[z], nss.at[k], nrs.at[k], pos.zmate(k), j)

    for k in (1, 2, 3):
        n_copy(k).start()
    for k in (1, 2, 3):
        n_copy(k).wait_recv()
    gram = nbuf[0]
    for k in (1, 2, 3):
        gram = gram + nbuf[k]

    g00, g01, g11 = gram[0:1, :], gram[1:2, :], gram[2:3, :]
    scale = (g00 + g11) / 2.0

    def eg_step(i, weights):
        a0, a1 = weights
        v0 = a0 * jnp.exp(-(g00 * a0 + g01 * a1) / scale)
        v1 = a1 * jnp.exp(-(g01 * a0 + g11 * a1) / scale)
        tot = v0 + v1
        return v0 / tot, v1 / tot

    half = jnp.full((1, 128), 0.5, F32)
    a0, a1 = lax.fori_loop(0, STEPS, eg_step, (half, half))
    lane = lax.broadcasted_iota(jnp.int32, (8, 128), 1)
    aw_ref[...] = jnp.where(lane == 0, a0, a1)

    b0 = jnp.concatenate([a0] * 6, axis=1)
    b1 = jnp.concatenate([a1] * 6, axis=1)
    for c in range(NCH):
        v = acc1[c, py, px, core]
        comb = b0[:, 0:CH] * v[:, 0:CH] + b1[:, 0:CH] * v[:, CH:2 * CH]
        for g in range(8):
            g1_ref[:, g * 96 + c * 32:g * 96 + c * 32 + 32] = comb[:, g * 32:g * 32 + 32]
        v = acc2[c, py, px, core]
        g2_ref[c * 32:(c + 1) * 32, :] = b0 * v[:, 0:D] + b1 * v[:, D:2 * D]

    for k in (1, 2, 3):
        e_copy(k).wait_send()
        n_copy(k).wait_send()
    for c in range(NCH):
        for cp in core_copies(c) + side_copies(c) + last_copies(c):
            cp.wait_send()
    for i in range(1, 8):
        m_copy(i).wait_send()


def backward(x, a, w2r, hcat, e):
    dma = pltpu.SemaphoreType.DMA
    anyspec = pl.BlockSpec(memory_space=pl.ANY)
    vspec = pl.BlockSpec(memory_space=pltpu.VMEM)
    return pl.pallas_call(
        backward_kernel,
        out_shape=(jax.ShapeDtypeStruct((8, 128), F32), jax.ShapeDtypeStruct((96, FL), F32),
                   jax.ShapeDtypeStruct((96, D), F32)),
        in_specs=[anyspec, anyspec, anyspec, vspec, vspec],
        out_specs=(vspec, vspec, vspec),
        scratch_shapes=[
            pltpu.VMEM((8, TB, 2 * D), BF),
            pltpu.VMEM((NCH, 2, 2, 2, 96, 2 * CH), F32),
            pltpu.VMEM((NCH, 2, 2, 2, 32, 2 * D), F32),
            pltpu.VMEM((NCH, 2, 2, 96, 2 * CH), F32),
            pltpu.VMEM((NCH, 2, 2, 32, 2 * D), F32),
            pltpu.VMEM((NCH, 2, 96, 2 * CH), F32),
            pltpu.VMEM((NCH, 2, 32, 2 * D), F32),
            pltpu.VMEM((NCH, 96, 2 * CH), F32),
            pltpu.VMEM((NCH, 32, 2 * D), F32),
            pltpu.VMEM((2, TB, CH), F32),
            pltpu.VMEM((2, TB, D), BF),
            pltpu.VMEM((TB, CH), BF),
            pltpu.VMEM((TB, 2 * CH), BF),
            pltpu.VMEM((4, ER, NOWN), F32),
            pltpu.VMEM((NCH, 8, 32, D), BF),
            pltpu.VMEM((3 * ER, 2 * D), BF),
            pltpu.VMEM((8, 8, 128), F32),
            pltpu.VMEM((4, 8, 128), F32),
            dma((4,)), dma((4,)), dma((NCH,)), dma((2,)), dma((2,)),
            dma((NCH, 2)), dma((NCH, 2)), dma((NCH, 2)), dma((NCH, 2)), dma((NCH, 2)), dma((NCH, 2)),
            dma((8,)), dma((8,)), dma((4,)), dma((4,)),
        ],
        compiler_params=pltpu.CompilerParams(
            collective_id=1, has_side_effects=True, vmem_limit_bytes=VMEM_BYTES),
        name='backward',
    )(x, a, w2r, hcat, e)


def solution(mesh):
    def local_step(tokens, w_up, w_down, task_heads, labels):
        heads = jnp.transpose(task_heads, (0, 2, 1)).reshape(2 * NC, D)
        hcat = jnp.pad(heads, ((0, ER - 2 * NC), (0, 0)))
        w2r = w_down.reshape(8, NCH, 32, D)
        a, e = forward(tokens, w_up, w2r, hcat, labels)
        weights, grad_up, grad_down = backward(tokens, a, w2r, hcat, e)
        return weights[0, 0:2], grad_up, grad_down

    return jax.shard_map(
        local_step, mesh=mesh,
        in_specs=(P('data', None), P(None, 'model'), P('model', None), P(None, None, None), P(None, 'data')),
        out_specs=(P(None), P('data', 'model'), P(('model', 'data'), None)),
        check_vma=False)
```

time: 1310 us -> 199 us (0.15)
  waiting for transfers between devices: 942 us -> 0 us
  matrix products: 230 us -> 0 us
  Pallas kernels: 0 us -> 192 us
  blocking collectives: 39.8 us -> 0 us
  local copies, waits for them, and re-layouts: 43 us -> 6.07 us
  other arithmetic: 28.3 us -> 0 us
  between operations: 15.9 us -> 0.66 us
    psum x1 -> x0, waiting for transfers between devices: 807 us -> none  [local_step(): mlp_out = lax.psum(part_out, 'model')]
    dot_general x10 -> x0, matrix products: 216 us -> none  [the longest x1 60.2 us: local_step(): jnp.einsum('tbd,fd->tbf', d_trunk, w_down, preferred_element_type=jnp.flo...]
    pallas_call x0 -> x2, Pallas kernels: none -> 192 us  [the longest x1 117 us: backward(): pl.pallas_call(backward_kernel, out_shape=(jax.ShapeDtypeStruct((8, 128),...]
    unnamed x3 -> x0, waiting for transfers between devices: 135 us -> none
    psum x1 -> x0, blocking collectives: 39.8 us -> none  [local_step(): gram_mat = lax.psum(gram_part, ('model', 'data'))]
    add_any x1 -> x0, local copies, waits for them, and re-layouts: 25.2 us -> none  [local_step(): jax.jvp(jax.nn.gelu, (pre_act,), (jnp.ones_like(pre_act),))]
    transpose x2 -> x1, local copies, waits for them, and re-layouts: 16.4 us -> 0.83 us  [local_step(): heads = jnp.transpose(task_heads, (0, 2, 1)).reshape(2 * NC, D)]
    reduce_sum x41 -> x0, other arithmetic: 15.3 us -> none  [the longest x20 12.4 us: eg_step(): return updated / jnp.sum(updated)]
  transfers between devices with their start and end apart: 2 -> 0, of which waited for: 2 -> 0; matrix products, arithmetic and copies ran while one was open for 2% -> 0% of each run, Pallas kernels for 0% -> 0%
where the time goes in v1:
time: 199 us
  Pallas kernels  192 us (96%)
  local copies, waits for them, and re-layouts  6.07 us (3%)
    pallas_call x1, Pallas kernels, backward(): pl.pallas_call(backward_kernel, out_shape=(jax.ShapeDtypeStruct((8, 128),...  117 us
    pallas_call x1, Pallas kernels, forward(): pl.pallas_call(forward_kernel, out_shape=(jax.ShapeDtypeStruct((NCH, NTOK...  75.1 us

profile of v1, /device:TPU:0, one launch (start us, length us, event | category | flops | bytes accessed | tf_op | source)
XLA Modules:
  0.0 199.0 jit_solution(4985100288807103731)
XLA Ops:
  0.6 0.8 copy.9
  1.5 0.6 pad.4.hcat_ref
  2.1 75.1 %forward.1 = (f32[3,8192,256]{2,1,0:T(8,128)}, f32[40,2048]{1,0:T(8,128)}) custom-call(bf16[8192,768]{1,0:T(8,128)(2,1)} %x_hbm.3, bf16[768,768]{1,0:T(8,128)(2,1)} %w1_ref.1, bf16[8,3,32,768]{3,2,1,0:T(8,128)(2,1)} %bitcast.4, bf16[40,768]{1,0:T(8,128)(2,1)} %pad.4.hcat_ref, s32[2,8192]{1,0:T(2,128)} %lab_hbm.1), custom_call_target="tpu_custom_call" | custom-call | tf_op jit(solution)/shard_map/forward/pallas_call | solution.py:314
  77.2 117.2 %backward.1 = (f32[8,128]{1,0:T(8,128)}, f32[96,768]{1,0:T(8,128)}, f32[96,768]{1,0:T(8,128)}) custom-call(bf16[8192,768]{1,0:T(8,128)(2,1)} %x_hbm.3, f32[3,8192,256]{2,1,0:T(8,128)} %get-tuple-element.8.a_hbm, bf16[8,3,32,768]{3,2,1,0:T(8,128)(2,1)} %bitcast.5, bf16[40,768]{1,0:T(8,128)(2,1)} %pad.4.hcat_ref, f32[40,2048]{1,0:T(8,128)} %get-tuple-element.9.e_ref), custom_call_target="tpu_custom_call" | custom-call | tf_op jit(solution)/shard_map/backward/pallas_call | solution.py:595
  194.4 1.2 slice_bitcast_fusion
  195.6 1.7 copy.12
  197.3 1.7 copy.13
  (1 shorter events, 0.0 us)

commit v2 on v0

v2 whole, which is shorter than its diff:
```python
import jax
import jax.numpy as jnp
from jax import lax
from jax.experimental import pallas as pl
from jax.experimental.pallas import tpu as pltpu
from jax.sharding import PartitionSpec as P

STEPS = 20
BF = jnp.bfloat16
F32 = jnp.float32
MESH = pl.DeviceIdType.MESH
VMEM_BYTES = 67043328

D = 768
FL = 768
NTOK = 8192
NOWN = 2048
TB = 1024
SUB = 256
NC = 19
ER = 40
CH = 256
NCH = 3
NG = 9
LAST = NCH - 1

G0 = 0.7978845608028654
G1C = 0.044715 * G0


def dot_nn(a, b):
    return lax.dot_general(a, b, (((1,), (0,)), ((), ())), preferred_element_type=F32)


def dot_nt(a, b):
    return lax.dot_general(a, b, (((1,), (1,)), ((), ())), preferred_element_type=F32)


def dot_tn(a, b):
    return lax.dot_general(a, b, (((0,), (0,)), ((), ())), preferred_element_type=F32)


def gelu(x):
    t = jnp.tanh(x * (G0 + G1C * (x * x)))
    h = 0.5 * x
    return h + h * t


def gelu_and_slope(x):
    x2 = x * x
    t = jnp.tanh(x * (G0 + G1C * x2))
    h = 0.5 * x
    u = h + h * t
    s = 0.5 + 0.5 * t + h * (1.0 - t * t) * (G0 + (3.0 * G1C) * x2)
    return u, s


class Place:
    def __init__(self):
        self.z = lax.axis_index('model')
        self.j = lax.axis_index('data')
        self.core = self.j % 2
        self.x = (self.j // 2) % 2
        self.y = self.j // 4
        self.jc = self.j + 1 - 2 * self.core
        self.jx = self.j + 2 - 4 * self.x
        self.jy = self.j + 4 - 8 * self.y
        self.jd = self.jx + 4 - 8 * self.y

    def zmate(self, k):
        return (self.z % 2 + k % 2) % 2 + 2 * ((self.z // 2 + k // 2) % 2)


def remote(src, dst, ssem, rsem, z, j):
    return pltpu.make_async_remote_copy(
        src_ref=src, dst_ref=dst, send_sem=ssem, recv_sem=rsem, device_id=(z, j), device_id_type=MESH)


class Scatter:
    def __init__(self, pos, acc, r1, r2, r3, lanes, sems, idx, x_first):
        self.pos, self.acc, self.r1, self.r2, self.r3 = pos, acc, r1, r2, r3
        self.lanes, self.sems, self.idx, self.x_first = lanes, sems, idx, x_first

    def copy(self, stage):
        p, ln = self.pos, self.lanes
        ssem, rsem = self.sems[0].at[self.idx, stage], self.sems[1].at[self.idx, stage]
        if stage == 0:
            return remote(self.acc.at[:, :, 1 - p.core, :, ln], self.r1.at[:, :, :, ln], ssem, rsem, p.z, p.jc)
        if stage == 1:
            if self.x_first:
                return remote(self.acc.at[:, 1 - p.x, p.core, :, ln], self.r2.at[:, :, ln], ssem, rsem, p.z, p.jx)
            return remote(self.acc.at[1 - p.y, :, p.core, :, ln], self.r2.at[:, :, ln], ssem, rsem, p.z, p.jy)
        if self.x_first:
            return remote(self.acc.at[1 - p.y, p.x, p.core, :, ln], self.r3.at[:, ln], ssem, rsem, p.z, p.jy)
        return remote(self.acc.at[p.y, 1 - p.x, p.core, :, ln], self.r3.at[:, ln], ssem, rsem, p.z, p.jx)

    def start(self):
        self.copy(0).start()

    def side(self):
        p, ln = self.pos, self.lanes
        self.copy(0).wait_recv()
        for yy in range(2):
            for xx in range(2):
                self.acc[yy, xx, p.core, :, ln] += self.r1[yy, xx, :, ln]
        self.copy(1).start()

    def last(self):
        p, ln = self.pos, self.lanes
        self.copy(1).wait_recv()
        for i in range(2):
            if self.x_first:
                self.acc[i, p.x, p.core, :, ln] += self.r2[i, :, ln]
            else:
                self.acc[p.y, i, p.core, :, ln] += self.r2[i, :, ln]
        self.copy(2).start()

    def done(self):
        p, ln = self.pos, self.lanes
        self.copy(2).wait_recv()
        self.acc[p.y, p.x, p.core, :, ln] += self.r3[:, ln]

    def drain(self):
        for stage in range(3):
            self.copy(stage).wait_send()


def main_kernel(x_hbm, w1_hbm, w2_hbm, heads_hbm, lab_hbm,
                a_hbm, sh1_hbm, sh2_hbm, aw_ref,
                dz, wown, acc1, acc2, r1a, r1b, r2a, r2b, r3a, r3b, eall, ast, hbd, hcat, heads, lab_v,
                gm, mbuf, nbuf,
                zss, zrs, xss, xrs, yss, yrs, dss, drs, css, crs,
                ld_sem, w2_sem, xs_sem, as_sem, ess, ers,
                rss, rsr, mss, mrs, nss, nrs, sh_sem):
    pos = Place()
    z, j = pos.z, pos.j

    barrier = pltpu.get_barrier_semaphore()
    for k in (1, 2, 3):
        pl.semaphore_signal(barrier, 1, device_id=(pos.zmate(k), j), device_id_type=MESH)
    for i in range(1, 8):
        pl.semaphore_signal(barrier, 1, device_id=(z, (j + i) % 8), device_id_type=MESH)

    w1_raw = dz.at[3, 0:D, 0:FL]
    w1_nat = dz.at[3, 0:D, FL:FL + CH]

    def xo_at(m):
        return dz.at[0, (m % 4) * SUB:(m % 4 + 1) * SUB, (m // 4) * D:(m // 4 + 1) * D]

    def us_at(m):
        return dz.at[2, (m % 4) * SUB:(m % 4 + 1) * SUB, D + (m // 4) * CH:D + (m // 4 + 1) * CH]

    own_row = pl.multiple_of(z * NOWN, NOWN)
    ld_w1 = pltpu.make_async_copy(w1_hbm, w1_raw, ld_sem.at[0])
    ld_x = [pltpu.make_async_copy(x_hbm.at[pl.ds(own_row + b * TB, TB)], dz.at[0, :, b * D:(b + 1) * D],
                                  ld_sem.at[1 + b]) for b in range(2)]
    ld_l = pltpu.make_async_copy(lab_hbm.at[:, pl.ds(own_row, NOWN)], lab_v, ld_sem.at[3])
    ld_h = pltpu.make_async_copy(heads_hbm, heads, ld_sem.at[4])
    ld_w2 = [pltpu.make_async_copy(w2_hbm.at[:, c], wown.at[c, :, :, D:2 * D], w2_sem.at[c]) for c in range(NCH)]

    def share_row(k, b):
        return pl.multiple_of((pos.zmate(k) * 2 + b) * TB, TB)

    def xs_load(i):
        half = dz.at[1, :, pl.ds(pl.multiple_of((i % 2) * D, D), D)]
        return pltpu.make_async_copy(x_hbm.at[pl.ds(share_row(1 + i // 2, i % 2), TB)], half, xs_sem.at[i % 2])

    ld_w1.start()
    for cp in ld_w2:
        cp.start()
    xs_load(0).start()
    for cp in ld_x:
        cp.start()
    ld_h.start()
    ld_l.start()

    ld_w1.wait()
    w1t = w1_raw[...].T
    for c in range(NCH):
        for g in range(8):
            wown[c, g, :, 0:D] = w1t[g * 96 + c * 32:g * 96 + c * 32 + 32, :]
    acc1[...] = jnp.zeros_like(acc1)
    acc2[...] = jnp.zeros_like(acc2)
    gm[...] = jnp.zeros_like(gm)
    for cp in ld_w2:
        cp.wait()
    pl.semaphore_wait(barrier, 10)

    def piece(i, jj):
        row = pl.multiple_of((i % NCH) * CH + jj * 32, 32)
        return dz.at[5 + i // NCH, pl.ds(row, 32), :]

    def z_copy(i):
        return remote(wown.at[i % NCH, j], piece(i, j), zss.at[i], zrs.at[i], pos.zmate(1 + i // NCH), j)

    def x_copy(i):
        return remote(piece(i, j), piece(i, j), xss.at[i], xrs.at[i], z, pos.jx)

    def y_copy(i):
        return remote(piece(i, j), piece(i, j), yss.at[i], yrs.at[i], z, pos.jy)

    def diag_copy_y(i):
        return remote(piece(i, pos.jx), piece(i, pos.jx), dss.at[i], drs.at[i], z, pos.jy)

    def diag_copy_x(i):
        return remote(piece(i, pos.jy), piece(i, pos.jy), dss.at[i], drs.at[i], z, pos.jx)

    def core_copy(i, q):
        jj = (j, pos.jx, pos.jy, pos.jd)[q]
        return remote(piece(i, jj), piece(i, jj), css.at[i, q], crs.at[i, q], z, pos.jc)

    def send_own(i):
        z_copy(i).wait_recv()
        x_copy(i).start()
        y_copy(i).start()
        core_copy(i, 0).start()

    def send_side(i):
        x_copy(i).wait_recv()

        @pl.when(pos.core == 0)
        def _():
            diag_copy_y(i).start()

        core_copy(i, 1).start()
        y_copy(i).wait_recv()

        @pl.when(pos.core == 1)
        def _():
            diag_copy_x(i).start()

        core_copy(i, 2).start()

    def send_diag(i):
        diag_copy_y(i).wait_recv()
        core_copy(i, 3).start()

    def start_z(i, carry):
        z_copy(i).start()
        return carry

    lax.fori_loop(0, NG, start_z, 0)

    def a_store(c, row):
        return pltpu.make_async_copy(
            ast.at[c], a_hbm.at[c, pl.ds(pl.multiple_of(row, TB), TB)], as_sem.at[c])

    def other_tokens(i, carry):
        xs_load(i).wait()

        @pl.when(i < 5)
        def _():
            xs_load(i + 1).start()

        xs = dz.at[1, :, pl.ds(pl.multiple_of((i % 2) * D, D), D)]
        for c in range(NCH):
            @pl.when(i >= 1)
            def _():
                a_store(c, 0).wait()

            ast[c] = dot_nt(xs[...], wown[c, :, :, 0:D].reshape(CH, D))
            a_store(c, share_row(1 + i // 2, i % 2)).start()

        @pl.when(i == 2)
        def _():
            send_own(0)

        @pl.when(i == 3)
        def _():
            send_own(1)

        @pl.when(i == 5)
        def _():
            send_side(0)
            send_own(2)

        return carry

    lax.fori_loop(0, 6, other_tokens, 0)
    for cp in ld_x:
        cp.wait()

    def forward(facc):
        for b in range(2):
            for c in range(NCH):
                a_store(c, 0).wait()
            for m in range(4):
                rows = slice(m * SUB, (m + 1) * SUB)
                for c in range(NCH):
                    a = dot_nt(xo_at(b * 4 + m)[...], wown[c, :, :, 0:D].reshape(CH, D))
                    ast[c, rows, :] = a
                    dz[2, rows, c * CH:(c + 1) * CH] = gelu(a).astype(BF)
            for m in range(4):
                rows = slice(m * SUB, (m + 1) * SUB)
                facc[b * TB + m * SUB:b * TB + (m + 1) * SUB, :] = dot_nn(
                    dz[2, rows, 0:FL], wown[:, :, :, D:2 * D].reshape(FL, D))
            for c in range(NCH):
                a_store(c, (z * 2 + b) * TB).start()
            if b == 0:
                send_diag(0)
                send_side(1)
                send_own(3)

        def granule(n, carry):
            for q in range(4):
                core_copy(n, q).wait_recv()
            gran = dz.at[5 + n // NCH, pl.ds(pl.multiple_of((n % NCH) * CH, CH), CH), :]
            w1_nat[...] = gran[:, 0:D].T
            for m in range(8):
                us_at(m)[...] = gelu(dot_nn(xo_at(m)[...], w1_nat[...])).astype(BF)
            for m in range(8):
                facc[m * SUB:(m + 1) * SUB, :] += dot_nn(us_at(m)[...], gran[:, D:2 * D])

            @pl.when(n + 1 < NG)
            def _():
                send_diag(n + 1)

            @pl.when(n + 2 < NG)
            def _():
                send_side(n + 2)

            @pl.when(n + 4 < NG)
            def _():
                send_own(n + 4)

            return carry

        lax.fori_loop(0, NG, granule, 0)

        for m in range(8):
            us = (xo_at(m)[...].astype(F32) + facc[m * SUB:(m + 1) * SUB, :]).astype(BF)
            xo_at(m)[...] = us

    ld_h.wait()
    r40 = lax.broadcasted_iota(jnp.int32, (ER, NC), 0)
    c19 = lax.broadcasted_iota(jnp.int32, (ER, NC), 1)
    hc = (dot_nt(jnp.where(r40 == c19, 1.0, 0.0).astype(BF), heads[0])
          + dot_nt(jnp.where(r40 == c19 + NC, 1.0, 0.0).astype(BF), heads[1]))
    hcat[...] = hc.astype(BF)
    r = lax.broadcasted_iota(jnp.int32, (ER, D), 0)
    hb = jnp.concatenate([jnp.where(r < NC, hc, 0.0), jnp.where(r >= NC, hc, 0.0)], axis=1)
    hbd[...] = jnp.concatenate([hb, hb, hb], axis=0).astype(BF)

    pl.run_scoped(forward, pltpu.VMEM((NOWN, D), F32))

    ld_l.wait()
    r = lax.broadcasted_iota(jnp.int32, (ER, TB), 0)
    first = r < NC
    real = r < 2 * NC
    second = jnp.logical_and(r >= NC, real)
    neg = jnp.float32(-jnp.inf)
    for b in range(2):
        cols = slice(b * TB, (b + 1) * TB)
        logit = dot_nt(hcat[...], dz[0, :, b * D:(b + 1) * D])
        m0 = jnp.max(jnp.where(first, logit, neg), axis=0, keepdims=True)
        m1 = jnp.max(jnp.where(second, logit, neg), axis=0, keepdims=True)
        ex = jnp.where(real, jnp.exp(logit - jnp.where(first, m0, m1)), 0.0)
        s0 = jnp.sum(jnp.where(first, ex, 0.0), axis=0, keepdims=True)
        s1 = jnp.sum(jnp.where(second, ex, 0.0), axis=0, keepdims=True)
        prob = ex / jnp.where(first, s0, s1)
        lab = jnp.where(first, lab_v[0:1, cols], lab_v[1:2, cols] + NC)
        eall[0, :, cols] = (prob - jnp.where(r == lab, 1.0, 0.0)) / (NTOK * 8.0)

    def e_copy(k):
        return remote(eall.at[0], eall.at[k], ess.at[k], ers.at[k], pos.zmate(k), j)

    for k in (1, 2, 3):
        e_copy(k).start()
    for c in range(NCH):
        a_store(c, 0).wait()

    def drain(i, carry):
        z_copy(i).wait_send()
        x_copy(i).wait_send()
        y_copy(i).wait_send()
        diag_copy_y(i).wait_send()
        for q in range(4):
            core_copy(i, q).wait_send()
        return carry

    lax.fori_loop(0, NG, drain, 0)

    everything = slice(None)
    sems = (rss, rsr)

    def up(c, t):
        return Scatter(pos, acc1.at[c, t], r1a.at[c, t], r2a.at[c, t], r3a.at[c, t], everything, sems,
                       c * 6 + t, t == 0)

    def down(c, t, part=None):
        if part is None:
            lanes, idx, x_first = everything, c * 6 + 2 + t, t == 0
        else:
            lanes, idx, x_first = slice(part * (D // 2), (part + 1) * (D // 2)), c * 6 + 2 + t * 2 + part, part == 0
        return Scatter(pos, acc2.at[c, t], r1b.at[c, t], r2b.at[c, t], r3b.at[c, t], lanes, sems, idx, x_first)

    def whole(c):
        return [up(c, 0), down(c, 1), up(c, 1), down(c, 0)]

    up_last = [up(LAST, 0), up(LAST, 1)]
    down_last = [[down(LAST, t, part) for part in range(2)] for t in range(2)]

    def fold(v):
        rows, cols = v.shape
        total = jnp.zeros((8, 128), F32)
        for q in range(cols // 128):
            total = total + jnp.sum(v[:, q * 128:(q + 1) * 128].reshape(rows // 8, 8, 128), axis=0)
        return total

    def shard(acc, c, t):
        return acc.at[c, t, pos.y, pos.x, pos.core]

    def finish(acc, out, c, sem):
        v0, v1 = shard(acc, c, 0)[...], shard(acc, c, 1)[...]
        gm[0] += fold(v0 * v0)
        gm[1] += fold(v0 * v1)
        gm[2] += fold(v1 * v1)
        for t in range(2):
            pltpu.make_async_copy(shard(acc, c, t), out.at[c, t], sh_sem.at[c, sem, t]).start()

    def backward(xbuf, us_all, das):
        def step_of(s):
            c = jnp.where(s < 8, (s // 2) % 2, jnp.where(s < 16, (s - 8) // 4, 2))
            k = jnp.where(s < 8, s // 4, jnp.where(s < 16, 2 + (s % 4) // 2, (s - 16) // 2))
            return c, k, s % 2

        def a_load(s):
            c, k, b = step_of(s)
            return pltpu.make_async_copy(a_hbm.at[c, pl.ds(share_row(k, b), TB)], ast.at[s % 2], as_sem.at[s % 2])

        def x_load(s):
            c, k, b = step_of(s)
            return pltpu.make_async_copy(x_hbm.at[pl.ds(share_row(k, b), TB)], xbuf.at[s % 2], xs_sem.at[s % 2])

        a_load(0).start()
        x_load(0).start()

        def prepare(s):
            c, k, b = step_of(s)
            a_load(s).wait()
            x_load(s).wait()

            @pl.when(s < 23)
            def _():
                a_load(s + 1).start()
                x_load(s + 1).start()

        def d_act(s, t, us):
            c, _, _ = step_of(s)
            w2c = wown[c, :, :, D:2 * D].reshape(CH, D)
            for m in range(TB // SUB):
                rows = slice(m * SUB, (m + 1) * SUB)
                u, slope = gelu_and_slope(ast[s % 2, rows, :])
                us[rows, :] = u.astype(BF)
                for task in range(2):
                    da = dot_nt(dz[t, rows, task * D:(task + 1) * D], w2c)
                    das[rows, task * CH:(task + 1) * CH] = (da * slope).astype(BF)

        def add_up(s, c):
            g = dot_tn(xbuf[s % 2], das[...])
            for task in range(2):
                acc1[c, task] += g[:, task * CH:(task + 1) * CH].reshape(2, 2, 2, 96, CH)

        def add_down(t, c, us):
            g = dot_tn(us[...], dz[t])
            for task in range(2):
                acc2[c, task] += g[:, task * D:(task + 1) * D].reshape(2, 2, 2, 32, D)

        def step(s, carry):
            c, k, b = step_of(s)
            t = k * 2 + b
            prepare(s)

            @pl.when(c == 0)
            def _():
                @pl.when(jnp.logical_and(b == 0, k > 0))
                def _():
                    e_copy(k).wait_recv()

                e = eall[k, :, pl.ds(pl.multiple_of(b * TB, TB), TB)]
                e1 = e.astype(BF).astype(F32)
                rest = e - e1
                e2 = rest.astype(BF).astype(F32)
                e3 = rest - e2
                es = jnp.concatenate([e1, e2, e3], axis=0).astype(BF)
                dz[t] = dot_tn(es, hbd[...]).astype(BF)

            us = us_all.at[0]
            d_act(s, t, us)
            add_down(t, c, us)
            add_up(s, c)

            @pl.when(s == 11)
            def _():
                for sc in whole(0):
                    sc.start()

            @pl.when(s == 12)
            def _():
                for sc in whole(0):
                    sc.side()

            @pl.when(s == 15)
            def _():
                for sc in whole(1):
                    sc.start()

            return carry

        lax.fori_loop(0, 16, step, 0)

        def last_step(s, carry):
            c, k, b = step_of(s)
            t = k * 2 + b
            prepare(s)
            d_act(s, t, us_all.at[t])
            add_up(s, c)

            @pl.when(s == 16)
            def _():
                for sc in whole(0):
                    sc.last()
                for sc in whole(1):
                    sc.side()

            @pl.when(s == 19)
            def _():
                for sc in whole(0):
                    sc.done()
                finish(acc1, sh1_hbm, 0, 0)
                finish(acc2, sh2_hbm, 0, 1)

            @pl.when(s == 21)
            def _():
                for sc in whole(1):
                    sc.last()

            return carry

        lax.fori_loop(16, 24, last_step, 0)
        for sc in up_last:
            sc.start()

        def down_pass(task):
            def two_blocks(i, carry):
                g = dot_tn(us_all[i * 2], dz[i * 2, :, task * D:(task + 1) * D])
                g = g + dot_tn(us_all[i * 2 + 1], dz[i * 2 + 1, :, task * D:(task + 1) * D])
                acc2[LAST, task] += g.reshape(2, 2, 2, 32, D)

                @pl.when(i == 1)
                def _():
                    if task == 0:
                        for sc in up_last:
                            sc.side()
                    else:
                        for sc in down_last[0]:
                            sc.side()

                return carry

            lax.fori_loop(0, 4, two_blocks, 0)
            for sc in down_last[task]:
                sc.start()

        down_pass(0)
        for sc in whole(1):
            sc.done()
        finish(acc1, sh1_hbm, 1, 0)
        finish(acc2, sh2_hbm, 1, 1)
        down_pass(1)

    pl.run_scoped(backward, pltpu.VMEM((2, TB, D), BF), pltpu.VMEM((8, TB, CH), BF), pltpu.VMEM((TB, 2 * CH), BF))

    for sc in up_last:
        sc.last()
    for sc in down_last[1]:
        sc.side()
    for sc in down_last[0]:
        sc.last()
    for sc in up_last:
        sc.done()
    finish(acc1, sh1_hbm, LAST, 0)
    for sc in down_last[1]:
        sc.last()
    for sc in down_last[0]:
        sc.done()
    for sc in down_last[1]:
        sc.done()
    finish(acc2, sh2_hbm, LAST, 1)

    def full(v):
        return jnp.sum(jnp.sum(v, axis=0, keepdims=True), axis=1, keepdims=True)

    row = lax.broadcasted_iota(jnp.int32, (8, 128), 0)
    mbuf[j] = jnp.where(row == 0, full(gm[0]), jnp.where(row == 1, full(gm[1]), full(gm[2])))

    def m_copy(i):
        return remote(mbuf.at[j], mbuf.at[j], mss.at[i], mrs.at[i], z, (j + i) % 8)

    for i in range(1, 8):
        m_copy(i).start()
    for i in range(1, 8):
        m_copy(i).wait_recv()
    total = mbuf[0]
    for i in range(1, 8):
        total = total + mbuf[i]
    nbuf[z] = total

    def n_copy(k):
        return remote(nbuf.at[z], nbuf.at[z], nss.at[k], nrs.at[k], pos.zmate(k), j)

    for k in (1, 2, 3):
        n_copy(k).start()

    for k in (1, 2, 3):
        e_copy(k).wait_send()
    for sc in whole(0) + whole(1) + up_last + down_last[0] + down_last[1]:
        sc.drain()
    for i in range(1, 8):
        m_copy(i).wait_send()
    for c in range(NCH):
        for t in range(2):
            pltpu.make_async_copy(shard(acc1, c, t), sh1_hbm.at[c, t], sh_sem.at[c, 0, t]).wait()
            pltpu.make_async_copy(shard(acc2, c, t), sh2_hbm.at[c, t], sh_sem.at[c, 1, t]).wait()

    for k in (1, 2, 3):
        n_copy(k).wait_recv()
    gram = nbuf[0]
    for k in (1, 2, 3):
        gram = gram + nbuf[k]
    g00, g01, g11 = gram[0:1, :], gram[1:2, :], gram[2:3, :]
    scale = (g00 + g11) / 2.0

    def eg_step(i, weights):
        a0, a1 = weights
        v0 = a0 * jnp.exp(-(g00 * a0 + g01 * a1) / scale)
        v1 = a1 * jnp.exp(-(g01 * a0 + g11 * a1) / scale)
        tot = v0 + v1
        return v0 / tot, v1 / tot

    half = jnp.full((1, 128), 0.5, F32)
    a0, a1 = lax.fori_loop(0, STEPS, eg_step, (half, half))
    aw_ref[...] = jnp.where(row == 0, a0, a1)
    for k in (1, 2, 3):
        n_copy(k).wait_send()


def main_call(x, w1, w2r, heads, labels):
    dma = pltpu.SemaphoreType.DMA
    anyspec = pl.BlockSpec(memory_space=pl.ANY)
    vspec = pl.BlockSpec(memory_space=pltpu.VMEM)
    return pl.pallas_call(
        main_kernel,
        out_shape=(jax.ShapeDtypeStruct((NCH, NTOK, CH), F32),
                   jax.ShapeDtypeStruct((NCH, 2, 96, CH), F32),
                   jax.ShapeDtypeStruct((NCH, 2, 32, D), F32),
                   jax.ShapeDtypeStruct((8, 128), F32)),
        in_specs=[anyspec] * 5,
        out_specs=(anyspec, anyspec, anyspec, vspec),
        scratch_shapes=[
            pltpu.VMEM((8, TB, 2 * D), BF),
            pltpu.VMEM((NCH, 8, 32, 2 * D), BF),
            pltpu.VMEM((NCH, 2, 2, 2, 2, 96, CH), F32),
            pltpu.VMEM((NCH, 2, 2, 2, 2, 32, D), F32),
            pltpu.VMEM((NCH, 2, 2, 2, 96, CH), F32),
            pltpu.VMEM((NCH, 2, 2, 2, 32, D), F32),
            pltpu.VMEM((NCH, 2, 2, 96, CH), F32),
            pltpu.VMEM((NCH, 2, 2, 32, D), F32),
            pltpu.VMEM((NCH, 2, 96, CH), F32),
            pltpu.VMEM((NCH, 2, 32, D), F32),
            pltpu.VMEM((4, ER, NOWN), F32),
            pltpu.VMEM((NCH, TB, CH), F32),
            pltpu.VMEM((3 * ER, 2 * D), BF),
            pltpu.VMEM((ER, D), BF),
            pltpu.VMEM((2, D, NC), BF),
            pltpu.VMEM((2, NOWN), jnp.int32),
            pltpu.VMEM((3, 8, 128), F32),
            pltpu.VMEM((8, 8, 128), F32),
            pltpu.VMEM((4, 8, 128), F32),
            dma((NG,)), dma((NG,)), dma((NG,)), dma((NG,)), dma((NG,)), dma((NG,)),
            dma((NG,)), dma((NG,)), dma((NG, 4)), dma((NG, 4)),
            dma((5,)), dma((NCH,)), dma((2,)), dma((NCH,)), dma((4,)), dma((4,)),
            dma((6 * NCH, 3)), dma((6 * NCH, 3)), dma((8,)), dma((8,)), dma((4,)), dma((4,)), dma((NCH, 2, 2)),
        ],
        compiler_params=pltpu.CompilerParams(
            collective_id=0, has_side_effects=True, vmem_limit_bytes=VMEM_BYTES),
        name='main',
    )(x, w1, w2r, heads, labels)


def result_kernel(aw_ref, sh1, sh2, a_ref, g1_ref, g2_ref):
    a0, a1 = aw_ref[0:1, :], aw_ref[1:2, :]
    a_ref[0] = aw_ref[0, 0]
    a_ref[1] = aw_ref[1, 0]
    b0 = jnp.concatenate([a0] * 6, axis=1)
    b1 = jnp.concatenate([a1] * 6, axis=1)
    for c in range(NCH):
        comb = b0[:, 0:CH] * sh1[c, 0] + b1[:, 0:CH] * sh1[c, 1]
        for g in range(8):
            g1_ref[:, g * 96 + c * 32:g * 96 + c * 32 + 32] = comb[:, g * 32:g * 32 + 32]
        g2_ref[c * 32:(c + 1) * 32, :] = b0 * sh2[c, 0] + b1 * sh2[c, 1]


def result_call(aw, sh1, sh2):
    vspec = pl.BlockSpec(memory_space=pltpu.VMEM)
    return pl.pallas_call(
        result_kernel,
        out_shape=(jax.ShapeDtypeStruct((2,), F32), jax.ShapeDtypeStruct((96, FL), F32),
                   jax.ShapeDtypeStruct((96, D), F32)),
        in_specs=[vspec] * 3,
        out_specs=(pl.BlockSpec(memory_space=pltpu.SMEM), vspec, vspec),
        name='result',
    )(aw, sh1, sh2)


def solution(mesh):
    def local_step(tokens, w_up, w_down, task_heads, labels):
        w2r = w_down.reshape(8, NCH, 32, D)
        _, sh1, sh2, aw = main_call(tokens, w_up, w2r, task_heads, labels)
        return result_call(aw, sh1, sh2)

    return jax.shard_map(
        local_step, mesh=mesh,
        in_specs=(P('data', None), P(None, 'model'), P('model', None), P(None, None, None), P(None, 'data')),
        out_specs=(P(None), P('data', 'model'), P(('model', 'data'), None)),
        check_vma=False)
```

time: 1310 us -> 173 us (0.13)
  waiting for transfers between devices: 942 us -> 0 us
  matrix products: 230 us -> 0 us
  Pallas kernels: 0 us -> 170 us
  local copies, waits for them, and re-layouts: 43 us -> 1.79 us
  blocking collectives: 39.8 us -> 0 us
  other arithmetic: 28.3 us -> 0 us
  between operations: 15.9 us -> 0.8 us
    psum x1 -> x0, waiting for transfers between devices: 807 us -> none  [local_step(): mlp_out = lax.psum(part_out, 'model')]
    dot_general x10 -> x0, matrix products: 216 us -> none  [the longest x1 60.2 us: local_step(): jnp.einsum('tbd,fd->tbf', d_trunk, w_down, preferred_element_type=jnp.flo...]
    pallas_call x0 -> x2, Pallas kernels: none -> 170 us  [the longest x1 168 us: main_call(): pl.pallas_call(main_kernel, out_shape=(jax.ShapeDtypeStruct((NCH, NTOK, C...]
    unnamed x3 -> x0, waiting for transfers between devices: 135 us -> none
    psum x1 -> x0, blocking collectives: 39.8 us -> none  [local_step(): gram_mat = lax.psum(gram_part, ('model', 'data'))]
    add_any x1 -> x0, local copies, waits for them, and re-layouts: 25.2 us -> none  [local_step(): jax.jvp(jax.nn.gelu, (pre_act,), (jnp.ones_like(pre_act),))]
    transpose x2 -> x0, local copies, waits for them, and re-layouts: 16.4 us -> none  [the longest x1 8.19 us: local_step(): jnp.einsum('bd,tbf->tdf', tokens, d_pre, preferred_element_type=jnp.float32)]
    reduce_sum x41 -> x0, other arithmetic: 15.3 us -> none  [the longest x20 12.4 us: eg_step(): return updated / jnp.sum(updated)]
  transfers between devices with their start and end apart: 2 -> 0, of which waited for: 2 -> 0; matrix products, arithmetic and copies ran while one was open for 2% -> 0% of each run, Pallas kernels for 0% -> 0%
where the time goes in v2:
time: 173 us
  Pallas kernels  170 us (98%)
  local copies, waits for them, and re-layouts  1.79 us (1%)
    pallas_call x1, Pallas kernels, main_call(): pl.pallas_call(main_kernel, out_shape=(jax.ShapeDtypeStruct((NCH, NTOK, C...  168 us

profile of v2, /device:TPU:0, one launch (start us, length us, event | category | flops | bytes accessed | tf_op | source)
XLA Modules:
  0.0 173.0 jit_solution(4760390707821888741)
XLA Ops:
  0.6 1.8 %copy.8.heads_hbm = bf16[2,768,19]{2,1,0:T(8,128)(2,1)} copy(bf16[2,768,19]{1,0,2:T(2,128)(2,1)} %param.8) | data formatting | bytes 116736 | tf_op args[3]
  2.4 168.2 %main.1 = (f32[3,8192,256]{2,1,0:T(8,128)}, f32[3,2,96,256]{3,2,1,0:T(8,128)}, f32[3,2,32,768]{3,2,1,0:T(8,128)}, f32[8,128]{1,0:T(8,128)}) custom-call(bf16[8192,768]{1,0:T(8,128)(2,1)} %x_hbm.1, bf16[768,768]{1,0:T(8,128)(2,1)} %w1_hbm.1, bf16[8,3,32,768]{3,2,1,0:T(8,128)(2,1)} %bitcast.1, bf16[2,768,19]{2,1,0:T(8,128)(2,1)} %copy.8.heads_hbm, ...), custom_call_target="tpu_custom_call" | custom-call | tf_op jit(solution)/shard_map/main/pallas_call | solution.py:652
  170.6 2.2 %result.1 = (f32[2]{0:T(128)}, f32[96,768]{1,0:T(8,128)}, f32[96,768]{1,0:T(8,128)}) custom-call(f32[8,128]{1,0:T(8,128)} %get-tuple-element.6.aw_ref, f32[3,2,96,256]{3,2,1,0:T(8,128)} %get-tuple-element.7.sh1, f32[3,2,32,768]{3,2,1,0:T(8,128)} %get-tuple-element.8.sh2), custom_call_target="tpu_custom_call" | custom-call | tf_op jit(solution)/shard_map/result/pallas_call | solution.py:706

commit v3 on v2

v3 whole, which is shorter than its diff:
```python
import jax
import jax.numpy as jnp
from jax import lax
from jax.experimental import pallas as pl
from jax.experimental.pallas import tpu as pltpu
from jax.sharding import PartitionSpec as P

STEPS = 20
BF = jnp.bfloat16
F32 = jnp.float32
MESH = pl.DeviceIdType.MESH
VMEM_BYTES = 67043328

D = 768
DD = D + D
NTOK = 8192
NOWN = 2048
TB = 1024
SUB = 256
NC = 19
ER = 40
CH = 256
NCH = 3
LAST = NCH - 1
NG = NCH * NCH
FAR = NG - NCH
GR = 32
OWN = CH // GR * 12
LO = slice(D)
HI = slice(D, DD)
SIDES = (LO, HI)
TWO = range(2)
MATES = range(1, 8)
LINE = range(1, 4)
BLOCKS = range(TB // SUB)
NDEV = 32

G0 = 0.7978845608028654
G1C = 0.044715 * G0


def dot_nn(a, b):
    return lax.dot_general(a, b, (((1,), (0,)), ((), ())), preferred_element_type=F32)


def dot_nt(a, b):
    return lax.dot_general(a, b, (((1,), (1,)), ((), ())), preferred_element_type=F32)


def dot_tn(a, b):
    return lax.dot_general(a, b, (((0,), (0,)), ((), ())), preferred_element_type=F32)


def gelu(x):
    t = jnp.tanh(x * (G0 + G1C * (x * x)))
    h = 0.5 * x
    return h + h * t


def gelu_and_slope(x):
    x2 = x * x
    t = jnp.tanh(x * (G0 + G1C * x2))
    h = 0.5 * x
    u = h + h * t
    s = 0.5 + 0.5 * t + h * (1.0 - t * t) * (G0 + (3.0 * G1C) * x2)
    return u, s


class Place:
    def __init__(self):
        self.z = lax.axis_index('model')
        self.j = lax.axis_index('data')
        self.core = self.j % 2
        self.x = (self.j // 2) % 2
        self.y = self.j // 4
        self.jc = self.j + 1 - 2 * self.core
        self.jx = self.j + 2 - 4 * self.x
        self.jy = self.j + 4 - 8 * self.y
        self.jd = self.jx + 4 - 8 * self.y
        self.js = self.jx + self.core * (self.jy - self.jx)
        self.j2 = self.jx + self.jy - self.js

        self.inner = self.z % 3 > 0
        self.pair = self.z + 1 - 2 * (self.z % 2)
        self.mirror = 3 - self.z
        half = self.z // 2
        self.shares = (self.z, self.pair, 2 - half, 3 - 3 * half)

    def share(self, k):
        own, near, far, end = self.shares
        return jnp.where(k == 0, own, jnp.where(k == 1, near, jnp.where(k == 2, far, end)))


def remote(src, dst, ssem, rsem, z, j):
    return pltpu.make_async_remote_copy(
        src_ref=src, dst_ref=dst, send_sem=ssem, recv_sem=rsem, device_id=(z, j), device_id_type=MESH)


class Scatter:
    def __init__(self, pos, acc, r1, r2, r3, lanes, sems, idx, x_first):
        self.pos, self.acc, self.r1, self.r2, self.r3 = pos, acc, r1, r2, r3
        self.lanes, self.sems, self.idx, self.x_first = lanes, sems, idx, x_first

    def copy(self, stage):
        p, ln = self.pos, self.lanes
        ssem, rsem = self.sems[0].at[self.idx, stage], self.sems[1].at[self.idx, stage]
        if stage == 0:
            return remote(self.acc.at[:, :, 1 - p.core, :, ln], self.r1.at[:, :, :, ln], ssem, rsem, p.z, p.jc)
        if stage == 1:
            if self.x_first:
                return remote(self.acc.at[:, 1 - p.x, p.core, :, ln], self.r2.at[:, :, ln], ssem, rsem, p.z, p.jx)
            return remote(self.acc.at[1 - p.y, :, p.core, :, ln], self.r2.at[:, :, ln], ssem, rsem, p.z, p.jy)
        if self.x_first:
            return remote(self.acc.at[1 - p.y, p.x, p.core, :, ln], self.r3.at[:, ln], ssem, rsem, p.z, p.jy)
        return remote(self.acc.at[p.y, 1 - p.x, p.core, :, ln], self.r3.at[:, ln], ssem, rsem, p.z, p.jx)

    def start(self):
        self.copy(0).start()

    def side(self):
        p, ln = self.pos, self.lanes
        self.copy(0).wait_recv()
        for yy in TWO:
            for xx in TWO:
                self.acc[yy, xx, p.core, :, ln] += self.r1[yy, xx, :, ln]
        self.copy(1).start()

    def last(self):
        p, ln = self.pos, self.lanes
        self.copy(1).wait_recv()
        for i in TWO:
            if self.x_first:
                self.acc[i, p.x, p.core, :, ln] += self.r2[i, :, ln]
            else:
                self.acc[p.y, i, p.core, :, ln] += self.r2[i, :, ln]
        self.copy(2).start()

    def done(self):
        p, ln = self.pos, self.lanes
        self.copy(2).wait_recv()
        self.acc[p.y, p.x, p.core, :, ln] += self.r3[:, ln]

    def drain(self):
        for stage in range(3):
            self.copy(stage).wait_send()


def main_kernel(x_hbm, w1_hbm, w2_hbm, heads_hbm, lab_hbm,
                a_hbm, sh1_hbm, sh2_hbm, aw_ref,
                dz, wown, acc1, acc2, r1a, r1b, r2a, r2b, r3a, r3b, eall, ast, xbuf, hbd, hcat, heads, lab_v,
                gm, mbuf,
                zss, zfs, zrs, zgs, zqs, xss, xrs, yss, yrs, dss, drs, css, crs,
                ld_sem, w2_sem, xs_sem, as_sem, ess, efs, ers,
                rss, rsr, mss, mrs, sh_sem):
    pos = Place()
    z, j, inner = pos.z, pos.j, pos.inner
    outer = jnp.logical_not(inner)

    barrier = pltpu.get_barrier_semaphore()
    me = z * 8 + j

    def greet(i, carry):
        to = (me + i) % NDEV
        pl.semaphore_signal(barrier, device_id=(to // 8, to % 8), device_id_type=MESH)
        return carry

    lax.fori_loop(1, NDEV, greet, 0)

    own_x, act, room = dz.at[0], dz.at[2], dz.at[3]
    w1_raw = room.at[LO, LO]
    w1_nat = room.at[LO, D:D + CH]
    w1_own = dz.at[4, LO, HI]

    def sub(m):
        return slice((m % 4) * SUB, (m % 4 + 1) * SUB)

    def xo_at(m):
        return own_x.at[sub(m), HI if m >= 4 else LO]

    def us_at(m):
        lane = D + (m // 4) * CH
        return act.at[sub(m), lane:lane + CH]

    def share_row(k, b):
        return pl.multiple_of((pos.share(k) * 2 + b) * TB, TB)

    own_row = pl.multiple_of(z * NOWN, NOWN)
    ld_w1 = pltpu.make_async_copy(w1_hbm, w1_raw, ld_sem.at[0])
    ld_x = [pltpu.make_async_copy(x_hbm.at[pl.ds(own_row + b * TB, TB)], own_x.at[:, SIDES[b]], ld_sem.at[1 + b])
            for b in TWO]
    ld_l = pltpu.make_async_copy(lab_hbm.at[:, pl.ds(own_row, NOWN)], lab_v, ld_sem.at[3])
    ld_h = pltpu.make_async_copy(heads_hbm, heads, ld_sem.at[4])
    ld_w2 = [pltpu.make_async_copy(w2_hbm.at[:, c], wown.at[c, :, :, HI], w2_sem.at[c]) for c in range(NCH)]

    def stream_half(i):
        return dz.at[1 + 3 * (i % 2), :, LO]

    def xs_load(i):
        return pltpu.make_async_copy(
            x_hbm.at[pl.ds(share_row(1 + i // 2, i % 2), TB)], stream_half(i), xs_sem.at[i % 2])

    ld_w1.start()
    for cp in ld_w2:
        cp.start()
    xs_load(0).start()
    for cp in ld_x:
        cp.start()
    ld_h.start()
    ld_l.start()

    ld_w1.wait()
    w1t = w1_raw[...].T
    for c in range(NCH):
        for g in range(8):
            row = g * NCH * GR + c * GR
            wown[c, g, :, LO] = w1t[row:row + GR, :]
    for cp in ld_w2:
        cp.wait()
    pl.semaphore_wait(barrier, NDEV - 1)

    def piece(i, jj):
        row = pl.multiple_of((i % NCH) * CH + jj * GR, GR)
        return dz.at[5 + i // NCH, pl.ds(row, GR), :]

    def z_pair(c):
        return remote(wown.at[c, j], piece(c, j), zss.at[c], zrs.at[c], pos.pair, j)

    def z_mirror(c):
        return remote(wown.at[c, j], piece(NCH + c, j), zss.at[NCH + c], zrs.at[NCH + c], pos.mirror, j)

    def z_forward(i):
        first = i < NCH
        to = jnp.where(first, i + 2 * NCH, i)
        return remote(piece(i, j), piece(to, j), zfs.at[i], zrs.at[to], jnp.where(first, pos.mirror, pos.pair), j)

    def more_forward(i):
        first = i < NCH
        to = jnp.where(first, i + 2 * NCH, i)
        return remote(piece(i, pos.j2), piece(to, pos.j2), zgs.at[i], zqs.at[to], jnp.where(first, pos.mirror, pos.pair), j)

    def side_copy(i):
        return remote(piece(i, j), piece(i, j), xss.at[i], xrs.at[i], z, pos.js)

    def more_copy(i):
        return remote(piece(i, pos.j2), piece(i, pos.j2), dss.at[i], drs.at[i], z, pos.js)

    def x_copy(i):
        return remote(piece(i, j), piece(i, j), xss.at[i], xrs.at[i], z, pos.jx)

    def y_copy(i):
        return remote(piece(i, j), piece(i, j), yss.at[i], yrs.at[i], z, pos.jy)

    def diag_copy_y(i):
        return remote(piece(i, pos.jx), piece(i, pos.jx), dss.at[i], drs.at[i], z, pos.jy)

    def diag_copy_x(i):
        return remote(piece(i, pos.jy), piece(i, pos.jy), dss.at[i], drs.at[i], z, pos.jx)

    def core_copy(i, q):
        jj = (j, pos.jx, pos.jy, pos.jd)[q]
        return remote(piece(i, jj), piece(i, jj), css.at[i, q], crs.at[i, q], z, pos.jc)

    def core_side(i, q):
        jj = (j, pos.js, pos.j2, pos.jd)[q]
        return remote(piece(i, jj), piece(i, jj), css.at[i, q], crs.at[i, q], z, pos.jc)

    def take(i):
        remote(piece(i, j), piece(i, j), zfs.at[i], zrs.at[i], pos.pair, j).wait_recv()

        @pl.when(inner)
        def _():
            z_forward(i).start()

    def take_both(i):
        remote(piece(i, j), piece(i, j), zfs.at[i], zrs.at[i], pos.pair, j).wait_recv()
        remote(piece(i, j), piece(i, j), zgs.at[i], zqs.at[i], pos.pair, j).wait_recv()

        @pl.when(inner)
        def _():
            z_forward(i).start()
            more_forward(i).start()

    def send_both(i):
        side_copy(i).start()
        more_copy(i).start()
        core_side(i, 0).start()
        core_side(i, 2).start()

    def pass_both(i):
        side_copy(i).wait_recv()
        core_side(i, 1).start()
        more_copy(i).wait_recv()
        core_side(i, 3).start()

    def take_if(cond, i):
        @pl.when(cond)
        def _():
            take(i)

    def send_own(i):
        x_copy(i).start()
        y_copy(i).start()
        core_copy(i, 0).start()

    def send_side(i):
        x_copy(i).wait_recv()

        @pl.when(pos.core == 0)
        def _():
            diag_copy_y(i).start()

        core_copy(i, 1).start()
        y_copy(i).wait_recv()

        @pl.when(pos.core == 1)
        def _():
            diag_copy_x(i).start()

        core_copy(i, 2).start()

    def more_on(i):
        @pl.when(inner)
        def _():
            more_forward(i).start()

    def send_diag(i):
        diag_copy_y(i).wait_recv()
        core_copy(i, 3).start()

    for c in range(NCH):
        z_pair(c).start()

    @pl.when(inner)
    def _():
        for c in range(NCH):
            z_mirror(c).start()

    def a_store(src, c, row, sem):
        return pltpu.make_async_copy(src, a_hbm.at[c, pl.ds(pl.multiple_of(row, TB), TB)], as_sem.at[sem])

    def forward(facc):
        for c in range(NCH):
            w1_own[:, c * CH:(c + 1) * CH] = wown[c, :, :, LO].reshape(CH, D).T

        def staged(i, c):
            rows = pl.ds(pl.multiple_of((i % 2) * TB, TB), TB)
            return a_store(facc.at[rows, c * CH:(c + 1) * CH], c, share_row(1 + i // 2, i % 2), (i % 2) * NCH + c)

        def other_tokens(i, carry):
            xs_load(i).wait()

            @pl.when(i < 5)
            def _():
                xs_load(i + 1).start()

            @pl.when(i >= 2)
            def _():
                for c in range(NCH):
                    staged(i, c).wait()

            base = (i % 2) * TB
            for m in BLOCKS:
                rows = pl.ds(pl.multiple_of(base + m * SUB, SUB), SUB)
                facc[rows, :] = dot_nn(stream_half(i)[sub(m), :], w1_own[...])
            for c in range(NCH):
                staged(i, c).start()

            @pl.when(i == 2)
            def _():
                take(0)
                send_own(0)
                take_if(inner, 3)

            @pl.when(i == 3)
            def _():
                take(1)
                send_own(1)
                take_if(inner, 4)

            @pl.when(i == 4)
            def _():
                take_if(inner, 5)

            @pl.when(i == 5)
            def _():
                take(2)
                send_own(2)
                send_side(0)
                more_on(0)

            return carry

        lax.fori_loop(0, 6, other_tokens, 0)
        for cp in ld_x:
            cp.wait()

        for b in TWO:
            for c in range(NCH):
                staged(b, c).wait()
            for m in BLOCKS:
                a = dot_nn(xo_at(b * 4 + m)[...], w1_own[...])
                for c in range(NCH):
                    ast[c, sub(m), :] = a[:, c * CH:(c + 1) * CH]
                act[sub(m), LO] = gelu(a).astype(BF)
            for m in BLOCKS:
                facc[b * TB + m * SUB:b * TB + (m + 1) * SUB, :] = dot_nn(
                    act[sub(m), LO], wown[:, :, :, HI].reshape(D, D))
            for c in range(NCH):
                a_store(ast.at[c], c, (z * 2 + b) * TB, c).start()
            if b == 0:
                send_side(1)
                more_on(1)
                send_diag(0)
                take_if(outer, 3)
                send_own(3)
                for c in range(NCH):
                    a_store(ast.at[c], c, z * NOWN, c).wait()
            else:
                send_side(2)
                more_on(2)

                @pl.when(inner)
                def _():
                    take_both(FAR)

        def granule(n, carry):
            for q in range(4):
                core_copy(n, q).wait_recv()
            gran = dz.at[5 + n // NCH, pl.ds(pl.multiple_of((n % NCH) * CH, CH), CH), :]
            w1_nat[...] = gran[:, LO].T
            for m in range(8):
                us_at(m)[...] = gelu(dot_nn(xo_at(m)[...], w1_nat[...])).astype(BF)
            for m in range(8):
                facc[m * SUB:(m + 1) * SUB, :] += dot_nn(us_at(m)[...], gran[:, HI])

            @pl.when(jnp.logical_and(n > 0, n + 2 < FAR))
            def _():
                send_side(n + 2)

            @pl.when(n + 1 < FAR)
            def _():
                send_diag(n + 1)

            @pl.when(jnp.logical_and(n + 1 >= FAR, n + 1 < NG))
            def _():
                pass_both(n + 1)

            @pl.when(n + 4 < FAR)
            def _():
                take_if(outer, n + 4)
                send_own(n + 4)

            @pl.when(jnp.logical_and(n + 4 >= FAR, n + 4 < NG))
            def _():
                @pl.when(outer)
                def _():
                    take_both(n + 4)

                send_both(n + 4)

            @pl.when(jnp.logical_and(inner, n < LAST))
            def _():
                take_both(n + FAR + 1)

            @pl.when(n < NCH)
            def _():
                acc1[n] = jnp.zeros(acc1.shape[1:], F32)
                acc2[n] = jnp.zeros(acc2.shape[1:], F32)

            return carry

        lax.fori_loop(0, NG, granule, 0)
        for m in range(8):
            xo_at(m)[...] = (xo_at(m)[...].astype(F32) + facc[m * SUB:(m + 1) * SUB, :]).astype(BF)

    ld_h.wait()
    hf = jnp.concatenate([heads[i].astype(F32) for i in range(NC)] + [jnp.zeros((2, D), F32)], axis=0)
    hcat[...] = hf.astype(BF)
    r = lax.broadcasted_iota(jnp.int32, (ER, D), 0)
    hb = jnp.concatenate([jnp.where(r % 2 == 0, hf, 0.0), jnp.where(r % 2 == 1, hf, 0.0)], axis=1)
    hbd[...] = jnp.concatenate([hb, hb, hb], axis=0).astype(BF)
    gm[...] = jnp.zeros_like(gm)

    pl.run_scoped(forward, pltpu.VMEM((NOWN, D), F32))

    for c in range(NCH):
        a_store(ast.at[c], c, z * NOWN, c).wait()

    def e_half(k, b):
        return eall.at[k, :, pl.ds(pl.multiple_of(b * TB, TB), TB)]

    def e_pair(b):
        return remote(e_half(0, b), e_half(1, b), ess.at[0, b], ers.at[1, b], pos.pair, j)

    def e_mirror(b):
        return remote(e_half(0, b), e_half(2, b), ess.at[1, b], ers.at[2, b], pos.mirror, j)

    def e_forward(k, b):
        to = 3 if k == 1 else k
        return remote(e_half(k, b), e_half(to, b), efs.at[k, b], ers.at[to, b], pos.mirror if k == 1 else pos.pair, j)

    def e_wait(k, b):
        remote(e_half(k, b), e_half(k, b), efs.at[k, b], ers.at[k, b], pos.pair, j).wait_recv()

    def step_of(s):
        return s // 8, (s % 8) // 2, s % 2

    def a_load(s):
        c, k, b = step_of(s)
        return pltpu.make_async_copy(a_hbm.at[c, pl.ds(share_row(k, b), TB)], ast.at[s % 2], as_sem.at[s % 2])

    def x_load(s):
        c, k, b = step_of(s)
        return pltpu.make_async_copy(x_hbm.at[pl.ds(share_row(k, b), TB)], xbuf.at[s % 2], xs_sem.at[s % 2])

    a_load(0).start()
    x_load(0).start()

    ld_l.wait()
    r = lax.broadcasted_iota(jnp.int32, (ER, TB), 0)
    first = r % 2 == 0
    real = r < 2 * NC
    neg = jnp.float32(-jnp.inf)
    for b in TWO:
        cols = slice(b * TB, (b + 1) * TB)
        logit = jnp.where(real, dot_nt(hcat[...], own_x[:, SIDES[b]]), neg)
        m0 = jnp.max(jnp.where(first, logit, neg), axis=0, keepdims=True)
        m1 = jnp.max(jnp.where(first, neg, logit), axis=0, keepdims=True)
        ex = jnp.exp(logit - jnp.where(first, m0, m1))
        s0 = jnp.sum(jnp.where(first, ex, 0.0), axis=0, keepdims=True)
        s1 = jnp.sum(jnp.where(first, 0.0, ex), axis=0, keepdims=True)
        prob = ex / jnp.where(first, s0, s1)
        lab = jnp.where(first, lab_v[0:1, cols], lab_v[1:2, cols])
        hot = jnp.where(jnp.logical_and(r // 2 == lab, real), 1.0, 0.0)
        eall[0, :, cols] = (prob - hot) / (NTOK * 8.0)
        e_pair(b).start()

        @pl.when(inner)
        def _():
            e_mirror(b).start()

    def drain(i, carry):
        x_copy(i).wait_send()
        diag_copy_y(i).wait_send()
        for q in range(4):
            core_copy(i, q).wait_send()

        @pl.when(i < FAR)
        def _():
            y_copy(i).wait_send()

        @pl.when(inner)
        def _():
            z_forward(i).wait_send()

            @pl.when(jnp.logical_or(i < NCH, i >= FAR))
            def _():
                more_forward(i).wait_send()

        return carry

    lax.fori_loop(0, NG, drain, 0)
    for c in range(NCH):
        z_pair(c).wait_send()

    @pl.when(inner)
    def _():
        for c in range(NCH):
            z_mirror(c).wait_send()

    everything = slice(None)
    sems = (rss, rsr)

    def up(c, t):
        return Scatter(pos, acc1.at[c, t], r1a.at[c, t], r2a.at[c, t], r3a.at[c, t], everything, sems,
                       c * 6 + t, t == 0)

    def down(c, t, part=None):
        if part is None:
            lanes, idx, x_first = everything, c * 6 + 2 + t, t == 0
        else:
            lanes, idx, x_first = slice(part * (D // 2), (part + 1) * (D // 2)), c * 6 + 2 + t * 2 + part, part == 0
        return Scatter(pos, acc2.at[c, t], r1b.at[c, t], r2b.at[c, t], r3b.at[c, t], lanes, sems, idx, x_first)

    ups = [[up(c, t) for t in TWO] for c in range(NCH)]
    downs = [[down(c, t) for t in TWO] for c in range(LAST)]
    tails = [[down(LAST, t, part) for part in TWO] for t in TWO]

    def each(group, stage):
        for sc in group:
            getattr(sc, stage)()

    def fold(v):
        rows, cols = v.shape
        total = jnp.zeros((8, 128), F32)
        for q in range(cols // 128):
            total = total + jnp.sum(v[:, q * 128:(q + 1) * 128].reshape(rows // 8, 8, 128), axis=0)
        return total

    def shard(acc, c, t):
        return acc.at[c, t, pos.y, pos.x, pos.core]

    def out_copy(acc, out, c, sem, t):
        return pltpu.make_async_copy(shard(acc, c, t), out.at[c, t], sh_sem.at[c, sem, t])

    def finish(acc, out, c, sem):
        v0, v1 = shard(acc, c, 0)[...], shard(acc, c, 1)[...]
        gm[0] += fold(v0 * v0)
        gm[1] += fold(v0 * v1)
        gm[2] += fold(v1 * v1)
        for t in TWO:
            out_copy(acc, out, c, sem, t).start()

    def finish_chunk(c):
        each(ups[c] + downs[c], 'done')
        finish(acc1, sh1_hbm, c, 0)
        finish(acc2, sh2_hbm, c, 1)

    def backward(us_all, das):
        def prepare(s):
            a_load(s).wait()
            x_load(s).wait()

            @pl.when(s < 23)
            def _():
                a_load(s + 1).start()
                x_load(s + 1).start()

        def d_act(s, us):
            c, k, b = step_of(s)
            w2c = wown[c, :, :, HI].reshape(CH, D)
            for m in BLOCKS:
                u, slope = gelu_and_slope(ast[s % 2, sub(m), :])
                us[sub(m), :] = u.astype(BF)
                for task in TWO:
                    da = dot_nt(dz[k * 2 + b, sub(m), SIDES[task]], w2c)
                    das[sub(m), task * CH:(task + 1) * CH] = (da * slope).astype(BF)

        def add_up(s):
            c, _, _ = step_of(s)
            g = dot_tn(xbuf[s % 2], das[...])
            for task in TWO:
                acc1[c, task] += g[:, task * CH:(task + 1) * CH].reshape(acc1.shape[2:])

        def step(s, carry):
            c, k, b = step_of(s)
            t = k * 2 + b
            prepare(s)

            @pl.when(c == 0)
            def _():
                @pl.when(jnp.logical_and(outer, k > 0))
                def _():
                    e_wait(k, b)

                e = e_half(k, b)[...]
                e1 = e.astype(BF).astype(F32)
                rest = e - e1
                e2 = rest.astype(BF).astype(F32)
                e3 = rest - e2
                es = jnp.concatenate([e1, e2, e3], axis=0).astype(BF)
                dz[t] = dot_tn(es, hbd[...]).astype(BF)

            us = us_all.at[0]
            d_act(s, us)
            add_up(s)
            g = dot_tn(us[...], dz[t])
            for task in TWO:
                acc2[c, task] += g[:, SIDES[task]].reshape(acc2.shape[2:])

            for when, k_f, b_f in ((1, 1, 0), (1, 2, 0), (2, 1, 1), (2, 2, 1), (3, 3, 0), (4, 3, 1)):
                @pl.when(jnp.logical_and(s == when, inner))
                def _():
                    e_forward_after_wait(k_f, b_f)

            @pl.when(s == 7)
            def _():
                each(ups[0] + downs[0], 'start')

            @pl.when(s == 9)
            def _():
                each(ups[0] + downs[0], 'side')

            @pl.when(s == 12)
            def _():
                each(ups[0], 'last')

            @pl.when(s == 13)
            def _():
                each(downs[0], 'last')

            @pl.when(s == 15)
            def _():
                each(ups[1] + downs[1], 'start')

            return carry

        def e_forward_after_wait(k, b):
            e_wait(k, b)
            e_forward(k, b).start()

        lax.fori_loop(0, 16, step, 0)

        def last_step(s, carry):
            c, k, b = step_of(s)
            prepare(s)
            d_act(s, us_all.at[k * 2 + b])
            add_up(s)

            @pl.when(s == 16)
            def _():
                finish_chunk(0)

            @pl.when(s == 17)
            def _():
                each(ups[1] + downs[1], 'side')

            @pl.when(s == 20)
            def _():
                each(ups[1], 'last')

            @pl.when(s == 22)
            def _():
                each(downs[1], 'last')

            return carry

        lax.fori_loop(16, 24, last_step, 0)
        each(ups[LAST], 'start')

        def down_pass(task):
            def two_blocks(i, carry):
                lanes = SIDES[task]
                g = dot_tn(us_all[i * 2], dz[i * 2, :, lanes])
                g = g + dot_tn(us_all[i * 2 + 1], dz[i * 2 + 1, :, lanes])
                acc2[LAST, task] += g.reshape(acc2.shape[2:])

                @pl.when(i == 1)
                def _():
                    each(ups[LAST] if task == 0 else tails[0], 'side')

                return carry

            lax.fori_loop(0, 4, two_blocks, 0)
            each(tails[task], 'start')

        down_pass(0)
        finish_chunk(1)
        down_pass(1)

    pl.run_scoped(backward, pltpu.VMEM((8, TB, CH), BF), pltpu.VMEM((TB, 2 * CH), BF))

    each(ups[LAST], 'last')
    each(tails[1], 'side')
    each(tails[0], 'last')
    each(ups[LAST], 'done')
    finish(acc1, sh1_hbm, LAST, 0)
    each(tails[1], 'last')
    each(tails[0], 'done')
    each(tails[1], 'done')
    finish(acc2, sh2_hbm, LAST, 1)

    def full(v):
        return jnp.sum(jnp.sum(v, axis=0, keepdims=True), axis=1, keepdims=True)

    lane = lax.broadcasted_iota(jnp.int32, (1, 128), 1)
    mbuf[pl.ds(me, 1), :] = jnp.where(lane == 0, full(gm[0]), jnp.where(lane == 1, full(gm[1]), full(gm[2])))

    def m_copy(i):
        to = (me + i) % NDEV
        line = mbuf.at[pl.ds(me, 1), :]
        return remote(line, line, mss.at[i], mrs.at[i], to // 8, to % 8)

    def m_start(i, carry):
        m_copy(i).start()
        return carry

    lax.fori_loop(1, NDEV, m_start, 0)

    for b in TWO:
        e_pair(b).wait_send()

        @pl.when(inner)
        def _():
            e_mirror(b).wait_send()
            for k in LINE:
                e_forward(k, b).wait_send()

    for group in ups + downs + tails:
        each(group, 'drain')
    for c in range(NCH):
        for t in TWO:
            out_copy(acc1, sh1_hbm, c, 0, t).wait()
            out_copy(acc2, sh2_hbm, c, 1, t).wait()

    def m_wait(i, carry):
        m_copy(i).wait()
        return carry

    lax.fori_loop(1, NDEV, m_wait, 0)
    gram = jnp.sum(mbuf[...], axis=0, keepdims=True)

    def entry(i):
        return jnp.sum(jnp.where(lane == i, gram, 0.0), axis=1, keepdims=True)

    g00, g01, g11 = entry(0), entry(1), entry(2)
    scale = (g00 + g11) / 2.0

    def eg_step(i, weights):
        a0, a1 = weights
        v0 = a0 * jnp.exp(-(g00 * a0 + g01 * a1) / scale)
        v1 = a1 * jnp.exp(-(g01 * a0 + g11 * a1) / scale)
        tot = v0 + v1
        return v0 / tot, v1 / tot

    half = jnp.full((1, 1), 0.5, F32)
    a0, a1 = lax.fori_loop(0, STEPS, eg_step, (half, half))
    row = lax.broadcasted_iota(jnp.int32, aw_ref.shape, 0)
    aw_ref[...] = jnp.where(row == 0, a0, a1)


def main_call(x, w1, w2r, heads, labels):
    dma = pltpu.SemaphoreType.DMA
    anyspec = pl.BlockSpec(memory_space=pl.ANY)
    vspec = pl.BlockSpec(memory_space=pltpu.VMEM)
    up, down = (OWN, CH), (GR, D)
    pair, quad, octet = (2,), (2, 2), (2, 2, 2)
    per_chunk = (NCH, 2)
    vmem = pltpu.VMEM
    return pl.pallas_call(
        main_kernel,
        out_shape=(jax.ShapeDtypeStruct((NCH, NTOK, CH), F32),
                   jax.ShapeDtypeStruct(per_chunk + up, F32),
                   jax.ShapeDtypeStruct(per_chunk + down, F32),
                   jax.ShapeDtypeStruct((8, 128), F32)),
        in_specs=[anyspec] * 5,
        out_specs=(anyspec, anyspec, anyspec, vspec),
        scratch_shapes=[
            vmem((8, TB, DD), BF),
            vmem((NCH, 8, GR, DD), BF),
            vmem(per_chunk + octet + up, F32), vmem(per_chunk + octet + down, F32),
            vmem(per_chunk + quad + up, F32), vmem(per_chunk + quad + down, F32),
            vmem(per_chunk + pair + up, F32), vmem(per_chunk + pair + down, F32),
            vmem(per_chunk + up, F32), vmem(per_chunk + down, F32),
            vmem((4, ER, NOWN), F32),
            vmem((NCH, TB, CH), F32),
            vmem((2, TB, D), BF),
            vmem((3 * ER, DD), BF),
            vmem((ER, D), BF),
            vmem((NC, 2, D), BF),
            vmem((2, NOWN), jnp.int32),
            vmem((3, 8, 128), F32), vmem((NDEV, 128), F32),
            dma((6,)), *[dma((NG,)) for _ in range(10)], dma((NG, 4)), dma((NG, 4)),
            dma((5,)), dma((NCH,)), dma(pair), dma((6,)), dma(quad), dma((4, 2)), dma((4, 2)),
            dma((6 * NCH, 3)), dma((6 * NCH, 3)), dma((NDEV,)), dma((NDEV,)), dma((NCH, 2, 2)),
        ],
        compiler_params=pltpu.CompilerParams(
            collective_id=0, has_side_effects=True, vmem_limit_bytes=VMEM_BYTES),
        name='main',
    )(x, w1, w2r, heads, labels)


def result_kernel(aw_ref, sh1, sh2, a_ref, g1_ref, g2_ref):
    a0, a1 = aw_ref[0:1, :], aw_ref[1:2, :]
    a_ref[0] = aw_ref[0, 0]
    a_ref[1] = aw_ref[1, 0]
    b0 = jnp.concatenate([a0] * 6, axis=1)
    b1 = jnp.concatenate([a1] * 6, axis=1)
    for c in range(NCH):
        comb = b0[:, 0:CH] * sh1[c, 0] + b1[:, 0:CH] * sh1[c, 1]
        for g in range(8):
            col = g * NCH * GR + c * GR
            g1_ref[:, col:col + GR] = comb[:, g * GR:(g + 1) * GR]
        g2_ref[c * GR:(c + 1) * GR, :] = b0 * sh2[c, 0] + b1 * sh2[c, 1]


def result_call(aw, sh1, sh2):
    vspec = pl.BlockSpec(memory_space=pltpu.VMEM)
    return pl.pallas_call(
        result_kernel,
        out_shape=(jax.ShapeDtypeStruct((2,), F32), jax.ShapeDtypeStruct((OWN, D), F32),
                   jax.ShapeDtypeStruct((OWN, D), F32)),
        in_specs=[vspec] * 3,
        out_specs=(pl.BlockSpec(memory_space=pltpu.SMEM), vspec, vspec),
        name='result',
    )(aw, sh1, sh2)


def solution(mesh):
    def local_step(tokens, w_up, w_down, task_heads, labels):
        w2r = w_down.reshape(8, NCH, GR, D)
        heads = jnp.transpose(task_heads, (2, 0, 1))
        _, sh1, sh2, aw = main_call(tokens, w_up, w2r, heads, labels)
        return result_call(aw, sh1, sh2)

    return jax.shard_map(
        local_step, mesh=mesh,
        in_specs=(P('data', None), P(None, 'model'), P('model', None), P(None, None, None), P(None, 'data')),
        out_specs=(P(None), P('data', 'model'), P(('model', 'data'), None)),
        check_vma=False)
```

time: 173 us -> 160 us (0.925)
  Pallas kernels: 170 us -> 159 us
  local copies, waits for them, and re-layouts: 1.79 us -> 0 us
    pallas_call x1, Pallas kernels: 168 us -> 157 us  [main_call(): pl.pallas_call(main_kernel, out_shape=(jax.ShapeDtypeStruct((NCH, NTOK, C...]
    unnamed x1 -> x0, local copies, waits for them, and re-layouts: 1.79 us -> none
where the time goes in v3:
time: 160 us
  Pallas kernels  159 us (99%)
    pallas_call x1, Pallas kernels, main_call(): pl.pallas_call(main_kernel, out_shape=(jax.ShapeDtypeStruct((NCH, NTOK, C...  157 us

profile of v3, /device:TPU:0, one launch (start us, length us, event | category | flops | bytes accessed | tf_op | source)
XLA Modules:
  0.0 159.6 jit_solution(2449753977523775647)
XLA Ops:
  0.6 156.5 %main.1 = (f32[3,8192,256]{2,1,0:T(8,128)}, f32[3,2,96,256]{3,2,1,0:T(8,128)}, f32[3,2,32,768]{3,2,1,0:T(8,128)}, f32[8,128]{1,0:T(8,128)}) custom-call(bf16[8192,768]{1,0:T(8,128)(2,1)} %x_hbm.1, bf16[768,768]{1,0:T(8,128)(2,1)} %w1_hbm.1, bf16[8,3,32,768]{3,2,1,0:T(8,128)(2,1)} %bitcast.2, bf16[19,2,768]{2,1,0:T(2,128)(2,1)} %bitcast.3, s32[2,8192]{1,0:T(2,128)} %lab_hbm.1), custom_call_target="tpu_custom_call" | custom-call | tf_op jit(solution)/shard_map/main/pallas_call | solution.py:830
  157.2 2.2 %result.1 = (f32[2]{0:T(128)}, f32[96,768]{1,0:T(8,128)}, f32[96,768]{1,0:T(8,128)}) custom-call(f32[8,128]{1,0:T(8,128)} %get-tuple-element.6.aw_ref, f32[3,2,96,256]{3,2,1,0:T(8,128)} %get-tuple-element.7.sh1, f32[3,2,32,768]{3,2,1,0:T(8,128)} %get-tuple-element.8.sh2), custom_call_target="tpu_custom_call" | custom-call | tf_op jit(solution)/shard_map/result/pallas_call | solution.py:879

commit v4 on v3

--- a/solution.py
+++ b/solution.py
@@ -103,7 +103,7 @@
 
     def copy(self, stage):
         p, ln = self.pos, self.lanes
-        ssem, rsem = self.sems[0].at[self.idx, stage], self.sems[1].at[self.idx, stage]
+        ssem, rsem = self.sems[0].at[stage], self.sems[1].at[self.idx, stage]
         if stage == 0:
             return remote(self.acc.at[:, :, 1 - p.core, :, ln], self.r1.at[:, :, :, ln], ssem, rsem, p.z, p.jc)
         if stage == 1:
@@ -140,16 +140,12 @@
         self.copy(2).wait_recv()
         self.acc[p.y, p.x, p.core, :, ln] += self.r3[:, ln]
 
-    def drain(self):
-        for stage in range(3):
-            self.copy(stage).wait_send()
-
 
 def main_kernel(x_hbm, w1_hbm, w2_hbm, heads_hbm, lab_hbm,
-                a_hbm, sh1_hbm, sh2_hbm, aw_ref,
+                a_hbm, sh1_hbm, sh2_hbm, rows_ref,
                 dz, wown, acc1, acc2, r1a, r1b, r2a, r2b, r3a, r3b, eall, ast, xbuf, hbd, hcat, heads, lab_v,
                 gm, mbuf,
-                zss, zfs, zrs, zgs, zqs, xss, xrs, yss, yrs, dss, drs, css, crs,
+                zss, zrs, zqs, xss, xrs, yss, yrs, dss, drs, css, crs,
                 ld_sem, w2_sem, xs_sem, as_sem, ess, efs, ers,
                 rss, rsr, mss, mrs, sh_sem):
     pos = Place()
@@ -158,13 +154,14 @@
 
     barrier = pltpu.get_barrier_semaphore()
     me = z * 8 + j
-
-    def greet(i, carry):
-        to = (me + i) % NDEV
-        pl.semaphore_signal(barrier, device_id=(to // 8, to % 8), device_id_type=MESH)
-        return carry
-
-    lax.fori_loop(1, NDEV, greet, 0)
+    pl.semaphore_signal(barrier, device_id=(pos.pair, j), device_id_type=MESH)
+
+    @pl.when(inner)
+    def _():
+        pl.semaphore_signal(barrier, device_id=(pos.mirror, j), device_id_type=MESH)
+
+    for jj in (pos.jx, pos.jy, pos.jc):
+        pl.semaphore_signal(barrier, device_id=(z, jj), device_id_type=MESH)
 
     own_x, act, room = dz.at[0], dz.at[2], dz.at[3]
     w1_raw = room.at[LO, LO]
@@ -216,64 +213,68 @@
             wown[c, g, :, LO] = w1t[row:row + GR, :]
     for cp in ld_w2:
         cp.wait()
-    pl.semaphore_wait(barrier, NDEV - 1)
+    pl.semaphore_wait(barrier, 4 + z * pos.mirror // 2)
 
     def piece(i, jj):
         row = pl.multiple_of((i % NCH) * CH + jj * GR, GR)
         return dz.at[5 + i // NCH, pl.ds(row, GR), :]
 
+    def rows_of(n, ssem, rsem):
+        part = dz.at[5, pl.ds(0, n * GR), :]
+        return remote(part, part, ssem, rsem, z, pos.jc)
+
     def z_pair(c):
-        return remote(wown.at[c, j], piece(c, j), zss.at[c], zrs.at[c], pos.pair, j)
+        return remote(wown.at[c, j], piece(c, j), zss.at[0], zrs.at[c], pos.pair, j)
 
     def z_mirror(c):
-        return remote(wown.at[c, j], piece(NCH + c, j), zss.at[NCH + c], zrs.at[NCH + c], pos.mirror, j)
+        return remote(wown.at[c, j], piece(NCH + c, j), zss.at[1], zrs.at[NCH + c], pos.mirror, j)
 
     def z_forward(i):
         first = i < NCH
         to = jnp.where(first, i + 2 * NCH, i)
-        return remote(piece(i, j), piece(to, j), zfs.at[i], zrs.at[to], jnp.where(first, pos.mirror, pos.pair), j)
+        return remote(piece(i, j), piece(to, j), zss.at[2], zrs.at[to], jnp.where(first, pos.mirror, pos.pair), j)
 
     def more_forward(i):
         first = i < NCH
         to = jnp.where(first, i + 2 * NCH, i)
-        return remote(piece(i, pos.j2), piece(to, pos.j2), zgs.at[i], zqs.at[to], jnp.where(first, pos.mirror, pos.pair), j)
+        return remote(piece(i, pos.j2), piece(to, pos.j2), zss.at[3], zqs.at[to - FAR], jnp.where(first, pos.mirror, pos.pair), j)
 
     def side_copy(i):
-        return remote(piece(i, j), piece(i, j), xss.at[i], xrs.at[i], z, pos.js)
+        return remote(piece(i, j), piece(i, j), xss, xrs.at[i], z, pos.js)
 
     def more_copy(i):
-        return remote(piece(i, pos.j2), piece(i, pos.j2), dss.at[i], drs.at[i], z, pos.js)
+        return remote(piece(i, pos.j2), piece(i, pos.j2), dss, drs.at[i], z, pos.js)
 
     def x_copy(i):
-        return remote(piece(i, j), piece(i, j), xss.at[i], xrs.at[i], z, pos.jx)
+        return remote(piece(i, j), piece(i, j), xss, xrs.at[i], z, pos.jx)
 
     def y_copy(i):
-        return remote(piece(i, j), piece(i, j), yss.at[i], yrs.at[i], z, pos.jy)
+        return remote(piece(i, j), piece(i, j), yss, yrs.at[i], z, pos.jy)
 
     def diag_copy_y(i):
-        return remote(piece(i, pos.jx), piece(i, pos.jx), dss.at[i], drs.at[i], z, pos.jy)
+        return remote(piece(i, pos.jx), piece(i, pos.jx), dss, drs.at[i], z, pos.jy)
 
     def diag_copy_x(i):
-        return remote(piece(i, pos.jy), piece(i, pos.jy), dss.at[i], drs.at[i], z, pos.jx)
+        return remote(piece(i, pos.jy), piece(i, pos.jy), dss, drs.at[i], z, pos.jx)
 
     def core_copy(i, q):
         jj = (j, pos.jx, pos.jy, pos.jd)[q]
-        return remote(piece(i, jj), piece(i, jj), css.at[i, q], crs.at[i, q], z, pos.jc)
+        return remote(piece(i, jj), piece(i, jj), css.at[i], crs.at[i], z, pos.jc)
 
     def core_side(i, q):
         jj = (j, pos.js, pos.j2, pos.jd)[q]
-        return remote(piece(i, jj), piece(i, jj), css.at[i, q], crs.at[i, q], z, pos.jc)
+        return remote(piece(i, jj), piece(i, jj), css.at[i], crs.at[i], z, pos.jc)
 
     def take(i):
-        remote(piece(i, j), piece(i, j), zfs.at[i], zrs.at[i], pos.pair, j).wait_recv()
+        remote(piece(i, j), piece(i, j), zss.at[2], zrs.at[i], pos.pair, j).wait_recv()
 
         @pl.when(inner)
         def _():
             z_forward(i).start()
 
     def take_both(i):
-        remote(piece(i, j), piece(i, j), zfs.at[i], zrs.at[i], pos.pair, j).wait_recv()
-        remote(piece(i, j), piece(i, j), zgs.at[i], zqs.at[i], pos.pair, j).wait_recv()
+        remote(piece(i, j), piece(i, j), zss.at[2], zrs.at[i], pos.pair, j).wait_recv()
+        remote(piece(i, j), piece(i, j), zss.at[3], zqs.at[i - FAR], pos.pair, j).wait_recv()
 
         @pl.when(inner)
         def _():
@@ -383,10 +384,10 @@
 
             @pl.when(i == 5)
             def _():
+                send_side(0)
+                more_on(0)
                 take(2)
                 send_own(2)
-                send_side(0)
-                more_on(0)
 
             return carry
 
@@ -418,14 +419,16 @@
             else:
                 send_side(2)
                 more_on(2)
+                send_diag(1)
+                take_if(outer, 4)
+                send_own(4)
 
                 @pl.when(inner)
                 def _():
                     take_both(FAR)
 
         def granule(n, carry):
-            for q in range(4):
-                core_copy(n, q).wait_recv()
+            rows_of(4, css.at[n], crs.at[n]).wait_recv()
             gran = dz.at[5 + n // NCH, pl.ds(pl.multiple_of((n % NCH) * CH, CH), CH), :]
             w1_nat[...] = gran[:, LO].T
             for m in range(8):
@@ -433,22 +436,26 @@
             for m in range(8):
                 facc[m * SUB:(m + 1) * SUB, :] += dot_nn(us_at(m)[...], gran[:, HI])
 
-            @pl.when(jnp.logical_and(n > 0, n + 2 < FAR))
-            def _():
-                send_side(n + 2)
-
-            @pl.when(n + 1 < FAR)
-            def _():
-                send_diag(n + 1)
-
-            @pl.when(jnp.logical_and(n + 1 >= FAR, n + 1 < NG))
-            def _():
-                pass_both(n + 1)
-
-            @pl.when(n + 4 < FAR)
-            def _():
-                take_if(outer, n + 4)
-                send_own(n + 4)
+            @pl.when(n + 3 < FAR)
+            def _():
+                send_side(n + 3)
+
+            @pl.when(n + 2 < FAR)
+            def _():
+                send_diag(n + 2)
+
+            @pl.when(jnp.logical_and(n + 2 >= FAR, n + 2 < NG))
+            def _():
+                pass_both(n + 2)
+
+            @pl.when(n == 0)
+            def _():
+                take_if(outer, 5)
+                send_own(5)
+
+            @pl.when(jnp.logical_and(inner, n < LAST))
+            def _():
+                take_both(FAR + 1 + n)
 
             @pl.when(jnp.logical_and(n + 4 >= FAR, n + 4 < NG))
             def _():
@@ -457,10 +464,6 @@
                     take_both(n + 4)
 
                 send_both(n + 4)
-
-            @pl.when(jnp.logical_and(inner, n < LAST))
-            def _():
-                take_both(n + FAR + 1)
 
             @pl.when(n < NCH)
             def _():
@@ -539,40 +542,23 @@
         def _():
             e_mirror(b).start()
 
-    def drain(i, carry):
-        x_copy(i).wait_send()
-        diag_copy_y(i).wait_send()
-        for q in range(4):
-            core_copy(i, q).wait_send()
-
-        @pl.when(i < FAR)
-        def _():
-            y_copy(i).wait_send()
-
-        @pl.when(inner)
-        def _():
-            z_forward(i).wait_send()
-
-            @pl.when(jnp.logical_or(i < NCH, i >= FAR))
-            def _():
-                more_forward(i).wait_send()
-
-        return carry
-
-    lax.fori_loop(0, NG, drain, 0)
-    for c in range(NCH):
-        z_pair(c).wait_send()
+    rows_of(NG, xss, xrs.at[0]).wait_send()
+    rows_of(FAR, yss, yrs.at[0]).wait_send()
+    rows_of(NG, dss, drs.at[0]).wait_send()
+    for i in range(NG):
+        rows_of(4, css.at[i], crs.at[i]).wait_send()
+    rows_of(NCH, zss.at[0], zrs.at[0]).wait_send()
 
     @pl.when(inner)
     def _():
-        for c in range(NCH):
-            z_mirror(c).wait_send()
+        for n, i in ((NCH, 1), (NG, 2), (FAR, 3)):
+            rows_of(n, zss.at[i], zrs.at[0]).wait_send()
 
     everything = slice(None)
-    sems = (rss, rsr)
+    up_sems, down_sems = (rss.at[0], rsr), (rss.at[1], rsr)
 
     def up(c, t):
-        return Scatter(pos, acc1.at[c, t], r1a.at[c, t], r2a.at[c, t], r3a.at[c, t], everything, sems,
+        return Scatter(pos, acc1.at[c, t], r1a.at[c, t], r2a.at[c, t], r3a.at[c, t], everything, up_sems,
                        c * 6 + t, t == 0)
 
     def down(c, t, part=None):
@@ -580,7 +566,7 @@
             lanes, idx, x_first = everything, c * 6 + 2 + t, t == 0
         else:
             lanes, idx, x_first = slice(part * (D // 2), (part + 1) * (D // 2)), c * 6 + 2 + t * 2 + part, part == 0
-        return Scatter(pos, acc2.at[c, t], r1b.at[c, t], r2b.at[c, t], r3b.at[c, t], lanes, sems, idx, x_first)
+        return Scatter(pos, acc2.at[c, t], r1b.at[c, t], r2b.at[c, t], r3b.at[c, t], lanes, down_sems, idx, x_first)
 
     ups = [[up(c, t) for t in TWO] for c in range(NCH)]
     downs = [[down(c, t) for t in TWO] for c in range(LAST)]
@@ -601,7 +587,7 @@
         return acc.at[c, t, pos.y, pos.x, pos.core]
 
     def out_copy(acc, out, c, sem, t):
-        return pltpu.make_async_copy(shard(acc, c, t), out.at[c, t], sh_sem.at[c, sem, t])
+        return pltpu.make_async_copy(shard(acc, c, t), out.at[c, t], sh_sem.at[sem])
 
     def finish(acc, out, c, sem):
         v0, v1 = shard(acc, c, 0)[...], shard(acc, c, 1)[...]
@@ -642,40 +628,47 @@
             for task in TWO:
                 acc1[c, task] += g[:, task * CH:(task + 1) * CH].reshape(acc1.shape[2:])
 
-        def step(s, carry):
+        def fill_dz(s):
+            _, k, b = step_of(s)
+            e = e_half(k, b)[...]
+            e1 = e.astype(BF).astype(F32)
+            rest = e - e1
+            e2 = rest.astype(BF).astype(F32)
+            e3 = rest - e2
+            es = jnp.concatenate([e1, e2, e3], axis=0).astype(BF)
+            for m in BLOCKS:
+                dz[k * 2 + b, sub(m), :] = dot_tn(es[:, sub(m)], hbd[...]).astype(BF)
+
+        def both(s):
             c, k, b = step_of(s)
-            t = k * 2 + b
-            prepare(s)
-
-            @pl.when(c == 0)
-            def _():
-                @pl.when(jnp.logical_and(outer, k > 0))
-                def _():
-                    e_wait(k, b)
-
-                e = e_half(k, b)[...]
-                e1 = e.astype(BF).astype(F32)
-                rest = e - e1
-                e2 = rest.astype(BF).astype(F32)
-                e3 = rest - e2
-                es = jnp.concatenate([e1, e2, e3], axis=0).astype(BF)
-                dz[t] = dot_tn(es, hbd[...]).astype(BF)
-
             us = us_all.at[0]
             d_act(s, us)
             add_up(s)
-            g = dot_tn(us[...], dz[t])
+            g = dot_tn(us[...], dz[k * 2 + b])
             for task in TWO:
                 acc2[c, task] += g[:, SIDES[task]].reshape(acc2.shape[2:])
+
+        def first_step(s, carry):
+            _, k, b = step_of(s)
+            prepare(s)
+
+            @pl.when(jnp.logical_and(outer, k > 0))
+            def _():
+                e_wait(k, b)
+
+            fill_dz(s)
+            both(s)
 
             for when, k_f, b_f in ((1, 1, 0), (1, 2, 0), (2, 1, 1), (2, 2, 1), (3, 3, 0), (4, 3, 1)):
                 @pl.when(jnp.logical_and(s == when, inner))
                 def _():
                     e_forward_after_wait(k_f, b_f)
 
-            @pl.when(s == 7)
-            def _():
-                each(ups[0] + downs[0], 'start')
+            return carry
+
+        def step(s, carry):
+            prepare(s)
+            both(s)
 
             @pl.when(s == 9)
             def _():
@@ -688,10 +681,6 @@
             @pl.when(s == 13)
             def _():
                 each(downs[0], 'last')
-
-            @pl.when(s == 15)
-            def _():
-                each(ups[1] + downs[1], 'start')
 
             return carry
 
@@ -699,7 +688,10 @@
             e_wait(k, b)
             e_forward(k, b).start()
 
-        lax.fori_loop(0, 16, step, 0)
+        lax.fori_loop(0, 8, first_step, 0)
+        each(ups[0] + downs[0], 'start')
+        lax.fori_loop(8, 16, step, 0)
+        each(ups[1] + downs[1], 'start')
 
         def last_step(s, carry):
             c, k, b = step_of(s)
@@ -713,20 +705,21 @@
 
             @pl.when(s == 17)
             def _():
-                each(ups[1] + downs[1], 'side')
+                each(ups[1], 'side')
+
+            @pl.when(s == 19)
+            def _():
+                each(downs[1], 'side')
 
             @pl.when(s == 20)
             def _():
                 each(ups[1], 'last')
-
-            @pl.when(s == 22)
-            def _():
-                each(downs[1], 'last')
 
             return carry
 
         lax.fori_loop(16, 24, last_step, 0)
         each(ups[LAST], 'start')
+        each(downs[1], 'last')
 
         def down_pass(task):
             def two_blocks(i, carry):
@@ -769,7 +762,7 @@
     def m_copy(i):
         to = (me + i) % NDEV
         line = mbuf.at[pl.ds(me, 1), :]
-        return remote(line, line, mss.at[i], mrs.at[i], to // 8, to % 8)
+        return remote(line, line, mss, mrs, to // 8, to % 8)
 
     def m_start(i, carry):
         m_copy(i).start()
@@ -786,37 +779,15 @@
             for k in LINE:
                 e_forward(k, b).wait_send()
 
-    for group in ups + downs + tails:
-        each(group, 'drain')
-    for c in range(NCH):
-        for t in TWO:
-            out_copy(acc1, sh1_hbm, c, 0, t).wait()
-            out_copy(acc2, sh2_hbm, c, 1, t).wait()
-
-    def m_wait(i, carry):
-        m_copy(i).wait()
-        return carry
-
-    lax.fori_loop(1, NDEV, m_wait, 0)
-    gram = jnp.sum(mbuf[...], axis=0, keepdims=True)
-
-    def entry(i):
-        return jnp.sum(jnp.where(lane == i, gram, 0.0), axis=1, keepdims=True)
-
-    g00, g01, g11 = entry(0), entry(1), entry(2)
-    scale = (g00 + g11) / 2.0
-
-    def eg_step(i, weights):
-        a0, a1 = weights
-        v0 = a0 * jnp.exp(-(g00 * a0 + g01 * a1) / scale)
-        v1 = a1 * jnp.exp(-(g01 * a0 + g11 * a1) / scale)
-        tot = v0 + v1
-        return v0 / tot, v1 / tot
-
-    half = jnp.full((1, 1), 0.5, F32)
-    a0, a1 = lax.fori_loop(0, STEPS, eg_step, (half, half))
-    row = lax.broadcasted_iota(jnp.int32, aw_ref.shape, 0)
-    aw_ref[...] = jnp.where(row == 0, a0, a1)
+    for kind, all_stages in enumerate(((r1a, r2a, r3a), (r1b, r2b, r3b))):
+        for stage, buf in enumerate(all_stages):
+            remote(buf, buf, rss.at[kind, stage], rsr.at[0, stage], z, pos.jc).wait_send()
+    pltpu.make_async_copy(r3a, sh1_hbm, sh_sem.at[0]).wait()
+    pltpu.make_async_copy(r3b, sh2_hbm, sh_sem.at[1]).wait()
+
+    lines = mbuf.at[pl.ds(0, NDEV - 1), :]
+    remote(lines, lines, mss, mrs, z, pos.jc).wait()
+    rows_ref[...] = mbuf[...]
 
 
 def main_call(x, w1, w2r, heads, labels):
@@ -832,7 +803,7 @@
         out_shape=(jax.ShapeDtypeStruct((NCH, NTOK, CH), F32),
                    jax.ShapeDtypeStruct(per_chunk + up, F32),
                    jax.ShapeDtypeStruct(per_chunk + down, F32),
-                   jax.ShapeDtypeStruct((8, 128), F32)),
+                   jax.ShapeDtypeStruct((NDEV, 128), F32)),
         in_specs=[anyspec] * 5,
         out_specs=(anyspec, anyspec, anyspec, vspec),
         scratch_shapes=[
@@ -850,9 +821,9 @@
             vmem((NC, 2, D), BF),
             vmem((2, NOWN), jnp.int32),
             vmem((3, 8, 128), F32), vmem((NDEV, 128), F32),
-            dma((6,)), *[dma((NG,)) for _ in range(10)], dma((NG, 4)), dma((NG, 4)),
+            dma((4,)), dma((NG,)), dma((NCH,)), dma(()), dma((NG,)), dma(()), dma((FAR,)), dma(()), dma((NG,)), dma((NG,)), dma((NG,)),
             dma((5,)), dma((NCH,)), dma(pair), dma((6,)), dma(quad), dma((4, 2)), dma((4, 2)),
-            dma((6 * NCH, 3)), dma((6 * NCH, 3)), dma((NDEV,)), dma((NDEV,)), dma((NCH, 2, 2)),
+            dma((2, NCH)), dma((6 * NCH, NCH)), dma(()), dma(()), dma(pair),
         ],
         compiler_params=pltpu.CompilerParams(
             collective_id=0, has_side_effects=True, vmem_limit_bytes=VMEM_BYTES),
@@ -860,38 +831,64 @@
     )(x, w1, w2r, heads, labels)
 
 
-def result_kernel(aw_ref, sh1, sh2, a_ref, g1_ref, g2_ref):
-    a0, a1 = aw_ref[0:1, :], aw_ref[1:2, :]
-    a_ref[0] = aw_ref[0, 0]
-    a_ref[1] = aw_ref[1, 0]
-    b0 = jnp.concatenate([a0] * 6, axis=1)
-    b1 = jnp.concatenate([a1] * 6, axis=1)
+def result_kernel(rows_hbm, sh1_hbm, sh2_hbm, a_ref, g1_ref, g2_ref, rows, sh1, sh2, sem):
+    ld_rows = pltpu.make_async_copy(rows_hbm, rows, sem.at[0])
+    loads = [pltpu.make_async_copy(sh1_hbm, sh1, sem.at[1]), pltpu.make_async_copy(sh2_hbm, sh2, sem.at[2])]
+    ld_rows.start()
+    for cp in loads:
+        cp.start()
+    ld_rows.wait()
+
+    gram = jnp.sum(rows[...], axis=0, keepdims=True)
+    lane = lax.broadcasted_iota(jnp.int32, gram.shape, 1)
+
+    def entry(i):
+        return jnp.sum(jnp.where(lane == i, gram, 0.0), axis=1, keepdims=True)
+
+    g00, g01, g11 = entry(0), entry(1), entry(2)
+    scale = (g00 + g11) / 2.0
+
+    def eg_step(i, weights):
+        a0, a1 = weights
+        v0 = a0 * jnp.exp(-(g00 * a0 + g01 * a1) / scale)
+        v1 = a1 * jnp.exp(-(g01 * a0 + g11 * a1) / scale)
+        tot = v0 + v1
+        return v0 / tot, v1 / tot
+
+    half = jnp.full((1, 1), 0.5, F32)
+    a0, a1 = lax.fori_loop(0, STEPS, eg_step, (half, half))
+    a_ref[0] = a0[0, 0]
+    a_ref[1] = a1[0, 0]
+    for cp in loads:
+        cp.wait()
     for c in range(NCH):
-        comb = b0[:, 0:CH] * sh1[c, 0] + b1[:, 0:CH] * sh1[c, 1]
+        comb = a0 * sh1[c, 0] + a1 * sh1[c, 1]
         for g in range(8):
             col = g * NCH * GR + c * GR
             g1_ref[:, col:col + GR] = comb[:, g * GR:(g + 1) * GR]
-        g2_ref[c * GR:(c + 1) * GR, :] = b0 * sh2[c, 0] + b1 * sh2[c, 1]
-
-
-def result_call(aw, sh1, sh2):
+        g2_ref[c * GR:(c + 1) * GR, :] = a0 * sh2[c, 0] + a1 * sh2[c, 1]
+
+
+def result_call(rows, sh1, sh2):
     vspec = pl.BlockSpec(memory_space=pltpu.VMEM)
+    anyspec = pl.BlockSpec(memory_space=pl.ANY)
     return pl.pallas_call(
         result_kernel,
         out_shape=(jax.ShapeDtypeStruct((2,), F32), jax.ShapeDtypeStruct((OWN, D), F32),
                    jax.ShapeDtypeStruct((OWN, D), F32)),
-        in_specs=[vspec] * 3,
+        in_specs=[anyspec] * NCH,
         out_specs=(pl.BlockSpec(memory_space=pltpu.SMEM), vspec, vspec),
+        scratch_shapes=[pltpu.VMEM(v.shape, F32) for v in (rows, sh1, sh2)] + [pltpu.SemaphoreType.DMA((NCH,))],
         name='result',
-    )(aw, sh1, sh2)
+    )(rows, sh1, sh2)
 
 
 def solution(mesh):
     def local_step(tokens, w_up, w_down, task_heads, labels):
         w2r = w_down.reshape(8, NCH, GR, D)
         heads = jnp.transpose(task_heads, (2, 0, 1))
-        _, sh1, sh2, aw = main_call(tokens, w_up, w2r, heads, labels)
-        return result_call(aw, sh1, sh2)
+        _, sh1, sh2, rows = main_call(tokens, w_up, w2r, heads, labels)
+        return result_call(rows, sh1, sh2)
 
     return jax.shard_map(
         local_step, mesh=mesh,

time: 160 us -> 146 us (0.912)
  Pallas kernels: 159 us -> 145 us
    pallas_call x1, Pallas kernels: 157 us -> 143 us  [main_call(): pl.pallas_call(main_kernel, out_shape=(jax.ShapeDtypeStruct((NCH, NTOK, C...]
where the time goes in v4:
time: 146 us
  Pallas kernels  145 us (99%)
    pallas_call x1, Pallas kernels, main_call(): pl.pallas_call(main_kernel, out_shape=(jax.ShapeDtypeStruct((NCH, NTOK, C...  143 us

profile of v4, /device:TPU:0, one launch (start us, length us, event | category | flops | bytes accessed | tf_op | source)
XLA Modules:
  0.0 146.1 jit_solution(8022792644621781573)
XLA Ops:
  0.6 143.0 %main.1 = (f32[3,8192,256]{2,1,0:T(8,128)}, f32[3,2,96,256]{3,2,1,0:T(8,128)}, f32[3,2,32,768]{3,2,1,0:T(8,128)}, f32[32,128]{1,0:T(8,128)}) custom-call(bf16[8192,768]{1,0:T(8,128)(2,1)} %x_hbm.1, bf16[768,768]{1,0:T(8,128)(2,1)} %w1_hbm.1, bf16[8,3,32,768]{3,2,1,0:T(8,128)(2,1)} %bitcast.2, bf16[19,2,768]{2,1,0:T(2,128)(2,1)} %bitcast.3, s32[2,8192]{1,0:T(2,128)} %lab_hbm.1), custom_call_target="tpu_custom_call" | custom-call | tf_op jit(solution)/shard_map/main/pallas_call | solution.py:801
  143.6 2.3 %result.1 = (f32[2]{0:T(128)}, f32[96,768]{1,0:T(8,128)}, f32[96,768]{1,0:T(8,128)}) custom-call(f32[32,128]{1,0:T(8,128)} %get-tuple-element.6.rows_hbm, f32[3,2,96,256]{3,2,1,0:T(8,128)} %get-tuple-element.7.sh1_hbm, f32[3,2,32,768]{3,2,1,0:T(8,128)} %get-tuple-element.8.sh2_hbm), custom_call_target="tpu_custom_call" | custom-call | tf_op jit(solution)/shard_map/result/pallas_call | solution.py:875

commit v5 on v4

--- a/solution.py
+++ b/solution.py
@@ -35,6 +35,10 @@
 BLOCKS = range(TB // SUB)
 NDEV = 32
 
+IN_OTHER = ('', 't0o0', 't1o1i3', 't2o2i4', 's0i5', 's1T3o3')
+IN_OWN = ('i6', 's2d0T4o4i7', 'd1i8', 's3T5o5g6')
+IN_LOOP = ('s4d2g7', 's5d3g8', 'B6x6d4', 'B7x7d5', 'p6B8x8', 'p7', 'p8', '', '')
+
 G0 = 0.7978845608028654
 G1C = 0.044715 * G0
 
@@ -165,7 +169,6 @@
 
     own_x, act, room = dz.at[0], dz.at[2], dz.at[3]
     w1_raw = room.at[LO, LO]
-    w1_nat = room.at[LO, D:D + CH]
     w1_own = dz.at[4, LO, HI]
 
     def sub(m):
@@ -173,10 +176,6 @@
 
     def xo_at(m):
         return own_x.at[sub(m), HI if m >= 4 else LO]
-
-    def us_at(m):
-        lane = D + (m // 4) * CH
-        return act.at[sub(m), lane:lane + CH]
 
     def share_row(k, b):
         return pl.multiple_of((pos.share(k) * 2 + b) * TB, TB)
@@ -196,14 +195,23 @@
         return pltpu.make_async_copy(
             x_hbm.at[pl.ds(share_row(1 + i // 2, i % 2), TB)], stream_half(i), xs_sem.at[i % 2])
 
+    ld_h.start()
     ld_w1.start()
     for cp in ld_w2:
         cp.start()
     xs_load(0).start()
     for cp in ld_x:
         cp.start()
-    ld_h.start()
     ld_l.start()
+
+    ld_h.wait()
+    hf = jnp.concatenate([heads[i].astype(F32) for i in range(NC)] + [jnp.zeros((2, D), F32)], axis=0)
+    hcat[...] = hf.astype(BF)
+    r = lax.broadcasted_iota(jnp.int32, (ER, D), 0)
+    hb = jnp.concatenate([jnp.where(r % 2 == 0, hf, 0.0), jnp.where(r % 2 == 1, hf, 0.0)], axis=1)
+    hbd[...] = jnp.concatenate([hb, hb, hb], axis=0).astype(BF)
+    gm[...] = jnp.zeros_like(gm)
+    acc1[...] = jnp.zeros_like(acc1)
 
     ld_w1.wait()
     w1t = w1_raw[...].T
@@ -272,14 +280,16 @@
         def _():
             z_forward(i).start()
 
-    def take_both(i):
-        remote(piece(i, j), piece(i, j), zss.at[2], zrs.at[i], pos.pair, j).wait_recv()
+    def take_more(i):
         remote(piece(i, j), piece(i, j), zss.at[3], zqs.at[i - FAR], pos.pair, j).wait_recv()
 
         @pl.when(inner)
         def _():
-            z_forward(i).start()
             more_forward(i).start()
+
+    def take_both(i):
+        take(i)
+        take_more(i)
 
     def send_both(i):
         side_copy(i).start()
@@ -293,11 +303,6 @@
         more_copy(i).wait_recv()
         core_side(i, 3).start()
 
-    def take_if(cond, i):
-        @pl.when(cond)
-        def _():
-            take(i)
-
     def send_own(i):
         x_copy(i).start()
         y_copy(i).start()
@@ -319,14 +324,34 @@
 
         core_copy(i, 2).start()
 
-    def more_on(i):
-        @pl.when(inner)
-        def _():
-            more_forward(i).start()
-
     def send_diag(i):
         diag_copy_y(i).wait_recv()
         core_copy(i, 3).start()
+
+    def side_and_on(i):
+        send_side(i)
+        if i < NCH:
+            @pl.when(inner)
+            def _():
+                more_forward(i).start()
+
+    def when_inner(f):
+        return lambda i: pl.when(inner)(lambda: f(i))
+
+    def when_outer(f):
+        return lambda i: pl.when(outer)(lambda: f(i))
+
+    kinds = {'t': take, 'T': when_outer(take), 'i': when_inner(take), 'o': send_own, 's': side_and_on, 'd': send_diag,
+             'g': when_inner(take_more), 'B': when_outer(take_both), 'x': send_both, 'p': pass_both}
+
+    def events(codes):
+        for kind, i in zip(codes[::2], codes[1::2]):
+            kinds[kind](int(i))
+
+    def events_at(i, table):
+        for n, codes in enumerate(table):
+            if codes:
+                pl.when(i == n)(lambda codes=codes: events(codes))
 
     for c in range(NCH):
         z_pair(c).start()
@@ -336,10 +361,12 @@
         for c in range(NCH):
             z_mirror(c).start()
 
+    acc2[...] = jnp.zeros_like(acc2)
+
     def a_store(src, c, row, sem):
         return pltpu.make_async_copy(src, a_hbm.at[c, pl.ds(pl.multiple_of(row, TB), TB)], as_sem.at[sem])
 
-    def forward(facc):
+    def forward(facc, u_own, w1_nat, w2_nat):
         for c in range(NCH):
             w1_own[:, c * CH:(c + 1) * CH] = wown[c, :, :, LO].reshape(CH, D).T
 
@@ -366,29 +393,7 @@
             for c in range(NCH):
                 staged(i, c).start()
 
-            @pl.when(i == 2)
-            def _():
-                take(0)
-                send_own(0)
-                take_if(inner, 3)
-
-            @pl.when(i == 3)
-            def _():
-                take(1)
-                send_own(1)
-                take_if(inner, 4)
-
-            @pl.when(i == 4)
-            def _():
-                take_if(inner, 5)
-
-            @pl.when(i == 5)
-            def _():
-                send_side(0)
-                more_on(0)
-                take(2)
-                send_own(2)
-
+            events_at(i, IN_OTHER)
             return carry
 
         lax.fori_loop(0, 6, other_tokens, 0)
@@ -403,72 +408,29 @@
                 for c in range(NCH):
                     ast[c, sub(m), :] = a[:, c * CH:(c + 1) * CH]
                 act[sub(m), LO] = gelu(a).astype(BF)
+            events(IN_OWN[2 * b])
             for m in BLOCKS:
                 facc[b * TB + m * SUB:b * TB + (m + 1) * SUB, :] = dot_nn(
                     act[sub(m), LO], wown[:, :, :, HI].reshape(D, D))
             for c in range(NCH):
                 a_store(ast.at[c], c, (z * 2 + b) * TB, c).start()
+            events(IN_OWN[2 * b + 1])
             if b == 0:
-                send_side(1)
-                more_on(1)
-                send_diag(0)
-                take_if(outer, 3)
-                send_own(3)
                 for c in range(NCH):
                     a_store(ast.at[c], c, z * NOWN, c).wait()
-            else:
-                send_side(2)
-                more_on(2)
-                send_diag(1)
-                take_if(outer, 4)
-                send_own(4)
-
-                @pl.when(inner)
-                def _():
-                    take_both(FAR)
 
         def granule(n, carry):
             rows_of(4, css.at[n], crs.at[n]).wait_recv()
             gran = dz.at[5 + n // NCH, pl.ds(pl.multiple_of((n % NCH) * CH, CH), CH), :]
             w1_nat[...] = gran[:, LO].T
+            w2_nat[...] = gran[:, HI]
             for m in range(8):
-                us_at(m)[...] = gelu(dot_nn(xo_at(m)[...], w1_nat[...])).astype(BF)
+                u_own[m * SUB:(m + 1) * SUB, :] = gelu(dot_nn(xo_at(m)[...], w1_nat[...])).astype(BF)
             for m in range(8):
-                facc[m * SUB:(m + 1) * SUB, :] += dot_nn(us_at(m)[...], gran[:, HI])
-
-            @pl.when(n + 3 < FAR)
-            def _():
-                send_side(n + 3)
-
-            @pl.when(n + 2 < FAR)
-            def _():
-                send_diag(n + 2)
-
-            @pl.when(jnp.logical_and(n + 2 >= FAR, n + 2 < NG))
-            def _():
-                pass_both(n + 2)
-
-            @pl.when(n == 0)
-            def _():
-                take_if(outer, 5)
-                send_own(5)
-
-            @pl.when(jnp.logical_and(inner, n < LAST))
-            def _():
-                take_both(FAR + 1 + n)
-
-            @pl.when(jnp.logical_and(n + 4 >= FAR, n + 4 < NG))
-            def _():
-                @pl.when(outer)
-                def _():
-                    take_both(n + 4)
-
-                send_both(n + 4)
-
-            @pl.when(n < NCH)
-            def _():
-                acc1[n] = jnp.zeros(acc1.shape[1:], F32)
-                acc2[n] = jnp.zeros(acc2.shape[1:], F32)
+                rows = slice(m * SUB, (m + 1) * SUB)
+                facc[rows, :] += dot_nn(u_own[rows, :], w2_nat[...])
+
+            events_at(n, IN_LOOP)
 
             return carry
 
@@ -476,15 +438,8 @@
         for m in range(8):
             xo_at(m)[...] = (xo_at(m)[...].astype(F32) + facc[m * SUB:(m + 1) * SUB, :]).astype(BF)
 
-    ld_h.wait()
-    hf = jnp.concatenate([heads[i].astype(F32) for i in range(NC)] + [jnp.zeros((2, D), F32)], axis=0)
-    hcat[...] = hf.astype(BF)
-    r = lax.broadcasted_iota(jnp.int32, (ER, D), 0)
-    hb = jnp.concatenate([jnp.where(r % 2 == 0, hf, 0.0), jnp.where(r % 2 == 1, hf, 0.0)], axis=1)
-    hbd[...] = jnp.concatenate([hb, hb, hb], axis=0).astype(BF)
-    gm[...] = jnp.zeros_like(gm)
-
-    pl.run_scoped(forward, pltpu.VMEM((NOWN, D), F32))
+    pl.run_scoped(forward, pltpu.VMEM((NOWN, D), F32), pltpu.VMEM((NOWN, CH), BF), pltpu.VMEM((D, CH), BF),
+                  pltpu.VMEM((CH, D), BF))
 
     for c in range(NCH):
         a_store(ast.at[c], c, z * NOWN, c).wait()
@@ -612,15 +567,14 @@
                 a_load(s + 1).start()
                 x_load(s + 1).start()
 
-        def d_act(s, us):
+        def d_act(s, m, us):
             c, k, b = step_of(s)
             w2c = wown[c, :, :, HI].reshape(CH, D)
-            for m in BLOCKS:
-                u, slope = gelu_and_slope(ast[s % 2, sub(m), :])
-                us[sub(m), :] = u.astype(BF)
-                for task in TWO:
-                    da = dot_nt(dz[k * 2 + b, sub(m), SIDES[task]], w2c)
-                    das[sub(m), task * CH:(task + 1) * CH] = (da * slope).astype(BF)
+            u, slope = gelu_and_slope(ast[s % 2, sub(m), :])
+            us[sub(m), :] = u.astype(BF)
+            for task in TWO:
+                da = dot_nt(dz[k * 2 + b, sub(m), SIDES[task]], w2c)
+                das[sub(m), task * CH:(task + 1) * CH] = (da * slope).astype(BF)
 
         def add_up(s):
             c, _, _ = step_of(s)
@@ -628,21 +582,17 @@
             for task in TWO:
                 acc1[c, task] += g[:, task * CH:(task + 1) * CH].reshape(acc1.shape[2:])
 
-        def fill_dz(s):
+        def e_parts(s):
             _, k, b = step_of(s)
             e = e_half(k, b)[...]
             e1 = e.astype(BF).astype(F32)
             rest = e - e1
             e2 = rest.astype(BF).astype(F32)
             e3 = rest - e2
-            es = jnp.concatenate([e1, e2, e3], axis=0).astype(BF)
-            for m in BLOCKS:
-                dz[k * 2 + b, sub(m), :] = dot_tn(es[:, sub(m)], hbd[...]).astype(BF)
-
-        def both(s):
+            return jnp.concatenate([e1, e2, e3], axis=0).astype(BF)
+
+        def grads(s, us):
             c, k, b = step_of(s)
-            us = us_all.at[0]
-            d_act(s, us)
             add_up(s)
             g = dot_tn(us[...], dz[k * 2 + b])
             for task in TWO:
@@ -656,8 +606,17 @@
             def _():
                 e_wait(k, b)
 
-            fill_dz(s)
-            both(s)
+            us = us_all.at[0]
+            es = e_parts(s)
+
+            def fill(m):
+                dz[k * 2 + b, sub(m), :] = dot_tn(es[:, sub(m)], hbd[...]).astype(BF)
+
+            for m in BLOCKS:
+                fill(m)
+            for m in BLOCKS:
+                d_act(s, m, us)
+            grads(s, us)
 
             for when, k_f, b_f in ((1, 1, 0), (1, 2, 0), (2, 1, 1), (2, 2, 1), (3, 3, 0), (4, 3, 1)):
                 @pl.when(jnp.logical_and(s == when, inner))
@@ -667,8 +626,11 @@
             return carry
 
         def step(s, carry):
+            us = us_all.at[0]
             prepare(s)
-            both(s)
+            for m in BLOCKS:
+                d_act(s, m, us)
+            grads(s, us)
 
             @pl.when(s == 9)
             def _():
@@ -696,7 +658,8 @@
         def last_step(s, carry):
             c, k, b = step_of(s)
             prepare(s)
-            d_act(s, us_all.at[k * 2 + b])
+            for m in BLOCKS:
+                d_act(s, m, us_all.at[k * 2 + b])
             add_up(s)
 
             @pl.when(s == 16)

time: 146 us -> 140 us (0.959)
  Pallas kernels: 145 us -> 139 us
    pallas_call x1, Pallas kernels: 143 us -> 137 us  [main_call(): pl.pallas_call(main_kernel, out_shape=(jax.ShapeDtypeStruct((NCH, NTOK, C...]
where the time goes in v5:
time: 140 us
  Pallas kernels  139 us (99%)
    pallas_call x1, Pallas kernels, main_call(): pl.pallas_call(main_kernel, out_shape=(jax.ShapeDtypeStruct((NCH, NTOK, C...  137 us

profile of v5, /device:TPU:0, one launch (start us, length us, event | category | flops | bytes accessed | tf_op | source)
XLA Modules:
  0.0 140.1 jit_solution(7857485100869450253)
XLA Ops:
  0.6 137.0 %main.1 = (f32[3,8192,256]{2,1,0:T(8,128)}, f32[3,2,96,256]{3,2,1,0:T(8,128)}, f32[3,2,32,768]{3,2,1,0:T(8,128)}, f32[32,128]{1,0:T(8,128)}) custom-call(bf16[8192,768]{1,0:T(8,128)(2,1)} %x_hbm.1, bf16[768,768]{1,0:T(8,128)(2,1)} %w1_hbm.1, bf16[8,3,32,768]{3,2,1,0:T(8,128)(2,1)} %bitcast.2, bf16[19,2,768]{2,1,0:T(2,128)(2,1)} %bitcast.3, s32[2,8192]{1,0:T(2,128)} %lab_hbm.1), custom_call_target="tpu_custom_call" | custom-call | tf_op jit(solution)/shard_map/main/pallas_call | solution.py:764
  137.7 2.3 %result.1 = (f32[2]{0:T(128)}, f32[96,768]{1,0:T(8,128)}, f32[96,768]{1,0:T(8,128)}) custom-call(f32[32,128]{1,0:T(8,128)} %get-tuple-element.6.rows_hbm, f32[3,2,96,256]{3,2,1,0:T(8,128)} %get-tuple-element.7.sh1_hbm, f32[3,2,32,768]{3,2,1,0:T(8,128)} %get-tuple-element.8.sh2_hbm), custom_call_target="tpu_custom_call" | custom-call | tf_op jit(solution)/shard_map/result/pallas_call | solution.py:838

commit v6 on v5

--- a/solution.py
+++ b/solution.py
@@ -37,7 +37,7 @@
 
 IN_OTHER = ('', 't0o0', 't1o1i3', 't2o2i4', 's0i5', 's1T3o3')
 IN_OWN = ('i6', 's2d0T4o4i7', 'd1i8', 's3T5o5g6')
-IN_LOOP = ('s4d2g7', 's5d3g8', 'B6x6d4', 'B7x7d5', 'p6B8x8', 'p7', 'p8', '', '')
+IN_LOOP = ('d2g7s4', 'd3g8', 's5B6x6d4', 'B7x7', 'd5p6B8x8', 'p7', 'p8', '', '')
 
 G0 = 0.7978845608028654
 G1C = 0.044715 * G0
@@ -147,7 +147,7 @@
 
 def main_kernel(x_hbm, w1_hbm, w2_hbm, heads_hbm, lab_hbm,
                 a_hbm, sh1_hbm, sh2_hbm, rows_ref,
-                dz, wown, acc1, acc2, r1a, r1b, r2a, r2b, r3a, r3b, eall, ast, xbuf, hbd, hcat, heads, lab_v,
+                dz, wown, acc1, acc2, r1a, r1b, r2a, r2b, r3a, r3b, eall, ast, hbd, hcat, heads, lab_v,
                 gm, mbuf,
                 zss, zrs, zqs, xss, xrs, yss, yrs, dss, drs, css, crs,
                 ld_sem, w2_sem, xs_sem, as_sem, ess, efs, ers,
@@ -360,8 +360,6 @@
     def _():
         for c in range(NCH):
             z_mirror(c).start()
-
-    acc2[...] = jnp.zeros_like(acc2)
 
     def a_store(src, c, row, sem):
         return pltpu.make_async_copy(src, a_hbm.at[c, pl.ds(pl.multiple_of(row, TB), TB)], as_sem.at[sem])
@@ -420,8 +418,9 @@
                     a_store(ast.at[c], c, z * NOWN, c).wait()
 
         def granule(n, carry):
-            rows_of(4, css.at[n], crs.at[n]).wait_recv()
-            gran = dz.at[5 + n // NCH, pl.ds(pl.multiple_of((n % NCH) * CH, CH), CH), :]
+            g = jnp.where(n == FAR - 1, FAR, jnp.where(n == FAR, FAR - 1, n))
+            rows_of(4, css.at[g], crs.at[g]).wait_recv()
+            gran = dz.at[5 + g // NCH, pl.ds(pl.multiple_of((g % NCH) * CH, CH), CH), :]
             w1_nat[...] = gran[:, LO].T
             w2_nat[...] = gran[:, HI]
             for m in range(8):
@@ -430,6 +429,10 @@
                 rows = slice(m * SUB, (m + 1) * SUB)
                 facc[rows, :] += dot_nn(u_own[rows, :], w2_nat[...])
 
+            @pl.when(n == 0)
+            def _():
+                acc2[...] = jnp.zeros_like(acc2)
+
             events_at(n, IN_LOOP)
 
             return carry
@@ -463,57 +466,15 @@
     def step_of(s):
         return s // 8, (s % 8) // 2, s % 2
 
-    def a_load(s):
+    def a_load(s, slot):
         c, k, b = step_of(s)
-        return pltpu.make_async_copy(a_hbm.at[c, pl.ds(share_row(k, b), TB)], ast.at[s % 2], as_sem.at[s % 2])
-
-    def x_load(s):
-        c, k, b = step_of(s)
-        return pltpu.make_async_copy(x_hbm.at[pl.ds(share_row(k, b), TB)], xbuf.at[s % 2], xs_sem.at[s % 2])
-
-    a_load(0).start()
-    x_load(0).start()
-
-    ld_l.wait()
-    r = lax.broadcasted_iota(jnp.int32, (ER, TB), 0)
-    first = r % 2 == 0
-    real = r < 2 * NC
-    neg = jnp.float32(-jnp.inf)
-    for b in TWO:
-        cols = slice(b * TB, (b + 1) * TB)
-        logit = jnp.where(real, dot_nt(hcat[...], own_x[:, SIDES[b]]), neg)
-        m0 = jnp.max(jnp.where(first, logit, neg), axis=0, keepdims=True)
-        m1 = jnp.max(jnp.where(first, neg, logit), axis=0, keepdims=True)
-        ex = jnp.exp(logit - jnp.where(first, m0, m1))
-        s0 = jnp.sum(jnp.where(first, ex, 0.0), axis=0, keepdims=True)
-        s1 = jnp.sum(jnp.where(first, 0.0, ex), axis=0, keepdims=True)
-        prob = ex / jnp.where(first, s0, s1)
-        lab = jnp.where(first, lab_v[0:1, cols], lab_v[1:2, cols])
-        hot = jnp.where(jnp.logical_and(r // 2 == lab, real), 1.0, 0.0)
-        eall[0, :, cols] = (prob - hot) / (NTOK * 8.0)
-        e_pair(b).start()
-
-        @pl.when(inner)
-        def _():
-            e_mirror(b).start()
-
-    rows_of(NG, xss, xrs.at[0]).wait_send()
-    rows_of(FAR, yss, yrs.at[0]).wait_send()
-    rows_of(NG, dss, drs.at[0]).wait_send()
-    for i in range(NG):
-        rows_of(4, css.at[i], crs.at[i]).wait_send()
-    rows_of(NCH, zss.at[0], zrs.at[0]).wait_send()
-
-    @pl.when(inner)
-    def _():
-        for n, i in ((NCH, 1), (NG, 2), (FAR, 3)):
-            rows_of(n, zss.at[i], zrs.at[0]).wait_send()
+        return pltpu.make_async_copy(a_hbm.at[c, pl.ds(share_row(k, b), TB)], ast.at[slot], as_sem.at[slot])
 
     everything = slice(None)
     up_sems, down_sems = (rss.at[0], rsr), (rss.at[1], rsr)
 
     def up(c, t):
-        return Scatter(pos, acc1.at[c, t], r1a.at[c, t], r2a.at[c, t], r3a.at[c, t], everything, up_sems,
+        return Scatter(pos, acc1.at[c, t], r1a.at[c % 2, t], r2a.at[c % 2, t], r3a.at[c, t], everything, up_sems,
                        c * 6 + t, t == 0)
 
     def down(c, t, part=None):
@@ -521,7 +482,7 @@
             lanes, idx, x_first = everything, c * 6 + 2 + t, t == 0
         else:
             lanes, idx, x_first = slice(part * (D // 2), (part + 1) * (D // 2)), c * 6 + 2 + t * 2 + part, part == 0
-        return Scatter(pos, acc2.at[c, t], r1b.at[c, t], r2b.at[c, t], r3b.at[c, t], lanes, down_sems, idx, x_first)
+        return Scatter(pos, acc2.at[c, t], r1b.at[c % 2, t], r2b.at[c % 2, t], r3b.at[c, t], lanes, down_sems, idx, x_first)
 
     ups = [[up(c, t) for t in TWO] for c in range(NCH)]
     downs = [[down(c, t) for t in TWO] for c in range(LAST)]
@@ -557,30 +518,72 @@
         finish(acc1, sh1_hbm, c, 0)
         finish(acc2, sh2_hbm, c, 1)
 
-    def backward(us_all, das):
-        def prepare(s):
-            a_load(s).wait()
-            x_load(s).wait()
-
-            @pl.when(s < 23)
-            def _():
-                a_load(s + 1).start()
-                x_load(s + 1).start()
-
-        def d_act(s, m, us):
-            c, k, b = step_of(s)
+    def backward(us_all, das, xbuf):
+        def x_load(s, slot):
+            _, k, b = step_of(s)
+            return pltpu.make_async_copy(x_hbm.at[pl.ds(share_row(k, b), TB)], xbuf.at[slot], xs_sem.at[slot])
+
+        def pair_slot(p):
+            return 2 * ((p + 1) % 2)
+
+        def load_pair(p, act):
+            for b in TWO:
+                getattr(a_load(p * 2 + b, pair_slot(p) + b), act)()
+                getattr(x_load(p * 2 + b, pair_slot(p) + b), act)()
+
+        a_load(0, 0).start()
+        x_load(0, 0).start()
+
+        ld_l.wait()
+        r = lax.broadcasted_iota(jnp.int32, (ER, TB), 0)
+        first = r % 2 == 0
+        real = r < 2 * NC
+        neg = jnp.float32(-jnp.inf)
+        for b in TWO:
+            cols = slice(b * TB, (b + 1) * TB)
+            logit = jnp.where(real, dot_nt(hcat[...], own_x[:, SIDES[b]]), neg)
+            m0 = jnp.max(jnp.where(first, logit, neg), axis=0, keepdims=True)
+            m1 = jnp.max(jnp.where(first, neg, logit), axis=0, keepdims=True)
+            ex = jnp.exp(logit - jnp.where(first, m0, m1))
+            s0 = jnp.sum(jnp.where(first, ex, 0.0), axis=0, keepdims=True)
+            s1 = jnp.sum(jnp.where(first, 0.0, ex), axis=0, keepdims=True)
+            prob = ex / jnp.where(first, s0, s1)
+            lab = jnp.where(first, lab_v[0:1, cols], lab_v[1:2, cols])
+            hot = jnp.where(jnp.logical_and(r // 2 == lab, real), 1.0, 0.0)
+            eall[0, :, cols] = (prob - hot) / (NTOK * 8.0)
+            e_pair(b).start()
+
+            @pl.when(inner)
+            def _():
+                e_mirror(b).start()
+
+        rows_of(NG, xss, xrs.at[0]).wait_send()
+        rows_of(FAR, yss, yrs.at[0]).wait_send()
+        rows_of(NG, dss, drs.at[0]).wait_send()
+        for i in range(NG):
+            rows_of(4, css.at[i], crs.at[i]).wait_send()
+        rows_of(NCH, zss.at[0], zrs.at[0]).wait_send()
+
+        @pl.when(inner)
+        def _():
+            for n, i in ((NCH, 1), (NG, 2), (FAR, 3)):
+                rows_of(n, zss.at[i], zrs.at[0]).wait_send()
+
+        def d_act(src, t, sl, c, us, rows):
             w2c = wown[c, :, :, HI].reshape(CH, D)
-            u, slope = gelu_and_slope(ast[s % 2, sub(m), :])
-            us[sub(m), :] = u.astype(BF)
+            u, slope = gelu_and_slope(src[...])
+            us[rows, :] = u.astype(BF)
             for task in TWO:
-                da = dot_nt(dz[k * 2 + b, sub(m), SIDES[task]], w2c)
-                das[sub(m), task * CH:(task + 1) * CH] = (da * slope).astype(BF)
-
-        def add_up(s):
-            c, _, _ = step_of(s)
-            g = dot_tn(xbuf[s % 2], das[...])
+                da = dot_nt(dz[t, sl, SIDES[task]], w2c)
+                das[rows, task * CH:(task + 1) * CH] = (da * slope).astype(BF)
+
+        def add_up(c, g):
             for task in TWO:
                 acc1[c, task] += g[:, task * CH:(task + 1) * CH].reshape(acc1.shape[2:])
+
+        def add_down(c, g):
+            for task in TWO:
+                acc2[c, task] += g[:, SIDES[task]].reshape(acc2.shape[2:])
 
         def e_parts(s):
             _, k, b = step_of(s)
@@ -591,32 +594,33 @@
             e3 = rest - e2
             return jnp.concatenate([e1, e2, e3], axis=0).astype(BF)
 
-        def grads(s, us):
-            c, k, b = step_of(s)
-            add_up(s)
-            g = dot_tn(us[...], dz[k * 2 + b])
-            for task in TWO:
-                acc2[c, task] += g[:, SIDES[task]].reshape(acc2.shape[2:])
-
         def first_step(s, carry):
             _, k, b = step_of(s)
-            prepare(s)
+            t = k * 2 + b
+            a_load(s, s % 2).wait()
+            x_load(s, s % 2).wait()
+
+            @pl.when(s < 7)
+            def _():
+                a_load(s + 1, (s + 1) % 2).start()
+                x_load(s + 1, (s + 1) % 2).start()
+
+            @pl.when(s == 7)
+            def _():
+                load_pair(4, 'start')
 
             @pl.when(jnp.logical_and(outer, k > 0))
             def _():
                 e_wait(k, b)
 
+            es = e_parts(s)
+            for m in BLOCKS:
+                dz[t, sub(m), :] = dot_tn(es[:, sub(m)], hbd[...]).astype(BF)
             us = us_all.at[0]
-            es = e_parts(s)
-
-            def fill(m):
-                dz[k * 2 + b, sub(m), :] = dot_tn(es[:, sub(m)], hbd[...]).astype(BF)
-
             for m in BLOCKS:
-                fill(m)
-            for m in BLOCKS:
-                d_act(s, m, us)
-            grads(s, us)
+                d_act(ast.at[s % 2, sub(m)], t, sub(m), 0, us, sub(m))
+            add_up(0, dot_tn(xbuf[s % 2], das[:TB]))
+            add_down(0, dot_tn(us[:TB], dz[t]))
 
             for when, k_f, b_f in ((1, 1, 0), (1, 2, 0), (2, 1, 1), (2, 2, 1), (3, 3, 0), (4, 3, 1)):
                 @pl.when(jnp.logical_and(s == when, inner))
@@ -625,24 +629,32 @@
 
             return carry
 
-        def step(s, carry):
-            us = us_all.at[0]
-            prepare(s)
-            for m in BLOCKS:
-                d_act(s, m, us)
-            grads(s, us)
-
-            @pl.when(s == 9)
+        def pair_front(p, c):
+            k = p % 4
+            load_pair(p, 'wait')
+
+            @pl.when(p < 11)
+            def _():
+                load_pair(p + 1, 'start')
+
+            for b in TWO:
+                for m in BLOCKS:
+                    rows = slice(b * TB + m * SUB, b * TB + (m + 1) * SUB)
+                    d_act(ast.at[pair_slot(p) + b, sub(m)], k * 2 + b, sub(m), c, us_all.at[k], rows)
+            add_up(c, dot_tn(xbuf[pl.ds(pair_slot(p), 2)].reshape(NOWN, D), das[...]))
+
+        def step(p, carry):
+            k = p % 4
+            pair_front(p, 1)
+            add_down(1, dot_tn(us_all[k], dz[pl.ds(k * 2, 2)].reshape(NOWN, DD)))
+
+            @pl.when(p == 4)
             def _():
                 each(ups[0] + downs[0], 'side')
 
-            @pl.when(s == 12)
-            def _():
-                each(ups[0], 'last')
-
-            @pl.when(s == 13)
-            def _():
-                each(downs[0], 'last')
+            @pl.when(p == 6)
+            def _():
+                each(ups[0] + downs[0], 'last')
 
             return carry
 
@@ -652,59 +664,52 @@
 
         lax.fori_loop(0, 8, first_step, 0)
         each(ups[0] + downs[0], 'start')
-        lax.fori_loop(8, 16, step, 0)
+        lax.fori_loop(4, 8, step, 0)
         each(ups[1] + downs[1], 'start')
 
-        def last_step(s, carry):
-            c, k, b = step_of(s)
-            prepare(s)
-            for m in BLOCKS:
-                d_act(s, m, us_all.at[k * 2 + b])
-            add_up(s)
-
-            @pl.when(s == 16)
+        def last_step(p, carry):
+            pair_front(p, LAST)
+
+            @pl.when(p == 8)
             def _():
                 finish_chunk(0)
-
-            @pl.when(s == 17)
-            def _():
                 each(ups[1], 'side')
 
-            @pl.when(s == 19)
+            @pl.when(p == 9)
             def _():
                 each(downs[1], 'side')
 
-            @pl.when(s == 20)
+            @pl.when(p == 10)
             def _():
                 each(ups[1], 'last')
 
             return carry
 
-        lax.fori_loop(16, 24, last_step, 0)
+        lax.fori_loop(8, 12, last_step, 0)
         each(ups[LAST], 'start')
         each(downs[1], 'last')
 
         def down_pass(task):
-            def two_blocks(i, carry):
-                lanes = SIDES[task]
-                g = dot_tn(us_all[i * 2], dz[i * 2, :, lanes])
-                g = g + dot_tn(us_all[i * 2 + 1], dz[i * 2 + 1, :, lanes])
-                acc2[LAST, task] += g.reshape(acc2.shape[2:])
-
-                @pl.when(i == 1)
+            def half(i, carry):
+                u = us_all[pl.ds(i * 2, 2)].reshape(4 * TB, CH)
+                d = dz[pl.ds(i * 4, 4), :, SIDES[task]].reshape(4 * TB, D)
+                acc2[LAST, task] += dot_tn(u, d).reshape(acc2.shape[2:])
+
+                @pl.when(i == 0)
                 def _():
                     each(ups[LAST] if task == 0 else tails[0], 'side')
 
                 return carry
 
-            lax.fori_loop(0, 4, two_blocks, 0)
+            lax.fori_loop(0, 2, half, 0)
             each(tails[task], 'start')
 
         down_pass(0)
         finish_chunk(1)
         down_pass(1)
 
-    pl.run_scoped(backward, pltpu.VMEM((8, TB, CH), BF), pltpu.VMEM((TB, 2 * CH), BF))
+    pl.run_scoped(backward, pltpu.VMEM((4, NOWN, CH), BF), pltpu.VMEM((NOWN, 2 * CH), BF),
+                  pltpu.VMEM((4, TB, D), BF))
 
     each(ups[LAST], 'last')
     each(tails[1], 'side')
@@ -742,9 +747,9 @@
             for k in LINE:
                 e_forward(k, b).wait_send()
 
-    for kind, all_stages in enumerate(((r1a, r2a, r3a), (r1b, r2b, r3b))):
-        for stage, buf in enumerate(all_stages):
-            remote(buf, buf, rss.at[kind, stage], rsr.at[0, stage], z, pos.jc).wait_send()
+    for kind, acc in enumerate((acc1, acc2)):
+        for stage, part in enumerate((acc.at[:, :, :, :, 0], acc.at[:, :, :, 0, 0], acc.at[:, :, 0, 0, 0])):
+            remote(part, part, rss.at[kind, stage], rsr.at[0, stage], z, pos.jc).wait_send()
     pltpu.make_async_copy(r3a, sh1_hbm, sh_sem.at[0]).wait()
     pltpu.make_async_copy(r3b, sh2_hbm, sh_sem.at[1]).wait()
 
@@ -773,19 +778,18 @@
             vmem((8, TB, DD), BF),
             vmem((NCH, 8, GR, DD), BF),
             vmem(per_chunk + octet + up, F32), vmem(per_chunk + octet + down, F32),
-            vmem(per_chunk + quad + up, F32), vmem(per_chunk + quad + down, F32),
-            vmem(per_chunk + pair + up, F32), vmem(per_chunk + pair + down, F32),
+            vmem((2, 2) + quad + up, F32), vmem((2, 2) + quad + down, F32),
+            vmem((2, 2) + pair + up, F32), vmem((2, 2) + pair + down, F32),
             vmem(per_chunk + up, F32), vmem(per_chunk + down, F32),
             vmem((4, ER, NOWN), F32),
-            vmem((NCH, TB, CH), F32),
-            vmem((2, TB, D), BF),
+            vmem((4, TB, CH), F32),
             vmem((3 * ER, DD), BF),
             vmem((ER, D), BF),
             vmem((NC, 2, D), BF),
             vmem((2, NOWN), jnp.int32),
             vmem((3, 8, 128), F32), vmem((NDEV, 128), F32),
             dma((4,)), dma((NG,)), dma((NCH,)), dma(()), dma((NG,)), dma(()), dma((FAR,)), dma(()), dma((NG,)), dma((NG,)), dma((NG,)),
-            dma((5,)), dma((NCH,)), dma(pair), dma((6,)), dma(quad), dma((4, 2)), dma((4, 2)),
+            dma((5,)), dma((NCH,)), dma((4,)), dma((6,)), dma(quad), dma((4, 2)), dma((4, 2)),
             dma((2, NCH)), dma((6 * NCH, NCH)), dma(()), dma(()), dma(pair),
         ],
         compiler_params=pltpu.CompilerParams(
@@ -809,17 +813,14 @@
         return jnp.sum(jnp.where(lane == i, gram, 0.0), axis=1, keepdims=True)
 
     g00, g01, g11 = entry(0), entry(1), entry(2)
-    scale = (g00 + g11) / 2.0
-
-    def eg_step(i, weights):
-        a0, a1 = weights
-        v0 = a0 * jnp.exp(-(g00 * a0 + g01 * a1) / scale)
-        v1 = a1 * jnp.exp(-(g01 * a0 + g11 * a1) / scale)
+    scale = (g00 + g11) * -0.5
+    g00, g01, g11 = g00 / scale, g01 / scale, g11 / scale
+    a0 = a1 = jnp.full((1, 1), 0.5, F32)
+    for _ in range(STEPS):
+        v0 = a0 * jnp.exp(g00 * a0 + g01 * a1)
+        v1 = a1 * jnp.exp(g01 * a0 + g11 * a1)
         tot = v0 + v1
-        return v0 / tot, v1 / tot
-
-    half = jnp.full((1, 1), 0.5, F32)
-    a0, a1 = lax.fori_loop(0, STEPS, eg_step, (half, half))
+        a0, a1 = v0 / tot, v1 / tot
     a_ref[0] = a0[0, 0]
     a_ref[1] = a1[0, 0]
     for cp in loads:

time: 140 us -> 139 us (level)
  no operation moved by 1% of the time
where the time goes in v6:
time: 139 us
  Pallas kernels  138 us (99%)
    pallas_call x1, Pallas kernels, main_call(): pl.pallas_call(main_kernel, out_shape=(jax.ShapeDtypeStruct((NCH, NTOK, C...  136 us

profile of v6, /device:TPU:0, one launch (start us, length us, event | category | flops | bytes accessed | tf_op | source)
XLA Modules:
  0.0 138.9 jit_solution(17937983815122318184)
XLA Ops:
  0.6 135.8 %main.1 = (f32[3,8192,256]{2,1,0:T(8,128)}, f32[3,2,96,256]{3,2,1,0:T(8,128)}, f32[3,2,32,768]{3,2,1,0:T(8,128)}, f32[32,128]{1,0:T(8,128)}) custom-call(bf16[8192,768]{1,0:T(8,128)(2,1)} %x_hbm.1, bf16[768,768]{1,0:T(8,128)(2,1)} %w1_hbm.1, bf16[8,3,32,768]{3,2,1,0:T(8,128)(2,1)} %bitcast.2, bf16[19,2,768]{2,1,0:T(2,128)(2,1)} %bitcast.3, s32[2,8192]{1,0:T(2,128)} %lab_hbm.1), custom_call_target="tpu_custom_call" | custom-call | tf_op jit(solution)/shard_map/main/pallas_call | solution.py:769
  136.4 2.3 %result.1 = (f32[2]{0:T(128)}, f32[96,768]{1,0:T(8,128)}, f32[96,768]{1,0:T(8,128)}) custom-call(f32[32,128]{1,0:T(8,128)} %get-tuple-element.6.rows_hbm, f32[3,2,96,256]{3,2,1,0:T(8,128)} %get-tuple-element.7.sh1_hbm, f32[3,2,32,768]{3,2,1,0:T(8,128)} %get-tuple-element.8.sh2_hbm), custom_call_target="tpu_custom_call" | custom-call | tf_op jit(solution)/shard_map/result/pallas_call | solution.py:839

commit v7 on v6

--- a/solution.py
+++ b/solution.py
@@ -35,6 +35,7 @@
 BLOCKS = range(TB // SUB)
 NDEV = 32
 
+E_ON = ('', '1020', '1121', '30', '31')
 IN_OTHER = ('', 't0o0', 't1o1i3', 't2o2i4', 's0i5', 's1T3o3')
 IN_OWN = ('i6', 's2d0T4o4i7', 'd1i8', 's3T5o5g6')
 IN_LOOP = ('d2g7s4', 'd3g8', 's5B6x6d4', 'B7x7', 'd5p6B8x8', 'p7', 'p8', '', '')
@@ -146,7 +147,7 @@
 
 
 def main_kernel(x_hbm, w1_hbm, w2_hbm, heads_hbm, lab_hbm,
-                a_hbm, sh1_hbm, sh2_hbm, rows_ref,
+                a_hbm, sh1_hbm, sh2_hbm, rows_hbm,
                 dz, wown, acc1, acc2, r1a, r1b, r2a, r2b, r3a, r3b, eall, ast, hbd, hcat, heads, lab_v,
                 gm, mbuf,
                 zss, zrs, zqs, xss, xrs, yss, yrs, dss, drs, css, crs,
@@ -622,10 +623,12 @@
             add_up(0, dot_tn(xbuf[s % 2], das[:TB]))
             add_down(0, dot_tn(us[:TB], dz[t]))
 
-            for when, k_f, b_f in ((1, 1, 0), (1, 2, 0), (2, 1, 1), (2, 2, 1), (3, 3, 0), (4, 3, 1)):
-                @pl.when(jnp.logical_and(s == when, inner))
-                def _():
-                    e_forward_after_wait(k_f, b_f)
+            for when, codes in enumerate(E_ON):
+                if codes:
+                    @pl.when(jnp.logical_and(s == when, inner))
+                    def _():
+                        for k_f, b_f in zip(codes[::2], codes[1::2]):
+                            e_forward_after_wait(int(k_f), int(b_f))
 
             return carry
 
@@ -727,16 +730,21 @@
     lane = lax.broadcasted_iota(jnp.int32, (1, 128), 1)
     mbuf[pl.ds(me, 1), :] = jnp.where(lane == 0, full(gm[0]), jnp.where(lane == 1, full(gm[1]), full(gm[2])))
 
-    def m_copy(i):
-        to = (me + i) % NDEV
-        line = mbuf.at[pl.ds(me, 1), :]
-        return remote(line, line, mss, mrs, to // 8, to % 8)
-
-    def m_start(i, carry):
-        m_copy(i).start()
-        return carry
-
-    lax.fori_loop(1, NDEV, m_start, 0)
+    def row_of(ref):
+        return ref.at[pl.ds(me, 1), :]
+
+    keep = pltpu.make_async_copy(row_of(mbuf), row_of(rows_hbm), ld_sem.at[0])
+    keep.start()
+
+    def m_send(to_z, to_j):
+        remote(row_of(mbuf), row_of(rows_hbm), mss, mrs, to_z, to_j).start()
+
+    mates = [(j + i) % 8 for i in MATES]
+    for to_z in reversed(pos.shares[1:]):
+        for to_j in [j] + mates:
+            m_send(to_z, to_j)
+    for to_j in mates:
+        m_send(z, to_j)
 
     for b in TWO:
         e_pair(b).wait_send()
@@ -753,15 +761,14 @@
     pltpu.make_async_copy(r3a, sh1_hbm, sh_sem.at[0]).wait()
     pltpu.make_async_copy(r3b, sh2_hbm, sh_sem.at[1]).wait()
 
-    lines = mbuf.at[pl.ds(0, NDEV - 1), :]
-    remote(lines, lines, mss, mrs, z, pos.jc).wait()
-    rows_ref[...] = mbuf[...]
+    keep.wait()
+    lines = pl.ds(0, NDEV - 1)
+    remote(mbuf.at[lines, :], rows_hbm.at[lines, :], mss, mrs, z, pos.jc).wait()
 
 
 def main_call(x, w1, w2r, heads, labels):
     dma = pltpu.SemaphoreType.DMA
     anyspec = pl.BlockSpec(memory_space=pl.ANY)
-    vspec = pl.BlockSpec(memory_space=pltpu.VMEM)
     up, down = (OWN, CH), (GR, D)
     pair, quad, octet = (2,), (2, 2), (2, 2, 2)
     per_chunk = (NCH, 2)
@@ -773,7 +780,7 @@
                    jax.ShapeDtypeStruct(per_chunk + down, F32),
                    jax.ShapeDtypeStruct((NDEV, 128), F32)),
         in_specs=[anyspec] * 5,
-        out_specs=(anyspec, anyspec, anyspec, vspec),
+        out_specs=(anyspec, anyspec, anyspec, anyspec),
         scratch_shapes=[
             vmem((8, TB, DD), BF),
             vmem((NCH, 8, GR, DD), BF),

time: 139 us -> 138 us (level)
  no operation moved by 1% of the time
where the time goes in v7:
time: 138 us
  Pallas kernels  137 us (99%)
    pallas_call x1, Pallas kernels, main_call(): pl.pallas_call(main_kernel, out_shape=(jax.ShapeDtypeStruct((NCH, NTOK, C...  135 us

profile of v7, /device:TPU:0, one launch (start us, length us, event | category | flops | bytes accessed | tf_op | source)
XLA Modules:
  0.0 138.2 jit_solution(10068256409166849678)
XLA Ops:
  0.6 135.1 %main.1 = (f32[3,8192,256]{2,1,0:T(8,128)}, f32[3,2,96,256]{3,2,1,0:T(8,128)}, f32[3,2,32,768]{3,2,1,0:T(8,128)}, f32[32,128]{1,0:T(8,128)}) custom-call(bf16[8192,768]{1,0:T(8,128)(2,1)} %x_hbm.1, bf16[768,768]{1,0:T(8,128)(2,1)} %w1_hbm.1, bf16[8,3,32,768]{3,2,1,0:T(8,128)(2,1)} %bitcast.2, bf16[19,2,768]{2,1,0:T(2,128)(2,1)} %bitcast.3, s32[2,8192]{1,0:T(2,128)} %lab_hbm.1), custom_call_target="tpu_custom_call" | custom-call | tf_op jit(solution)/shard_map/main/pallas_call | solution.py:776
  135.7 2.3 %result.1 = (f32[2]{0:T(128)}, f32[96,768]{1,0:T(8,128)}, f32[96,768]{1,0:T(8,128)}) custom-call(f32[32,128]{1,0:T(8,128)} %get-tuple-element.6.rows_hbm, f32[3,2,96,256]{3,2,1,0:T(8,128)} %get-tuple-element.7.sh1_hbm, f32[3,2,32,768]{3,2,1,0:T(8,128)} %get-tuple-element.8.sh2_hbm), custom_call_target="tpu_custom_call" | custom-call | tf_op jit(solution)/shard_map/result/pallas_call | solution.py:846

commit v8 on v7

--- a/solution.py
+++ b/solution.py
@@ -38,7 +38,7 @@
 E_ON = ('', '1020', '1121', '30', '31')
 IN_OTHER = ('', 't0o0', 't1o1i3', 't2o2i4', 's0i5', 's1T3o3')
 IN_OWN = ('i6', 's2d0T4o4i7', 'd1i8', 's3T5o5g6')
-IN_LOOP = ('d2g7s4', 'd3g8', 's5B6x6d4', 'B7x7', 'd5p6B8x8', 'p7', 'p8', '', '')
+IN_LOOP = ('d2g7s4', 'd3g8', 's5B6x6d4', 'B7x7', 'B8x8p6d5', 'p7', 'p8', '', '')
 
 G0 = 0.7978845608028654
 G1C = 0.044715 * G0
@@ -418,14 +418,16 @@
                 for c in range(NCH):
                     a_store(ast.at[c], c, z * NOWN, c).wait()
 
-        def granule(n, carry):
-            g = jnp.where(n == FAR - 1, FAR, jnp.where(n == FAR, FAR - 1, n))
+        def act_of(g):
             rows_of(4, css.at[g], crs.at[g]).wait_recv()
             gran = dz.at[5 + g // NCH, pl.ds(pl.multiple_of((g % NCH) * CH, CH), CH), :]
             w1_nat[...] = gran[:, LO].T
             w2_nat[...] = gran[:, HI]
             for m in range(8):
                 u_own[m * SUB:(m + 1) * SUB, :] = gelu(dot_nn(xo_at(m)[...], w1_nat[...])).astype(BF)
+
+        def granule(n, carry):
+            act_of(jnp.where(n == FAR - 1, FAR, jnp.where(n == FAR, FAR - 1, n)))
             for m in range(8):
                 rows = slice(m * SUB, (m + 1) * SUB)
                 facc[rows, :] += dot_nn(u_own[rows, :], w2_nat[...])
@@ -438,9 +440,12 @@
 
             return carry
 
-        lax.fori_loop(0, NG, granule, 0)
+        lax.fori_loop(0, NG - 1, granule, 0)
+        act_of(NG - 1)
         for m in range(8):
-            xo_at(m)[...] = (xo_at(m)[...].astype(F32) + facc[m * SUB:(m + 1) * SUB, :]).astype(BF)
+            rows = slice(m * SUB, (m + 1) * SUB)
+            out = facc[rows, :] + dot_nn(u_own[rows, :], w2_nat[...])
+            xo_at(m)[...] = (xo_at(m)[...].astype(F32) + out).astype(BF)
 
     pl.run_scoped(forward, pltpu.VMEM((NOWN, D), F32), pltpu.VMEM((NOWN, CH), BF), pltpu.VMEM((D, CH), BF),
                   pltpu.VMEM((CH, D), BF))

time: 138 us -> 138 us (level)
  no operation moved by 1% of the time
where the time goes in v8:
time: 138 us
  Pallas kernels  137 us (99%)
    pallas_call x1, Pallas kernels, main_call(): pl.pallas_call(main_kernel, out_shape=(jax.ShapeDtypeStruct((NCH, NTOK, C...  135 us

profile of v8, /device:TPU:0, one launch (start us, length us, event | category | flops | bytes accessed | tf_op | source)
XLA Modules:
  0.0 138.1 jit_solution(13631812972667522722)
XLA Ops:
  0.6 135.0 %main.1 = (f32[3,8192,256]{2,1,0:T(8,128)}, f32[3,2,96,256]{3,2,1,0:T(8,128)}, f32[3,2,32,768]{3,2,1,0:T(8,128)}, f32[32,128]{1,0:T(8,128)}) custom-call(bf16[8192,768]{1,0:T(8,128)(2,1)} %x_hbm.1, bf16[768,768]{1,0:T(8,128)(2,1)} %w1_hbm.1, bf16[8,3,32,768]{3,2,1,0:T(8,128)(2,1)} %bitcast.2, bf16[19,2,768]{2,1,0:T(2,128)(2,1)} %bitcast.3, s32[2,8192]{1,0:T(2,128)} %lab_hbm.1), custom_call_target="tpu_custom_call" | custom-call | tf_op jit(solution)/shard_map/main/pallas_call | solution.py:781
  135.7 2.3 %result.1 = (f32[2]{0:T(128)}, f32[96,768]{1,0:T(8,128)}, f32[96,768]{1,0:T(8,128)}) custom-call(f32[32,128]{1,0:T(8,128)} %get-tuple-element.6.rows_hbm, f32[3,2,96,256]{3,2,1,0:T(8,128)} %get-tuple-element.7.sh1_hbm, f32[3,2,32,768]{3,2,1,0:T(8,128)} %get-tuple-element.8.sh2_hbm), custom_call_target="tpu_custom_call" | custom-call | tf_op jit(solution)/shard_map/result/pallas_call | solution.py:851

commit v9 on v8

--- a/solution.py
+++ b/solution.py
@@ -268,11 +268,11 @@
 
     def core_copy(i, q):
         jj = (j, pos.jx, pos.jy, pos.jd)[q]
-        return remote(piece(i, jj), piece(i, jj), css.at[i], crs.at[i], z, pos.jc)
+        return remote(piece(i, jj), piece(i, jj), css, crs.at[i], z, pos.jc)
 
     def core_side(i, q):
         jj = (j, pos.js, pos.j2, pos.jd)[q]
-        return remote(piece(i, jj), piece(i, jj), css.at[i], crs.at[i], z, pos.jc)
+        return remote(piece(i, jj), piece(i, jj), css, crs.at[i], z, pos.jc)
 
     def take(i):
         remote(piece(i, j), piece(i, j), zss.at[2], zrs.at[i], pos.pair, j).wait_recv()
@@ -419,7 +419,7 @@
                     a_store(ast.at[c], c, z * NOWN, c).wait()
 
         def act_of(g):
-            rows_of(4, css.at[g], crs.at[g]).wait_recv()
+            rows_of(4, css, crs.at[g]).wait_recv()
             gran = dz.at[5 + g // NCH, pl.ds(pl.multiple_of((g % NCH) * CH, CH), CH), :]
             w1_nat[...] = gran[:, LO].T
             w2_nat[...] = gran[:, HI]
@@ -481,13 +481,13 @@
 
     def up(c, t):
         return Scatter(pos, acc1.at[c, t], r1a.at[c % 2, t], r2a.at[c % 2, t], r3a.at[c, t], everything, up_sems,
-                       c * 6 + t, t == 0)
+                       c * 4 + t, t == 0)
 
     def down(c, t, part=None):
         if part is None:
-            lanes, idx, x_first = everything, c * 6 + 2 + t, t == 0
+            lanes, idx, x_first = everything, c * 4 + 2 + t, t == 0
         else:
-            lanes, idx, x_first = slice(part * (D // 2), (part + 1) * (D // 2)), c * 6 + 2 + t * 2 + part, part == 0
+            lanes, idx, x_first = slice(part * (D // 2), (part + 1) * (D // 2)), c * 4 + 2 + t * 2 + part, part == 0
         return Scatter(pos, acc2.at[c, t], r1b.at[c % 2, t], r2b.at[c % 2, t], r3b.at[c, t], lanes, down_sems, idx, x_first)
 
     ups = [[up(c, t) for t in TWO] for c in range(NCH)]
@@ -566,8 +566,8 @@
         rows_of(NG, xss, xrs.at[0]).wait_send()
         rows_of(FAR, yss, yrs.at[0]).wait_send()
         rows_of(NG, dss, drs.at[0]).wait_send()
-        for i in range(NG):
-            rows_of(4, css.at[i], crs.at[i]).wait_send()
+        both = dz.at[pl.ds(5, 2), pl.ds(0, 2 * NG * GR), :]
+        remote(both, both, css, crs.at[0], z, pos.jc).wait_send()
         rows_of(NCH, zss.at[0], zrs.at[0]).wait_send()
 
         @pl.when(inner)
@@ -800,9 +800,9 @@
             vmem((NC, 2, D), BF),
             vmem((2, NOWN), jnp.int32),
             vmem((3, 8, 128), F32), vmem((NDEV, 128), F32),
-            dma((4,)), dma((NG,)), dma((NCH,)), dma(()), dma((NG,)), dma(()), dma((FAR,)), dma(()), dma((NG,)), dma((NG,)), dma((NG,)),
+            dma((4,)), dma((NG,)), dma((NCH,)), dma(()), dma((NG,)), dma(()), dma((FAR,)), dma(()), dma((NG,)), dma(()), dma((NG,)),
             dma((5,)), dma((NCH,)), dma((4,)), dma((6,)), dma(quad), dma((4, 2)), dma((4, 2)),
-            dma((2, NCH)), dma((6 * NCH, NCH)), dma(()), dma(()), dma(pair),
+            dma((2, NCH)), dma((14, NCH)), dma(()), dma(()), dma(pair),
         ],
         compiler_params=pltpu.CompilerParams(
             collective_id=0, has_side_effects=True, vmem_limit_bytes=VMEM_BYTES),
@@ -810,7 +810,7 @@
     )(x, w1, w2r, heads, labels)
 
 
-def result_kernel(rows_hbm, sh1_hbm, sh2_hbm, a_ref, g1_ref, g2_ref, rows, sh1, sh2, sem):
+def result_kernel(rows_hbm, sh1_hbm, sh2_hbm, a_ref, g1_hbm, g2_hbm, rows, sh1, sh2, g1_ref, g2_ref, sem):
     ld_rows = pltpu.make_async_copy(rows_hbm, rows, sem.at[0])
     loads = [pltpu.make_async_copy(sh1_hbm, sh1, sem.at[1]), pltpu.make_async_copy(sh2_hbm, sh2, sem.at[2])]
     ld_rows.start()
@@ -837,24 +837,31 @@
     a_ref[1] = a1[0, 0]
     for cp in loads:
         cp.wait()
+    out1 = pltpu.make_async_copy(g1_ref, g1_hbm, sem.at[3])
+    out2 = pltpu.make_async_copy(g2_ref, g2_hbm, sem.at[4])
+    for c in range(NCH):
+        g2_ref[c * GR:(c + 1) * GR, :] = a0 * sh2[c, 0] + a1 * sh2[c, 1]
+    out2.start()
     for c in range(NCH):
         comb = a0 * sh1[c, 0] + a1 * sh1[c, 1]
         for g in range(8):
             col = g * NCH * GR + c * GR
             g1_ref[:, col:col + GR] = comb[:, g * GR:(g + 1) * GR]
-        g2_ref[c * GR:(c + 1) * GR, :] = a0 * sh2[c, 0] + a1 * sh2[c, 1]
+    out1.start()
+    out2.wait()
+    out1.wait()
 
 
 def result_call(rows, sh1, sh2):
-    vspec = pl.BlockSpec(memory_space=pltpu.VMEM)
     anyspec = pl.BlockSpec(memory_space=pl.ANY)
     return pl.pallas_call(
         result_kernel,
         out_shape=(jax.ShapeDtypeStruct((2,), F32), jax.ShapeDtypeStruct((OWN, D), F32),
                    jax.ShapeDtypeStruct((OWN, D), F32)),
         in_specs=[anyspec] * NCH,
-        out_specs=(pl.BlockSpec(memory_space=pltpu.SMEM), vspec, vspec),
-        scratch_shapes=[pltpu.VMEM(v.shape, F32) for v in (rows, sh1, sh2)] + [pltpu.SemaphoreType.DMA((NCH,))],
+        out_specs=(pl.BlockSpec(memory_space=pltpu.SMEM), anyspec, anyspec),
+        scratch_shapes=[pltpu.VMEM(v.shape, F32) for v in (rows, sh1, sh2)] + [pltpu.VMEM((OWN, D), F32)] * 2 + [
+            pltpu.SemaphoreType.DMA((5,))],
         name='result',
     )(rows, sh1, sh2)
 

time: 138 us -> 139 us (level)
  no operation moved by 1% of the time
where the time goes in v9:
time: 139 us; the launch traced here: 138 us
  Pallas kernels  138 us (99%)
    pallas_call x1, Pallas kernels, main_call(): pl.pallas_call(main_kernel, out_shape=(jax.ShapeDtypeStruct((NCH, NTOK, C...  135 us

profile of v9, /device:TPU:0, one launch (start us, length us, event | category | flops | bytes accessed | tf_op | source)
XLA Modules:
  0.0 138.3 jit_solution(16075013047140810627)
XLA Ops:
  0.6 134.7 %main.1 = (f32[3,8192,256]{2,1,0:T(8,128)}, f32[3,2,96,256]{3,2,1,0:T(8,128)}, f32[3,2,32,768]{3,2,1,0:T(8,128)}, f32[32,128]{1,0:T(8,128)}) custom-call(bf16[8192,768]{1,0:T(8,128)(2,1)} %x_hbm.1, bf16[768,768]{1,0:T(8,128)(2,1)} %w1_hbm.1, bf16[8,3,32,768]{3,2,1,0:T(8,128)(2,1)} %bitcast.2, bf16[19,2,768]{2,1,0:T(2,128)(2,1)} %bitcast.3, s32[2,8192]{1,0:T(2,128)} %lab_hbm.1), custom_call_target="tpu_custom_call" | custom-call | tf_op jit(solution)/shard_map/main/pallas_call | solution.py:781
  135.4 2.8 %result.1 = (f32[2]{0:T(128)}, f32[96,768]{1,0:T(8,128)}, f32[96,768]{1,0:T(8,128)}) custom-call(f32[32,128]{1,0:T(8,128)} %get-tuple-element.6.rows_hbm, f32[3,2,96,256]{3,2,1,0:T(8,128)} %get-tuple-element.7.sh1_hbm, f32[3,2,32,768]{3,2,1,0:T(8,128)} %get-tuple-element.8.sh2_hbm), custom_call_target="tpu_custom_call" | custom-call | tf_op jit(solution)/shard_map/result/pallas_call | solution.py:857

commit v10 on v9

--- a/solution.py
+++ b/solution.py
@@ -810,7 +810,7 @@
     )(x, w1, w2r, heads, labels)
 
 
-def result_kernel(rows_hbm, sh1_hbm, sh2_hbm, a_ref, g1_hbm, g2_hbm, rows, sh1, sh2, g1_ref, g2_ref, sem):
+def result_kernel(rows_hbm, sh1_hbm, sh2_hbm, a_ref, g1_ref, g2_ref, rows, sh1, sh2, sem):
     ld_rows = pltpu.make_async_copy(rows_hbm, rows, sem.at[0])
     loads = [pltpu.make_async_copy(sh1_hbm, sh1, sem.at[1]), pltpu.make_async_copy(sh2_hbm, sh2, sem.at[2])]
     ld_rows.start()
@@ -837,31 +837,24 @@
     a_ref[1] = a1[0, 0]
     for cp in loads:
         cp.wait()
-    out1 = pltpu.make_async_copy(g1_ref, g1_hbm, sem.at[3])
-    out2 = pltpu.make_async_copy(g2_ref, g2_hbm, sem.at[4])
-    for c in range(NCH):
-        g2_ref[c * GR:(c + 1) * GR, :] = a0 * sh2[c, 0] + a1 * sh2[c, 1]
-    out2.start()
     for c in range(NCH):
         comb = a0 * sh1[c, 0] + a1 * sh1[c, 1]
         for g in range(8):
             col = g * NCH * GR + c * GR
             g1_ref[:, col:col + GR] = comb[:, g * GR:(g + 1) * GR]
-    out1.start()
-    out2.wait()
-    out1.wait()
+        g2_ref[c * GR:(c + 1) * GR, :] = a0 * sh2[c, 0] + a1 * sh2[c, 1]
 
 
 def result_call(rows, sh1, sh2):
+    vspec = pl.BlockSpec(memory_space=pltpu.VMEM)
     anyspec = pl.BlockSpec(memory_space=pl.ANY)
     return pl.pallas_call(
         result_kernel,
         out_shape=(jax.ShapeDtypeStruct((2,), F32), jax.ShapeDtypeStruct((OWN, D), F32),
                    jax.ShapeDtypeStruct((OWN, D), F32)),
         in_specs=[anyspec] * NCH,
-        out_specs=(pl.BlockSpec(memory_space=pltpu.SMEM), anyspec, anyspec),
-        scratch_shapes=[pltpu.VMEM(v.shape, F32) for v in (rows, sh1, sh2)] + [pltpu.VMEM((OWN, D), F32)] * 2 + [
-            pltpu.SemaphoreType.DMA((5,))],
+        out_specs=(pl.BlockSpec(memory_space=pltpu.SMEM), vspec, vspec),
+        scratch_shapes=[pltpu.VMEM(v.shape, F32) for v in (rows, sh1, sh2)] + [pltpu.SemaphoreType.DMA((NCH,))],
         name='result',
     )(rows, sh1, sh2)
 

time: 139 us -> 138 us (level)
  no operation moved by 1% of the time
where the time goes in v10:
time: 138 us
  Pallas kernels  137 us (99%)
    pallas_call x1, Pallas kernels, main_call(): pl.pallas_call(main_kernel, out_shape=(jax.ShapeDtypeStruct((NCH, NTOK, C...  135 us

profile of v10, /device:TPU:0, one launch (start us, length us, event | category | flops | bytes accessed | tf_op | source)
XLA Modules:
  0.0 137.8 jit_solution(13631700744275213660)
XLA Ops:
  0.6 134.7 %main.1 = (f32[3,8192,256]{2,1,0:T(8,128)}, f32[3,2,96,256]{3,2,1,0:T(8,128)}, f32[3,2,32,768]{3,2,1,0:T(8,128)}, f32[32,128]{1,0:T(8,128)}) custom-call(bf16[8192,768]{1,0:T(8,128)(2,1)} %x_hbm.1, bf16[768,768]{1,0:T(8,128)(2,1)} %w1_hbm.1, bf16[8,3,32,768]{3,2,1,0:T(8,128)(2,1)} %bitcast.2, bf16[19,2,768]{2,1,0:T(2,128)(2,1)} %bitcast.3, s32[2,8192]{1,0:T(2,128)} %lab_hbm.1), custom_call_target="tpu_custom_call" | custom-call | tf_op jit(solution)/shard_map/main/pallas_call | solution.py:781
  135.4 2.3 %result.1 = (f32[2]{0:T(128)}, f32[96,768]{1,0:T(8,128)}, f32[96,768]{1,0:T(8,128)}) custom-call(f32[32,128]{1,0:T(8,128)} %get-tuple-element.6.rows_hbm, f32[3,2,96,256]{3,2,1,0:T(8,128)} %get-tuple-element.7.sh1_hbm, f32[3,2,32,768]{3,2,1,0:T(8,128)} %get-tuple-element.8.sh2_hbm), custom_call_target="tpu_custom_call" | custom-call | tf_op jit(solution)/shard_map/result/pallas_call | solution.py:851
